TPU v7x, 32 devices: a whole 2x2x4 slice. The times are simulated.
32 devices in a mesh: fsdp: 4 (over x, core), rep: 8 (over z, y).
Axes of the slice: x: 2, y: 2, z: 4, core: 2. Of those that a mesh axis runs over, the one named last changes fastest.
Arguments:
- tokens: bfloat16 [12288, 1024], P(('fsdp', 'rep')), may hold values from -6 to 6
- out_grad: bfloat16 [12288, 1024], P(('fsdp', 'rep')), may hold values from -6 to 6
- norm1_gain: bfloat16 [1024], P('fsdp'), may hold values from 0.5 to 1.5
- norm1_bias: bfloat16 [1024], P('fsdp'), may hold values from -1.5 to 1.5
- w_qkv: bfloat16 [1024, 3072], P('fsdp'), may hold values from -0.1875 to 0.1875
- q_bias: bfloat16 [1024], P('fsdp'), may hold values from -2.5 to 2.5
- v_bias: bfloat16 [1024], P('fsdp'), may hold values from -2.5 to 2.5
- w_out: bfloat16 [1024, 1024], P('fsdp'), may hold values from -2 to 2
- out_bias: bfloat16 [1024], P('fsdp'), may hold values from -1.5 to 1.5
- attn_scale: bfloat16 [1024], P('fsdp'), may hold values from 0.5 to 1.5
- norm2_gain: bfloat16 [1024], P('fsdp'), may hold values from 0.5 to 1.5
- norm2_bias: bfloat16 [1024], P('fsdp'), may hold values from -1.5 to 1.5
- w_up: bfloat16 [1024, 4096], P('fsdp'), may hold values from -0.1875 to 0.1875
- up_bias: bfloat16 [4096], P('fsdp'), may hold values from -2.5 to 2.5
- w_down: bfloat16 [4096, 1024], P('fsdp'), may hold values from -0.09375 to 0.09375
- down_bias: bfloat16 [1024], P('fsdp'), may hold values from -1.5 to 1.5
- mlp_scale: bfloat16 [1024], P('fsdp'), may hold values from 0.5 to 1.5
- image_ids: int32 [12288], P(('fsdp', 'rep')), may hold values from 0 to 7, as said below
- pad_mask: int32 [12288], P(('fsdp', 'rep')), may hold values from 0 to 1, as said below
Outputs:
- layer_out: bfloat16 [12288, 1024], P(('fsdp', 'rep'))
- tokens_grad: bfloat16 [12288, 1024], P(('fsdp', 'rep'))
- norm1_gain_grad: float32 [1024], P('fsdp')
- norm1_bias_grad: float32 [1024], P('fsdp')
- w_qkv_grad: float32 [1024, 3072], P('fsdp')
- q_bias_grad: float32 [1024], P('fsdp')
- v_bias_grad: float32 [1024], P('fsdp')
- w_out_grad: float32 [1024, 1024], P('fsdp')
- out_bias_grad: float32 [1024], P('fsdp')
- attn_scale_grad: float32 [1024], P('fsdp')
- norm2_gain_grad: float32 [1024], P('fsdp')
- norm2_bias_grad: float32 [1024], P('fsdp')
- w_up_grad: float32 [1024, 4096], P('fsdp')
- up_bias_grad: float32 [4096], P('fsdp')
- w_down_grad: float32 [4096, 1024], P('fsdp')
- down_bias_grad: float32 [1024], P('fsdp')
- mlp_scale_grad: float32 [1024], P('fsdp')
Inputs may be any that keep to these rules, and one draw needn't show every extreme that they name: `image_ids`: nondecreasing along the tokens. The tokens with pad_mask 1 and one image number are 1370 consecutive tokens, and every number from 0 to 7 has such a run. A pad token carries the number of the image before it, or 0 before the first image. `pad_mask`: pad tokens lie only before, between or after the images' runs.
All inputs are finite; a program needn't handle non-finite values.
Results may differ from a plain program's by a relative error of at most 0.01.
Values may be sent and summed in bfloat16 or wider, within the bound.
A program may use at most 192 MiB of HBM per device.

v0:
```python
import jax
import jax.numpy as jnp
from jax import lax
from jax.sharding import PartitionSpec as P

D = 1024
HEADS = 16
HEAD_DIM = 64
REACH = 4


EPSILON = 1e-06
NEG_BIG = -1e30


def from_behind(block, axis, distance):
    devices = range(lax.axis_size(axis))
    route = [(i - distance, i) for i in devices if i - distance in devices]
    return lax.ppermute(block, axis, route)


def layer_norm(values, gain, shift):
    center = jnp.mean(values, axis=-1, keepdims=True)
    centered = values - center
    spread = jnp.mean(centered * centered, axis=-1, keepdims=True)
    return centered * lax.rsqrt(spread + EPSILON) * gain + shift


def exact_gelu(values):
    return jax.nn.gelu(values, approximate=False)


def matmul(left, right):
    return jnp.dot(left, right, preferred_element_type=jnp.float32)


def matmul_nt(left, right):
    return jnp.einsum("te,de->td", left, right, preferred_element_type=jnp.float32)


def matmul_tn(left, right):
    return jnp.einsum("td,te->de", left, right, preferred_element_type=jnp.float32)


def neighbor_rows(packed, offset):
    return from_behind((packed[0], packed[1], packed[2]), ("fsdp", "rep"), offset)


def returned_rows(packed, offset):
    return from_behind((packed[0], packed[1]), ("fsdp", "rep"), offset)


def unpack_params(gathered):
    vector_ids = (0, 1, 3, 4, 6, 7, 8, 9, 10, 11, 13, 14)
    return tuple(
        (
            member.astype(jnp.float32) if position in vector_ids else member
            for position, member in enumerate(gathered)
        )
    )


def shards(
    tokens,
    out_grad,
    norm1_gain,
    norm1_bias,
    w_qkv,
    q_bias,
    v_bias,
    w_out,
    out_bias,
    attn_scale,
    norm2_gain,
    norm2_bias,
    w_up,
    up_bias,
    w_down,
    down_bias,
    mlp_scale,
    image_ids,
    pad_mask,
):
    first = (
        lax.all_gather(norm1_gain, "fsdp", axis=0, tiled=True),
        lax.all_gather(norm1_bias, "fsdp", axis=0, tiled=True),
        lax.all_gather(w_qkv, "fsdp", axis=0, tiled=True),
        lax.all_gather(q_bias, "fsdp", axis=0, tiled=True),
        lax.all_gather(v_bias, "fsdp", axis=0, tiled=True),
        lax.all_gather(w_out, "fsdp", axis=0, tiled=True),
        lax.all_gather(out_bias, "fsdp", axis=0, tiled=True),
        lax.all_gather(attn_scale, "fsdp", axis=0, tiled=True),
        lax.all_gather(norm2_gain, "fsdp", axis=0, tiled=True),
        lax.all_gather(norm2_bias, "fsdp", axis=0, tiled=True),
        lax.all_gather(w_up, "fsdp", axis=0, tiled=True),
        lax.all_gather(up_bias, "fsdp", axis=0, tiled=True),
        lax.all_gather(w_down, "fsdp", axis=0, tiled=True),
        lax.all_gather(down_bias, "fsdp", axis=0, tiled=True),
        lax.all_gather(mlp_scale, "fsdp", axis=0, tiled=True),
    )
    (
        gain_first,
        shift_first,
        wide_qkv,
        query_bias,
        value_bias,
        wide_out,
        proj_bias,
        attn_gamma,
        gain_second,
        shift_second,
        wide_up,
        hidden_bias,
        wide_down,
        final_bias,
        mlp_gamma,
    ) = unpack_params(first)
    tok_rows = tokens.shape[0]
    width = (2 * REACH + 1) * tok_rows
    pair_cols = 2 * HEAD_DIM
    pairs = HEADS // 2
    factor = HEAD_DIM ** (-0.5)
    inputs = tokens.astype(jnp.float32)
    act_one = layer_norm(inputs, gain_first, shift_first).astype(jnp.bfloat16)
    qkv_rows = matmul(act_one, wide_qkv)
    query = ((qkv_rows[:, :D] + query_bias) * factor).astype(jnp.bfloat16)
    keys_own = qkv_rows[:, D : 2 * D].astype(jnp.bfloat16)
    values_own = (qkv_rows[:, 2 * D :] + value_bias).astype(jnp.bfloat16)
    codes_own = (
        jnp.where(pad_mask > 0, image_ids % 64 + 1, 0).astype(jnp.float32).astype(jnp.bfloat16)
    )
    packed = (keys_own, values_own, codes_own)
    members = [neighbor_rows(packed, offset) for offset in range(REACH, 0, -1)]
    members = (
        members + [packed] + [neighbor_rows(packed, -offset) for offset in range(1, REACH + 1)]
    )
    key_window = jnp.concatenate([member[0] for member in members], axis=0)
    value_window = jnp.concatenate([member[1] for member in members], axis=0)
    code_window = jnp.concatenate([member[2] for member in members], axis=0)
    allowed = (codes_own[:, None] == code_window[None, :]) & (codes_own[:, None] > 0)

    def pair_scores(query_pair, key_pair):
        return jnp.einsum(
            "qhd,khd->hqk",
            query_pair.reshape(tok_rows, 2, HEAD_DIM),
            key_pair.reshape(width, 2, HEAD_DIM),
            preferred_element_type=jnp.float32,
        )

    def forward_pair(pair_index, carry):
        attn_sum, log_total = carry
        column = pair_index * pair_cols
        query_pair = lax.dynamic_slice_in_dim(query, column, pair_cols, 1)
        key_pair = lax.dynamic_slice_in_dim(key_window, column, pair_cols, 1)
        value_pair = lax.dynamic_slice_in_dim(value_window, column, pair_cols, 1)
        masked = jnp.where(allowed[None], pair_scores(query_pair, key_pair), NEG_BIG)
        row_top = jnp.max(masked, axis=2, keepdims=True)
        weights_raw = jnp.where(allowed[None], jnp.exp(masked - row_top), 0.0)
        totals = jnp.sum(weights_raw, axis=2, keepdims=True)
        totals = jnp.where(totals > 0, totals, 1.0)
        weights_low = (weights_raw / totals).astype(jnp.bfloat16)
        mixed = jnp.einsum(
            "hqk,khd->qhd",
            weights_low,
            value_pair.reshape(width, 2, HEAD_DIM),
            preferred_element_type=jnp.float32,
        ).reshape(tok_rows, pair_cols)
        attn_sum = lax.dynamic_update_slice_in_dim(attn_sum, mixed, column, 1)
        log_total = lax.dynamic_update_slice_in_dim(
            log_total, (row_top + jnp.log(totals))[:, :, 0], 2 * pair_index, 0
        )
        return (attn_sum, log_total)

    attn_sum, log_total = lax.fori_loop(
        0,
        pairs,
        forward_pair,
        (jnp.zeros((tok_rows, D), jnp.float32), jnp.zeros((HEADS, tok_rows), jnp.float32)),
    )
    attn_low = attn_sum.astype(jnp.bfloat16)
    proj = matmul(attn_low, wide_out) + proj_bias
    residual = inputs + attn_gamma * proj
    act_two = layer_norm(residual, gain_second, shift_second).astype(jnp.bfloat16)
    pre_act = matmul(act_two, wide_up) + hidden_bias
    hidden = exact_gelu(pre_act).astype(jnp.bfloat16)
    branch = matmul(hidden, wide_down) + final_bias
    layer_out = (residual + mlp_gamma * branch).astype(jnp.bfloat16)
    second = (
        lax.all_gather(norm1_gain, "fsdp", axis=0, tiled=True),
        lax.all_gather(norm1_bias, "fsdp", axis=0, tiled=True),
        lax.all_gather(w_qkv, "fsdp", axis=0, tiled=True),
        lax.all_gather(q_bias, "fsdp", axis=0, tiled=True),
        lax.all_gather(v_bias, "fsdp", axis=0, tiled=True),
        lax.all_gather(w_out, "fsdp", axis=0, tiled=True),
        lax.all_gather(out_bias, "fsdp", axis=0, tiled=True),
        lax.all_gather(attn_scale, "fsdp", axis=0, tiled=True),
        lax.all_gather(norm2_gain, "fsdp", axis=0, tiled=True),
        lax.all_gather(norm2_bias, "fsdp", axis=0, tiled=True),
        lax.all_gather(w_up, "fsdp", axis=0, tiled=True),
        lax.all_gather(up_bias, "fsdp", axis=0, tiled=True),
        lax.all_gather(w_down, "fsdp", axis=0, tiled=True),
        lax.all_gather(down_bias, "fsdp", axis=0, tiled=True),
        lax.all_gather(mlp_scale, "fsdp", axis=0, tiled=True),
    )
    (
        gain_first,
        shift_first,
        wide_qkv,
        query_bias,
        value_bias,
        wide_out,
        proj_bias,
        attn_gamma,
        gain_second,
        shift_second,
        wide_up,
        hidden_bias,
        wide_down,
        final_bias,
        mlp_gamma,
    ) = unpack_params(second)
    upstream = out_grad.astype(jnp.float32)
    mlp_gamma_grad = jnp.sum(upstream * branch, axis=0)
    branch_grad = mlp_gamma * upstream
    final_bias_grad = jnp.sum(branch_grad, axis=0)
    branch_low = branch_grad.astype(jnp.bfloat16)
    down_grad = matmul_tn(hidden, branch_low)
    hidden_grad = matmul_nt(branch_low, wide_down)
    ignored, gelu_back = jax.vjp(exact_gelu, pre_act)
    pre_grad = gelu_back(hidden_grad)[0]
    hidden_bias_grad = jnp.sum(pre_grad, axis=0)
    pre_low = pre_grad.astype(jnp.bfloat16)
    up_grad = matmul_tn(act_two, pre_low)
    act_two_grad = matmul_nt(pre_low, wide_up)
    ignored, norm_two_back = jax.vjp(layer_norm, residual, gain_second, shift_second)
    residual_part, gain_second_grad, shift_second_grad = norm_two_back(act_two_grad)
    residual_grad = upstream + residual_part
    attn_gamma_grad = jnp.sum(residual_grad * proj, axis=0)
    proj_grad = attn_gamma * residual_grad
    proj_bias_grad = jnp.sum(proj_grad, axis=0)
    proj_low = proj_grad.astype(jnp.bfloat16)
    out_weight_grad = matmul_tn(attn_low, proj_low)
    attn_grad_low = matmul_nt(proj_low, wide_out).astype(jnp.bfloat16)

    def backward_pair(pair_index, carry):
        query_grad, key_grad, value_grad = carry
        column = pair_index * pair_cols
        query_pair = lax.dynamic_slice_in_dim(query, column, pair_cols, 1)
        key_pair = lax.dynamic_slice_in_dim(key_window, column, pair_cols, 1)
        value_pair = lax.dynamic_slice_in_dim(value_window, column, pair_cols, 1)
        masked = jnp.where(allowed[None], pair_scores(query_pair, key_pair), NEG_BIG)
        row_log = lax.dynamic_slice_in_dim(log_total, 2 * pair_index, 2, 0)[:, :, None]
        weights_full = jnp.where(allowed[None], jnp.exp(masked - row_log), 0.0)
        weights_low = weights_full.astype(jnp.bfloat16)
        grad_heads = lax.dynamic_slice_in_dim(attn_grad_low, column, pair_cols, 1).reshape(
            tok_rows, 2, HEAD_DIM
        )
        weight_grad = jnp.einsum(
            "qhd,khd->hqk",
            grad_heads,
            value_pair.reshape(width, 2, HEAD_DIM),
            preferred_element_type=jnp.float32,
        )
        value_part = jnp.einsum(
            "hqk,qhd->khd", weights_low, grad_heads, preferred_element_type=jnp.float32
        ).reshape(width, pair_cols)
        row_dot = jnp.sum(weights_full * weight_grad, axis=2, keepdims=True)
        score_grad = (weights_full * (weight_grad - row_dot)).astype(jnp.bfloat16)
        query_part = jnp.einsum(
            "hqk,khd->qhd",
            score_grad,
            key_pair.reshape(width, 2, HEAD_DIM),
            preferred_element_type=jnp.float32,
        ).reshape(tok_rows, pair_cols)
        key_part = jnp.einsum(
            "hqk,qhd->khd",
            score_grad,
            query_pair.reshape(tok_rows, 2, HEAD_DIM),
            preferred_element_type=jnp.float32,
        ).reshape(width, pair_cols)
        query_grad = lax.dynamic_update_slice_in_dim(query_grad, query_part, column, 1)
        key_grad = lax.dynamic_update_slice_in_dim(key_grad, key_part, column, 1)
        value_grad = lax.dynamic_update_slice_in_dim(value_grad, value_part, column, 1)
        return (query_grad, key_grad, value_grad)

    query_grad, key_grad, value_grad = lax.fori_loop(
        0,
        pairs,
        backward_pair,
        (
            jnp.zeros((tok_rows, D), jnp.float32),
            jnp.zeros((width, D), jnp.float32),
            jnp.zeros((width, D), jnp.float32),
        ),
    )
    own_start = REACH * tok_rows
    key_total = key_grad[own_start : own_start + tok_rows]
    value_total = value_grad[own_start : own_start + tok_rows]
    for offset in range(-REACH, REACH + 1):
        if offset != 0:
            begin = (offset + REACH) * tok_rows
            arrived = returned_rows(
                (key_grad[begin : begin + tok_rows], value_grad[begin : begin + tok_rows]), offset
            )
            key_total = key_total + arrived[0]
            value_total = value_total + arrived[1]
    query_scaled = factor * query_grad
    query_bias_grad = jnp.sum(query_scaled, axis=0)
    value_bias_grad = jnp.sum(value_total, axis=0)
    qkv_grad = jnp.concatenate(
        [
            query_scaled.astype(jnp.bfloat16),
            key_total.astype(jnp.bfloat16),
            value_total.astype(jnp.bfloat16),
        ],
        axis=1,
    )
    qkv_weight_grad = matmul_tn(act_one, qkv_grad)
    act_one_grad = matmul_nt(qkv_grad, wide_qkv)
    ignored, norm_one_back = jax.vjp(layer_norm, inputs, gain_first, shift_first)
    input_part, gain_first_grad, shift_first_grad = norm_one_back(act_one_grad)
    tokens_grad = (residual_grad + input_part).astype(jnp.bfloat16)
    owned = (
        lax.psum_scatter(gain_first_grad, "fsdp", scatter_dimension=0, tiled=True),
        lax.psum_scatter(shift_first_grad, "fsdp", scatter_dimension=0, tiled=True),
        lax.psum_scatter(qkv_weight_grad, "fsdp", scatter_dimension=0, tiled=True),
        lax.psum_scatter(query_bias_grad, "fsdp", scatter_dimension=0, tiled=True),
        lax.psum_scatter(value_bias_grad, "fsdp", scatter_dimension=0, tiled=True),
        lax.psum_scatter(out_weight_grad, "fsdp", scatter_dimension=0, tiled=True),
        lax.psum_scatter(proj_bias_grad, "fsdp", scatter_dimension=0, tiled=True),
        lax.psum_scatter(attn_gamma_grad, "fsdp", scatter_dimension=0, tiled=True),
        lax.psum_scatter(gain_second_grad, "fsdp", scatter_dimension=0, tiled=True),
        lax.psum_scatter(shift_second_grad, "fsdp", scatter_dimension=0, tiled=True),
        lax.psum_scatter(up_grad, "fsdp", scatter_dimension=0, tiled=True),
        lax.psum_scatter(hidden_bias_grad, "fsdp", scatter_dimension=0, tiled=True),
        lax.psum_scatter(down_grad, "fsdp", scatter_dimension=0, tiled=True),
        lax.psum_scatter(final_bias_grad, "fsdp", scatter_dimension=0, tiled=True),
        lax.psum_scatter(mlp_gamma_grad, "fsdp", scatter_dimension=0, tiled=True),
    )
    (
        owned_gain1,
        owned_shift1,
        owned_qkv,
        owned_qbias,
        owned_vbias,
        owned_out,
        owned_pbias,
        owned_agamma,
        owned_gain2,
        owned_shift2,
        owned_up,
        owned_hbias,
        owned_down,
        owned_fbias,
        owned_mgamma,
    ) = owned
    summed = lax.psum(
        (
            owned_gain1,
            owned_shift1,
            owned_qkv,
            owned_qbias,
            owned_vbias,
            owned_out,
            owned_pbias,
            owned_agamma,
            owned_gain2,
            owned_shift2,
            owned_up,
            owned_hbias,
            owned_down,
            owned_fbias,
            owned_mgamma,
        ),
        "rep",
    )
    return (
        layer_out,
        tokens_grad,
        summed[0],
        summed[1],
        summed[2],
        summed[3],
        summed[4],
        summed[5],
        summed[6],
        summed[7],
        summed[8],
        summed[9],
        summed[10],
        summed[11],
        summed[12],
        summed[13],
        summed[14],
    )


def solution(mesh):
    return jax.shard_map(
        shards,
        mesh=mesh,
        in_specs=(
            P(("fsdp", "rep"), None),
            P(("fsdp", "rep"), None),
            P("fsdp"),
            P("fsdp"),
            P("fsdp", None),
            P("fsdp"),
            P("fsdp"),
            P("fsdp", None),
            P("fsdp"),
            P("fsdp"),
            P("fsdp"),
            P("fsdp"),
            P("fsdp", None),
            P("fsdp"),
            P("fsdp", None),
            P("fsdp"),
            P("fsdp"),
            P(("fsdp", "rep")),
            P(("fsdp", "rep")),
        ),
        out_specs=(
            P(("fsdp", "rep"), None),
            P(("fsdp", "rep"), None),
            P("fsdp"),
            P("fsdp"),
            P("fsdp", None),
            P("fsdp"),
            P("fsdp"),
            P("fsdp", None),
            P("fsdp"),
            P("fsdp"),
            P("fsdp"),
            P("fsdp"),
            P("fsdp", None),
            P("fsdp"),
            P("fsdp", None),
            P("fsdp"),
            P("fsdp"),
        ),
        check_vma=False,
    )
```

profile of v0, /device:TPU:0, one launch (start us, length us, event | category | flops | bytes accessed | tf_op | source)
XLA Modules:
  0.0 2573.2 jit_solution(6176084686641847240)
XLA Ops:
  9.5 6.0 all-gather.2
  32.0 26.8 %all-gather.15.cloned.1.call-done = bf16[1024,3072]{1,0:T(8,128)(2,1)} async-done(((bf16[256,3072]{1,0:T(8,128)(2,1)}), bf16[1024,3072]{1,0:T(8,128)(2,1)}) %all-gather.15.cloned.1.call-update) | async-done | bytes 6291472 | tf_op jit(solution)/shard_map/all_gather | solution.py:87
  83.9 37.9 %collective-permute-done.8 = bf16[384]{0:T(512)(128)(2,1)S(1)} collective-permute-done((bf16[384]{0:T(512)(128)(2,1)S(1)}, bf16[384]{0:T(512)(128)(2,1)S(1)}, u32[]{:S(2)}, u32[]{:S(2)}) %collective-permute-start.8) | collective-permute-done | bytes 800 | tf_op jit(solution)/shard_map/ppermute | solution.py:19
  121.7 54.8 %collective-permute-start.9 = (bf16[384]{0:T(512)(128)(2,1)S(1)}, bf16[384]{0:T(512)(128)(2,1)S(1)}, u32[]{:S(2)}, u32[]{:S(2)}) collective-permute-start(bf16[384]{0:T(512)(128)(2,1)S(1)} %get-tuple-element.748), channel_id=1, source_target_pairs={{0,3},{1,4},{2,5},{3,6},{4,7},{5,8},{6,9},{7,10},{8,11},{9,12},{10... | collective-permute-start | bytes 2312 | tf_op jit(solution)/shard_map/ppermute | solution.py:19
  180.7 5.9 collective-permute-start.11
  208.5 8.0 collective-permute-done.15
  220.0 13.3 all-gather.9
  280.5 6.9 collective-permute-start.16
  301.8 80.4 %collective-permute-start.19 = (bf16[384,1024]{1,0:T(8,128)(2,1)S(1)}, bf16[384,1024]{1,0:T(8,128)(2,1)}, u32[]{:S(2)}, u32[]{:S(2)}) collective-permute-start(bf16[384,1024]{1,0:T(8,128)(2,1)S(1)} %copy-done.30), channel_id=1, source_target_pairs={{0,1},{1,2},{2,3},{3,4},{4,5},{5,6},{6,7},{7,8},{8,9},{9,10},{10,1... | collective-permute-start | bytes 2359304 | tf_op jit(solution)/shard_map/ppermute | solution.py:19
  385.3 9.5 collective-permute-done.7
  397.0 9.6 copy.62
  422.5 22.9 collective-permute-done.21
  446.2 17.8 collective-permute-done.22
  464.9 47.8 %collective-permute-done.23 = bf16[384,1024]{1,0:T(8,128)(2,1)S(1)} collective-permute-done((bf16[384,1024]{1,0:T(8,128)(2,1)S(1)}, bf16[384,1024]{1,0:T(8,128)(2,1)S(1)}, u32[]{:S(2)}, u32[]{:S(2)}) %collective-permute-start.23) | collective-permute-done | bytes 786464 | tf_op jit(solution)/shard_map/ppermute | solution.py:19
  513.7 9.8 copy.64
  525.1 169.7 %while.34 = (s32[]{:T(128)}, bf16[384,1024]{0,1:T(8,128)(2,1)}, f32[16,384]{1,0:T(8,128)}, bf16[3456,1024]{0,1:T(8,128)(2,1)}, bf16[384,1024]{0,1:T(8,128)(2,1)}...) while((s32[]{:T(128)}, bf16[384,1024]{0,1:T(8,128)(2,1)}, ...), condition=%wide.region_5.6_spmd.clone, body=%wide.region_2.5_spmd.clone.sunk | while | flops 713982720 | bytes 85560464 | solution.py:174
  534.6 6.5 fusion.121
  555.8 6.5 fusion.121
  577.0 6.5 fusion.121
  598.2 6.5 fusion.121
  613.5 5.9 select_reduce_fusion.2
  619.4 6.5 fusion.121
  640.6 6.5 fusion.121
  661.8 6.5 fusion.121
  677.1 5.9 select_reduce_fusion.2
  683.0 6.5 fusion.121
  700.3 20.7 multiply_convert_fusion.1
  721.0 12.9 fusion.69
  738.4 8.9 fusion.29
  756.7 7.3 broadcast.258.clone
  764.0 7.2 broadcast.258.clone2
  771.2 332.7 %while.35 = (s32[]{:T(128)}, f32[384,1024]{1,0:T(8,128)}, f32[3456,1024]{1,0:T(8,128)}, f32[3456,1024]{1,0:T(8,128)}, bf16[3456,1024]{0,1:T(8,128)(2,1)}, /*inde...) while((s32[]{:T(128)}, f32[384,1024]{1,0:T(8,128)}, ...), condition=%wide.region_12.13_spmd.clone, body=%wide.region_10.12_spmd.clone.sunk | while | flops 1727888640 | bytes 204102976 | solution.py:286
  783.2 7.6 multiply_reduce_fusion.8
  824.8 7.6 multiply_reduce_fusion.8
  866.4 7.6 multiply_reduce_fusion.8
  907.9 7.6 multiply_reduce_fusion.8
  949.5 7.5 multiply_reduce_fusion.8
  991.0 7.5 multiply_reduce_fusion.8
  1032.6 7.5 multiply_reduce_fusion.8
  1074.1 7.6 multiply_reduce_fusion.8
  1103.9 8.6 fusion.68
  1119.6 7.5 collective-permute-start.36
  1128.4 21.0 collective-permute-done.39
  1150.7 9.3 fusion.67
  1159.9 23.3 collective-permute-done.38
  1184.5 32.4 %collective-permute-done.37 = f32[384,1024]{1,0:T(8,128)} collective-permute-done((f32[384,1024]{1,0:T(8,128)}, f32[384,1024]{1,0:T(8,128)}, u32[]{:S(2)}, u32[]{:S(2)}) %collective-permute-start.37) | collective-permute-done | bytes 1572896 | tf_op jit(solution)/shard_map/ppermute | solution.py:19
  1218.2 34.9 %collective-permute-start.31 = (f32[384,1024]{1,0:T(8,128)}, f32[384,1024]{1,0:T(8,128)S(1)}, u32[]{:S(2)}, u32[]{:S(2)}) collective-permute-start(f32[384,1024]{1,0:T(8,128)} %get-tuple-element.519), channel_id=1, source_target_pairs={{0,4},{1,5},{2,6},{3,7},{4,8},{5,9},{6,10},{7,11},{8,12},{9,13},{1... | collective-permute-start | bytes 4718600 | tf_op jit(solution)/shard_map/ppermute | solution.py:19
  1253.2 22.1 collective-permute-start.30
  1279.6 166.0 %collective-permute-start.29 = (f32[384,1024]{1,0:T(8,128)}, f32[384,1024]{1,0:T(8,128)S(1)}, u32[]{:S(2)}, u32[]{:S(2)}) collective-permute-start(f32[384,1024]{1,0:T(8,128)} %get-tuple-element.514), channel_id=1, source_target_pairs={{0,2},{1,3},{2,4},{3,5},{4,6},{5,7},{6,8},{7,9},{8,10},{9,11},{10,... | collective-permute-start | bytes 4718600 | tf_op jit(solution)/shard_map/ppermute | solution.py:19
  1445.6 51.3 %collective-permute-start.28 = (f32[384,1024]{1,0:T(8,128)}, f32[384,1024]{1,0:T(8,128)S(1)}, u32[]{:S(2)}, u32[]{:S(2)}) collective-permute-start(f32[384,1024]{1,0:T(8,128)} %get-tuple-element.515), channel_id=1, source_target_pairs={{0,1},{1,2},{2,3},{3,4},{4,5},{5,6},{6,7},{7,8},{8,9},{9,10},{10,1... | collective-permute-start | bytes 4718600 | tf_op jit(solution)/shard_map/ppermute | solution.py:19
  1497.0 30.2 %collective-permute-done.32 = f32[384,1024]{1,0:T(8,128)S(1)} collective-permute-done((f32[384,1024]{1,0:T(8,128)S(1)}, f32[384,1024]{1,0:T(8,128)S(1)}, u32[]{:S(2)}, u32[]{:S(2)}) %collective-permute-start.32) | collective-permute-done | bytes 1572896 | tf_op jit(solution)/shard_map/ppermute | solution.py:19
  1538.3 50.0 %collective-permute-done.27 = f32[384,1024]{1,0:T(8,128)S(1)} collective-permute-done((f32[384,1024]{1,0:T(8,128)}, f32[384,1024]{1,0:T(8,128)S(1)}, u32[]{:S(2)}, u32[]{:S(2)}) %collective-permute-start.27) | collective-permute-done | bytes 1572896 | tf_op jit(solution)/shard_map/ppermute | solution.py:19
  1588.3 39.9 %collective-permute-done.26 = f32[384,1024]{1,0:T(8,128)S(1)} collective-permute-done((f32[384,1024]{1,0:T(8,128)}, f32[384,1024]{1,0:T(8,128)S(1)}, u32[]{:S(2)}, u32[]{:S(2)}) %collective-permute-start.26) | collective-permute-done | bytes 1572896 | tf_op jit(solution)/shard_map/ppermute | solution.py:19
  1628.3 60.8 %collective-permute-done.25 = f32[384,1024]{1,0:T(8,128)S(1)} collective-permute-done((f32[384,1024]{1,0:T(8,128)}, f32[384,1024]{1,0:T(8,128)S(1)}, u32[]{:S(2)}, u32[]{:S(2)}) %collective-permute-start.25) | collective-permute-done | bytes 1572896 | tf_op jit(solution)/shard_map/ppermute | solution.py:19
  1689.0 74.1 %collective-permute-done.24 = f32[384,1024]{1,0:T(8,128)S(1)} collective-permute-done((f32[384,1024]{1,0:T(8,128)S(1)}, f32[384,1024]{1,0:T(8,128)S(1)}, u32[]{:S(2)}, u32[]{:S(2)}) %collective-permute-start.24) | collective-permute-done | bytes 1572896 | tf_op jit(solution)/shard_map/ppermute | solution.py:19
  1766.0 6.9 fusion.37
  1774.3 10.2 fusion.33
  1785.7 10.2 fusion.39
  1796.2 103.9 %reduce-scatter.5.cloned.1.call-done = f32[256,3072]{1,0:T(8,128)} async-done(((f32[1024,3072]{1,0:T(8,128)}), f32[256,3072]{1,0:T(8,128)}) %reduce-scatter.5.cloned.1.call-update) | async-done | bytes 3145744 | tf_op jit(solution)/shard_map/reduce_scatter | solution.py:326
  1900.1 127.7 %reduce-scatter.9.cloned.1.call-done = f32[256,4096]{1,0:T(8,128)} async-done(((f32[1024,4096]{1,0:T(8,128)}), f32[256,4096]{1,0:T(8,128)}) %reduce-scatter.9.cloned.1.call-update) | async-done | bytes 4194320 | tf_op jit(solution)/shard_map/reduce_scatter | solution.py:334
  2027.8 127.7 %reduce-scatter.11.cloned.1.call-done = f32[1024,1024]{1,0:T(8,128)} async-done(((f32[4096,1024]{1,0:T(8,128)}), f32[1024,1024]{1,0:T(8,128)}) %reduce-scatter.11.cloned.1.call-update) | async-done | bytes 4194320 | tf_op jit(solution)/shard_map/reduce_scatter | solution.py:336
  2165.6 11.5 all-reduce.13
  2177.9 40.2 %all-reduce.11 = (f32[256]{0:T(256)}, f32[256]{0:T(256)}, f32[256]{0:T(256)}, f32[256]{0:T(256)}, f32[256]{0:T(256)}, /*index=5*/f32[256]{0:T(256)}, f32[256]{0:...) all-reduce(f32[256]{0:T(256)S(1)} %dynamic-slice.1, ...), channel_id=1, replica_groups=mesh['fsdp'=4,'rep'=8] {'rep'}, use_global_device_ids=true, to_apply=%region_17.18 | all-reduce | flops 3584 | bytes 28672 | tf_op jit(solution)/shard_map/psum | solution.py:357
  2220.9 334.6 %all-reduce.16.cloned.1.call-done = (f32[256,3072]{1,0:T(8,128)}, f32[256,1024]{1,0:T(8,128)}, f32[256,4096]{1,0:T(8,128)}, f32[1024,1024]{1,0:T(8,128)}) async-done(((f32[256,3072]{1,0:T(8,128)}, f32[256,1024]{1,0:T(8,128)}, f32[256,4096]{1,0:T(8,128)}, f32[1024,1024]{1,0:T(8,128)}), (f32[256,3072]{1,0:T(8,128)}, f32[256,1024]{1,0:T(8,128)}, f32[256,4096]{1,0:T(8,128)}, ...) | async-done | bytes 12582928 | tf_op jit(solution)/shard_map/psum | solution.py:357
  (633 shorter events, 612.3 us)
Async XLA Ops:
  7.2 51.5 %all-gather.15.cloned.1.call-start = ((), (), s32[]{:S(2)}) async-start(), calls=%async_computation.4 | async-start | bytes 7864320 | tf_op jit(solution)/shard_map/all_gather | solution.py:87
  8.0 686.8 %all-gather.17.cloned.1.call-start = ((), (), s32[]{:S(2)}) async-start(), calls=%async_computation.5 | async-start | bytes 2621440 | tf_op jit(solution)/shard_map/all_gather | solution.py:90
  8.7 691.5 %all-gather.19.cloned.1.call-start = ((), (), s32[]{:S(2)}) async-start(), calls=%async_computation.6 | async-start | bytes 10485760 | tf_op jit(solution)/shard_map/all_gather | solution.py:95
  9.5 711.5 %all-gather.21.cloned.1.call-start = ((), (), s32[]{:S(2)}) async-start(), calls=%async_computation.7 | async-start | bytes 10485760 | tf_op jit(solution)/shard_map/all_gather | solution.py:97
  65.9 174.0 %copy-start.69 = (bf16[256]{0:T(256)(128)(2,1)S(1)}, bf16[256]{0:T(256)(128)(2,1)}, u32[]{:S(2)}) copy-start(bf16[256]{0:T(256)(128)(2,1)} %param.32) | copy-start | bytes 1540
  65.9 179.2 %copy-start.70 = (bf16[256]{0:T(256)(128)(2,1)S(1)}, bf16[256]{0:T(256)(128)(2,1)}, u32[]{:S(2)}) copy-start(bf16[256]{0:T(256)(128)(2,1)} %param.31) | copy-start | bytes 1540
  65.9 184.4 %copy-start.71 = (bf16[256]{0:T(256)(128)(2,1)S(1)}, bf16[256]{0:T(256)(128)(2,1)}, u32[]{:S(2)}) copy-start(bf16[256]{0:T(256)(128)(2,1)} %param.33) | copy-start | bytes 1540
  65.9 189.6 %copy-start.59 = (bf16[1024]{0:T(1024)(128)(2,1)S(1)}, bf16[1024]{0:T(1024)(128)(2,1)}, u32[]{:S(2)}) copy-start(bf16[1024]{0:T(1024)(128)(2,1)} %param.36) | copy-start | bytes 6148
  65.9 195.0 %copy-start.72 = (bf16[256]{0:T(256)(128)(2,1)S(1)}, bf16[256]{0:T(256)(128)(2,1)}, u32[]{:S(2)}) copy-start(bf16[256]{0:T(256)(128)(2,1)} %param.34) | copy-start | bytes 1540
  66.4 151.3 %collective-permute-start = (bf16[384,1024]{1,0:T(8,128)(2,1)S(1)}, bf16[384,1024]{1,0:T(8,128)(2,1)S(1)}, u32[]{:S(2)}, u32[]{:S(2)}) collective-permute-start(bf16[384,1024]{1,0:T(8,128)(2,1)S(1)} %get-tuple-element.529), channel_id=1, source_target_pairs={{0,4},{1,5},{2,6},{3,7},{4,8},{5,9},{6,10},{7,11},{8,12},{9,13},{1... | collective-permute-start | bytes 2359304 | tf_op jit(solution)/shard_map/ppermute | solution.py:19
  70.8 200.7 %collective-permute-start.1 = (bf16[384,1024]{1,0:T(8,128)(2,1)S(1)}, bf16[384,1024]{1,0:T(8,128)(2,1)}, u32[]{:S(2)}, u32[]{:S(2)}) collective-permute-start(bf16[384,1024]{1,0:T(8,128)(2,1)S(1)} %get-tuple-element.529), channel_id=1, source_target_pairs={{0,3},{1,4},{2,5},{3,6},{4,7},{5,8},{6,9},{7,10},{8,11},{9,12},{10... | collective-permute-start | bytes 2359304 | tf_op jit(solution)/shard_map/ppermute | solution.py:19
  76.0 201.1 %collective-permute-start.2 = (bf16[384,1024]{1,0:T(8,128)(2,1)S(1)}, bf16[384,1024]{1,0:T(8,128)(2,1)}, u32[]{:S(2)}, u32[]{:S(2)}) collective-permute-start(bf16[384,1024]{1,0:T(8,128)(2,1)S(1)} %get-tuple-element.529), channel_id=1, source_target_pairs={{0,2},{1,3},{2,4},{3,5},{4,6},{5,7},{6,8},{7,9},{8,10},{9,11},{10,... | collective-permute-start | bytes 2359304 | tf_op jit(solution)/shard_map/ppermute | solution.py:19
  78.2 202.3 %collective-permute-start.3 = (bf16[384,1024]{1,0:T(8,128)(2,1)S(1)}, bf16[384,1024]{1,0:T(8,128)(2,1)}, u32[]{:S(2)}, u32[]{:S(2)}) collective-permute-start(bf16[384,1024]{1,0:T(8,128)(2,1)S(1)} %get-tuple-element.529), channel_id=1, source_target_pairs={{0,1},{1,2},{2,3},{3,4},{4,5},{5,6},{6,7},{7,8},{8,9},{9,10},{10,1... | collective-permute-start | bytes 2359304 | tf_op jit(solution)/shard_map/ppermute | solution.py:19
  81.6 40.1 %collective-permute-start.8 = (bf16[384]{0:T(512)(128)(2,1)S(1)}, bf16[384]{0:T(512)(128)(2,1)S(1)}, u32[]{:S(2)}, u32[]{:S(2)}) collective-permute-start(bf16[384]{0:T(512)(128)(2,1)S(1)} %get-tuple-element.748), channel_id=1, source_target_pairs={{0,4},{1,5},{2,6},{3,7},{4,8},{5,9},{6,10},{7,11},{8,12},{9,13},{1... | collective-permute-start | bytes 2312 | tf_op jit(solution)/shard_map/ppermute | solution.py:19
  121.7 56.1 %collective-permute-start.9 = (bf16[384]{0:T(512)(128)(2,1)S(1)}, bf16[384]{0:T(512)(128)(2,1)S(1)}, u32[]{:S(2)}, u32[]{:S(2)}) collective-permute-start(bf16[384]{0:T(512)(128)(2,1)S(1)} %get-tuple-element.748), channel_id=1, source_target_pairs={{0,3},{1,4},{2,5},{3,6},{4,7},{5,8},{6,9},{7,10},{8,11},{9,12},{10... | collective-permute-start | bytes 2312 | tf_op jit(solution)/shard_map/ppermute | solution.py:19
  177.9 2.9 collective-permute-start.10
  180.7 7.2 collective-permute-start.11
  188.0 5.7 collective-permute-start.12
  193.7 6.5 collective-permute-start.13
  200.2 7.0 collective-permute-start.14
  207.2 9.2 collective-permute-start.15
  216.4 73.0 %collective-permute-start.4 = (bf16[384,1024]{1,0:T(8,128)(2,1)S(1)}, bf16[384,1024]{1,0:T(8,128)(2,1)}, u32[]{:S(2)}, u32[]{:S(2)}) collective-permute-start(bf16[384,1024]{1,0:T(8,128)(2,1)S(1)} %get-tuple-element.529), channel_id=1, source_target_pairs={{1,0},{2,1},{3,2},{4,3},{5,4},{6,5},{7,6},{8,7},{9,8},{10,9},{11,1... | collective-permute-start | bytes 2359304 | tf_op jit(solution)/shard_map/ppermute | solution.py:19
  218.6 77.6 %collective-permute-start.5 = (bf16[384,1024]{1,0:T(8,128)(2,1)S(1)}, bf16[384,1024]{1,0:T(8,128)(2,1)}, u32[]{:S(2)}, u32[]{:S(2)}) collective-permute-start(bf16[384,1024]{1,0:T(8,128)(2,1)S(1)} %get-tuple-element.529), channel_id=1, source_target_pairs={{2,0},{3,1},{4,2},{5,3},{6,4},{7,5},{8,6},{9,7},{10,8},{11,9},{12,... | collective-permute-start | bytes 2359304 | tf_op jit(solution)/shard_map/ppermute | solution.py:19
  219.9 1576.3 %reduce-scatter.7.cloned.1.call-start = ((), (), s32[]{:S(2)}) async-start(), calls=%async_computation.9 | async-start | bytes 5242880 | tf_op jit(solution)/shard_map/reduce_scatter | solution.py:329
  255.5 482.8 %copy-start.35 = (f32[4,1,256]{2,1,0:T(1,128)}, f32[4,1,256]{2,1,0:T(1,128)S(1)}, u32[]{:S(2)}) copy-start(f32[4,1,256]{2,1,0:T(1,128)S(1)} %convert_element_type.155) | copy-start | bytes 12292
  266.1 434.1 %copy-start.37 = (f32[4,1,256]{2,1,0:T(1,128)}, f32[4,1,256]{2,1,0:T(1,128)S(1)}, u32[]{:S(2)}) copy-start(f32[4,1,256]{2,1,0:T(1,128)S(1)} %convert_element_type.156) | copy-start | bytes 12292
  271.5 30.4 %collective-permute-start.6 = (bf16[384,1024]{1,0:T(8,128)(2,1)S(1)}, bf16[384,1024]{1,0:T(8,128)(2,1)S(1)}, u32[]{:S(2)}, u32[]{:S(2)}) collective-permute-start(bf16[384,1024]{1,0:T(8,128)(2,1)S(1)} %get-tuple-element.529), channel_id=1, source_target_pairs={{3,0},{4,1},{5,2},{6,3},{7,4},{8,5},{9,6},{10,7},{11,8},{12,9},{13... | collective-permute-start | bytes 2359304 | tf_op jit(solution)/shard_map/ppermute | solution.py:19
  277.1 117.7 %collective-permute-start.7 = (bf16[384,1024]{1,0:T(8,128)(2,1)S(1)}, bf16[384,1024]{1,0:T(8,128)(2,1)S(1)}, u32[]{:S(2)}, u32[]{:S(2)}) collective-permute-start(bf16[384,1024]{1,0:T(8,128)(2,1)S(1)} %get-tuple-element.529), channel_id=1, source_target_pairs={{4,0},{5,1},{6,2},{7,3},{8,4},{9,5},{10,6},{11,7},{12,8},{13,9},{1... | collective-permute-start | bytes 2359304 | tf_op jit(solution)/shard_map/ppermute | solution.py:19
  280.5 126.2 %collective-permute-start.16 = (bf16[384,1024]{1,0:T(8,128)(2,1)S(1)}, bf16[384,1024]{1,0:T(8,128)(2,1)}, u32[]{:S(2)}, u32[]{:S(2)}) collective-permute-start(bf16[384,1024]{1,0:T(8,128)(2,1)S(1)} %copy-done.30), channel_id=1, source_target_pairs={{0,4},{1,5},{2,6},{3,7},{4,8},{5,9},{6,10},{7,11},{8,12},{9,13},{1... | collective-permute-start | bytes 2359304 | tf_op jit(solution)/shard_map/ppermute | solution.py:19
  289.4 120.6 %collective-permute-start.17 = (bf16[384,1024]{1,0:T(8,128)(2,1)S(1)}, bf16[384,1024]{1,0:T(8,128)(2,1)}, u32[]{:S(2)}, u32[]{:S(2)}) collective-permute-start(bf16[384,1024]{1,0:T(8,128)(2,1)S(1)} %copy-done.30), channel_id=1, source_target_pairs={{0,3},{1,4},{2,5},{3,6},{4,7},{5,8},{6,9},{7,10},{8,11},{9,12},{10... | collective-permute-start | bytes 2359304 | tf_op jit(solution)/shard_map/ppermute | solution.py:19
  296.2 117.2 %collective-permute-start.18 = (bf16[384,1024]{1,0:T(8,128)(2,1)S(1)}, bf16[384,1024]{1,0:T(8,128)(2,1)}, u32[]{:S(2)}, u32[]{:S(2)}) collective-permute-start(bf16[384,1024]{1,0:T(8,128)(2,1)S(1)} %copy-done.30), channel_id=1, source_target_pairs={{0,2},{1,3},{2,4},{3,5},{4,6},{5,7},{6,8},{7,9},{8,10},{9,11},{10,... | collective-permute-start | bytes 2359304 | tf_op jit(solution)/shard_map/ppermute | solution.py:19
  301.8 115.2 %collective-permute-start.19 = (bf16[384,1024]{1,0:T(8,128)(2,1)S(1)}, bf16[384,1024]{1,0:T(8,128)(2,1)}, u32[]{:S(2)}, u32[]{:S(2)}) collective-permute-start(bf16[384,1024]{1,0:T(8,128)(2,1)S(1)} %copy-done.30), channel_id=1, source_target_pairs={{0,1},{1,2},{2,3},{3,4},{4,5},{5,6},{6,7},{7,8},{8,9},{9,10},{10,1... | collective-permute-start | bytes 2359304 | tf_op jit(solution)/shard_map/ppermute | solution.py:19
  394.8 26.7 %collective-permute-start.20 = (bf16[384,1024]{1,0:T(8,128)(2,1)S(1)}, bf16[384,1024]{1,0:T(8,128)(2,1)S(1)}, u32[]{:S(2)}, u32[]{:S(2)}) collective-permute-start(bf16[384,1024]{1,0:T(8,128)(2,1)S(1)} %copy-done.30), channel_id=1, source_target_pairs={{1,0},{2,1},{3,2},{4,3},{5,4},{6,5},{7,6},{8,7},{9,8},{10,9},{11,1... | collective-permute-start | bytes 2359304 | tf_op jit(solution)/shard_map/ppermute | solution.py:19
  406.6 38.7 %collective-permute-start.21 = (bf16[384,1024]{1,0:T(8,128)(2,1)S(1)}, bf16[384,1024]{1,0:T(8,128)(2,1)S(1)}, u32[]{:S(2)}, u32[]{:S(2)}) collective-permute-start(bf16[384,1024]{1,0:T(8,128)(2,1)S(1)} %copy-done.30), channel_id=1, source_target_pairs={{2,0},{3,1},{4,2},{5,3},{6,4},{7,5},{8,6},{9,7},{10,8},{11,9},{12,... | collective-permute-start | bytes 2359304 | tf_op jit(solution)/shard_map/ppermute | solution.py:19
  410.1 54.0 %collective-permute-start.22 = (bf16[384,1024]{1,0:T(8,128)(2,1)S(1)}, bf16[384,1024]{1,0:T(8,128)(2,1)S(1)}, u32[]{:S(2)}, u32[]{:S(2)}) collective-permute-start(bf16[384,1024]{1,0:T(8,128)(2,1)S(1)} %copy-done.30), channel_id=1, source_target_pairs={{3,0},{4,1},{5,2},{6,3},{7,4},{8,5},{9,6},{10,7},{11,8},{12,9},{13... | collective-permute-start | bytes 2359304 | tf_op jit(solution)/shard_map/ppermute | solution.py:19
  413.4 99.4 %collective-permute-start.23 = (bf16[384,1024]{1,0:T(8,128)(2,1)S(1)}, bf16[384,1024]{1,0:T(8,128)(2,1)S(1)}, u32[]{:S(2)}, u32[]{:S(2)}) collective-permute-start(bf16[384,1024]{1,0:T(8,128)(2,1)S(1)} %copy-done.30), channel_id=1, source_target_pairs={{4,0},{5,1},{6,2},{7,3},{8,4},{9,5},{10,6},{11,7},{12,8},{13,9},{1... | collective-permute-start | bytes 2359304 | tf_op jit(solution)/shard_map/ppermute | solution.py:19
  751.7 1148.4 %reduce-scatter.5.cloned.1.call-start = ((), (), s32[]{:S(2)}) async-start(), calls=%async_computation.8 | async-start | bytes 15728640 | tf_op jit(solution)/shard_map/reduce_scatter | solution.py:326
  1112.4 36.9 %collective-permute-start.39 = (f32[384,1024]{1,0:T(8,128)S(1)}, f32[384,1024]{1,0:T(8,128)S(1)}, u32[]{:S(2)}, u32[]{:S(2)}) collective-permute-start(f32[384,1024]{1,0:T(8,128)S(1)} %get-tuple-element.527), channel_id=1, source_target_pairs={{0,4},{1,5},{2,6},{3,7},{4,8},{5,9},{6,10},{7,11},{8,12},{9,13},{1... | collective-permute-start | bytes 4718600 | tf_op jit(solution)/shard_map/ppermute | solution.py:19
  1114.7 68.6 %collective-permute-start.38 = (f32[384,1024]{1,0:T(8,128)}, f32[384,1024]{1,0:T(8,128)}, u32[]{:S(2)}, u32[]{:S(2)}) collective-permute-start(f32[384,1024]{1,0:T(8,128)} %get-tuple-element.521), channel_id=1, source_target_pairs={{0,3},{1,4},{2,5},{3,6},{4,7},{5,8},{6,9},{7,10},{8,11},{9,12},{10... | collective-permute-start | bytes 4718600 | tf_op jit(solution)/shard_map/ppermute | solution.py:19
  1117.1 99.8 %collective-permute-start.37 = (f32[384,1024]{1,0:T(8,128)}, f32[384,1024]{1,0:T(8,128)}, u32[]{:S(2)}, u32[]{:S(2)}) collective-permute-start(f32[384,1024]{1,0:T(8,128)} %get-tuple-element.522), channel_id=1, source_target_pairs={{0,2},{1,3},{2,4},{3,5},{4,6},{5,7},{6,8},{7,9},{8,10},{9,11},{10,... | collective-permute-start | bytes 4718600 | tf_op jit(solution)/shard_map/ppermute | solution.py:19
  1119.6 98.7 %collective-permute-start.36 = (f32[384,1024]{1,0:T(8,128)}, f32[384,1024]{1,0:T(8,128)}, u32[]{:S(2)}, u32[]{:S(2)}) collective-permute-start(f32[384,1024]{1,0:T(8,128)} %get-tuple-element.523), channel_id=1, source_target_pairs={{0,1},{1,2},{2,3},{3,4},{4,5},{5,6},{6,7},{7,8},{8,9},{9,10},{10,1... | collective-permute-start | bytes 4718600 | tf_op jit(solution)/shard_map/ppermute | solution.py:19
  1127.1 126.1 %collective-permute-start.35 = (f32[384,1024]{1,0:T(8,128)}, f32[384,1024]{1,0:T(8,128)}, u32[]{:S(2)}, u32[]{:S(2)}) collective-permute-start(f32[384,1024]{1,0:T(8,128)} %get-tuple-element.524), channel_id=1, source_target_pairs={{1,0},{2,1},{3,2},{4,3},{5,4},{6,5},{7,6},{8,7},{9,8},{10,9},{11,1... | collective-permute-start | bytes 4718600 | tf_op jit(solution)/shard_map/ppermute | solution.py:19
  1149.4 130.3 %collective-permute-start.34 = (f32[384,1024]{1,0:T(8,128)}, f32[384,1024]{1,0:T(8,128)}, u32[]{:S(2)}, u32[]{:S(2)}) collective-permute-start(f32[384,1024]{1,0:T(8,128)} %get-tuple-element.525), channel_id=1, source_target_pairs={{2,0},{3,1},{4,2},{5,3},{6,4},{7,5},{8,6},{9,7},{10,8},{11,9},{12,... | collective-permute-start | bytes 4718600 | tf_op jit(solution)/shard_map/ppermute | solution.py:19
  1150.7 381.8 %copy-start.12 = (f32[384,1024]{1,0:T(8,128)S(1)}, f32[384,1024]{1,0:T(8,128)}, u32[]{:S(2)}) copy-start(f32[384,1024]{1,0:T(8,128)} %get-tuple-element.315) | copy-start | bytes 4718596
  1159.9 372.7 %copy-start.27 = (f32[384,1024]{1,0:T(8,128)S(1)}, f32[384,1024]{1,0:T(8,128)}, u32[]{:S(2)}) copy-start(f32[384,1024]{1,0:T(8,128)} %copy-done.26) | copy-start | bytes 4718596
  1183.2 262.4 %collective-permute-start.33 = (f32[384,1024]{1,0:T(8,128)S(1)}, f32[384,1024]{1,0:T(8,128)S(1)}, u32[]{:S(2)}, u32[]{:S(2)}) collective-permute-start(f32[384,1024]{1,0:T(8,128)S(1)} %get-tuple-element.526), channel_id=1, source_target_pairs={{3,0},{4,1},{5,2},{6,3},{7,4},{8,5},{9,6},{10,7},{11,8},{12,9},{13... | collective-permute-start | bytes 4718600 | tf_op jit(solution)/shard_map/ppermute | solution.py:19
  1216.9 310.3 %collective-permute-start.32 = (f32[384,1024]{1,0:T(8,128)S(1)}, f32[384,1024]{1,0:T(8,128)S(1)}, u32[]{:S(2)}, u32[]{:S(2)}) collective-permute-start(f32[384,1024]{1,0:T(8,128)S(1)} %get-tuple-element.520), channel_id=1, source_target_pairs={{4,0},{5,1},{6,2},{7,3},{8,4},{9,5},{10,6},{11,7},{12,8},{13,9},{1... | collective-permute-start | bytes 4718600 | tf_op jit(solution)/shard_map/ppermute | solution.py:19
  1218.2 310.3 %collective-permute-start.31 = (f32[384,1024]{1,0:T(8,128)}, f32[384,1024]{1,0:T(8,128)S(1)}, u32[]{:S(2)}, u32[]{:S(2)}) collective-permute-start(f32[384,1024]{1,0:T(8,128)} %get-tuple-element.519), channel_id=1, source_target_pairs={{0,4},{1,5},{2,6},{3,7},{4,8},{5,9},{6,10},{7,11},{8,12},{9,13},{1... | collective-permute-start | bytes 4718600 | tf_op jit(solution)/shard_map/ppermute | solution.py:19
  1253.2 276.6 %collective-permute-start.30 = (f32[384,1024]{1,0:T(8,128)}, f32[384,1024]{1,0:T(8,128)S(1)}, u32[]{:S(2)}, u32[]{:S(2)}) collective-permute-start(f32[384,1024]{1,0:T(8,128)} %get-tuple-element.513), channel_id=1, source_target_pairs={{0,3},{1,4},{2,5},{3,6},{4,7},{5,8},{6,9},{7,10},{8,11},{9,12},{10... | collective-permute-start | bytes 4718600 | tf_op jit(solution)/shard_map/ppermute | solution.py:19
  1279.6 251.5 %collective-permute-start.29 = (f32[384,1024]{1,0:T(8,128)}, f32[384,1024]{1,0:T(8,128)S(1)}, u32[]{:S(2)}, u32[]{:S(2)}) collective-permute-start(f32[384,1024]{1,0:T(8,128)} %get-tuple-element.514), channel_id=1, source_target_pairs={{0,2},{1,3},{2,4},{3,5},{4,6},{5,7},{6,8},{7,9},{8,10},{9,11},{10,... | collective-permute-start | bytes 4718600 | tf_op jit(solution)/shard_map/ppermute | solution.py:19
  1445.6 92.7 %collective-permute-start.28 = (f32[384,1024]{1,0:T(8,128)}, f32[384,1024]{1,0:T(8,128)S(1)}, u32[]{:S(2)}, u32[]{:S(2)}) collective-permute-start(f32[384,1024]{1,0:T(8,128)} %get-tuple-element.515), channel_id=1, source_target_pairs={{0,1},{1,2},{2,3},{3,4},{4,5},{5,6},{6,7},{7,8},{8,9},{9,10},{10,1... | collective-permute-start | bytes 4718600 | tf_op jit(solution)/shard_map/ppermute | solution.py:19
  1527.2 61.1 %collective-permute-start.27 = (f32[384,1024]{1,0:T(8,128)}, f32[384,1024]{1,0:T(8,128)S(1)}, u32[]{:S(2)}, u32[]{:S(2)}) collective-permute-start(f32[384,1024]{1,0:T(8,128)} %get-tuple-element.516), channel_id=1, source_target_pairs={{1,0},{2,1},{3,2},{4,3},{5,4},{6,5},{7,6},{8,7},{9,8},{10,9},{11,1... | collective-permute-start | bytes 4718600 | tf_op jit(solution)/shard_map/ppermute | solution.py:19
  1528.5 99.7 %collective-permute-start.26 = (f32[384,1024]{1,0:T(8,128)}, f32[384,1024]{1,0:T(8,128)S(1)}, u32[]{:S(2)}, u32[]{:S(2)}) collective-permute-start(f32[384,1024]{1,0:T(8,128)} %get-tuple-element.517), channel_id=1, source_target_pairs={{2,0},{3,1},{4,2},{5,3},{6,4},{7,5},{8,6},{9,7},{10,8},{11,9},{12,... | collective-permute-start | bytes 4718600 | tf_op jit(solution)/shard_map/ppermute | solution.py:19
  1529.8 159.2 %collective-permute-start.25 = (f32[384,1024]{1,0:T(8,128)}, f32[384,1024]{1,0:T(8,128)S(1)}, u32[]{:S(2)}, u32[]{:S(2)}) collective-permute-start(f32[384,1024]{1,0:T(8,128)} %get-tuple-element.518), channel_id=1, source_target_pairs={{3,0},{4,1},{5,2},{6,3},{7,4},{8,5},{9,6},{10,7},{11,8},{12,9},{13... | collective-permute-start | bytes 4718600 | tf_op jit(solution)/shard_map/ppermute | solution.py:19
  1531.1 232.0 %collective-permute-start.24 = (f32[384,1024]{1,0:T(8,128)S(1)}, f32[384,1024]{1,0:T(8,128)S(1)}, u32[]{:S(2)}, u32[]{:S(2)}) collective-permute-start(f32[384,1024]{1,0:T(8,128)S(1)} %get-tuple-element.512), channel_id=1, source_target_pairs={{4,0},{5,1},{6,2},{7,3},{8,4},{9,5},{10,6},{11,7},{12,8},{13,9},{1... | collective-permute-start | bytes 4718600 | tf_op jit(solution)/shard_map/ppermute | solution.py:19
  1532.7 233.2 %copy-start.22 = (bf16[384,1024]{1,0:T(8,128)(2,1)}, bf16[384,1024]{1,0:T(8,128)(2,1)S(1)}, u32[]{:S(2)}) copy-start(bf16[384,1024]{1,0:T(8,128)(2,1)S(1)} %get-tuple-element.534) | copy-start | bytes 2359300
  1538.3 227.7 %copy-start.4 = (bf16[384,1024]{1,0:T(8,128)(2,1)S(1)}, bf16[384,1024]{1,0:T(8,128)(2,1)}, u32[]{:S(2)}) copy-start(bf16[384,1024]{1,0:T(8,128)(2,1)} %param.23) | copy-start | bytes 2359300
  1538.3 227.7 %copy-start.32 = (f32[4,1,256]{2,1,0:T(1,128)S(1)}, f32[4,1,256]{2,1,0:T(1,128)}, u32[]{:S(2)}) copy-start(f32[4,1,256]{2,1,0:T(1,128)} %copy-done.31) | copy-start | bytes 12292
  1538.3 227.7 %copy-start.34 = (f32[4,1,256]{2,1,0:T(1,128)S(1)}, f32[4,1,256]{2,1,0:T(1,128)}, u32[]{:S(2)}) copy-start(f32[4,1,256]{2,1,0:T(1,128)} %copy-done.33) | copy-start | bytes 12292
  1538.3 227.7 %copy-start.40 = (f32[384]{0:T(512)S(1)}, f32[384]{0:T(512)}, u32[]{:S(2)}) copy-start(f32[384]{0:T(512)} %copy-done.39) | copy-start | bytes 4612
  1538.3 227.7 %copy-start.42 = (f32[384]{0:T(512)S(1)}, f32[384]{0:T(512)}, u32[]{:S(2)}) copy-start(f32[384]{0:T(512)} %copy-done.41) | copy-start | bytes 4612
  1773.0 254.8 %reduce-scatter.9.cloned.1.call-start = ((), (), s32[]{:S(2)}) async-start(), calls=%async_computation.10 | async-start | bytes 20971520 | tf_op jit(solution)/shard_map/reduce_scatter | solution.py:334
  1784.6 370.8 %reduce-scatter.11.cloned.1.call-start = ((), (), s32[]{:S(2)}) async-start(), calls=%async_computation.11 | async-start | bytes 20971520 | tf_op jit(solution)/shard_map/reduce_scatter | solution.py:336
  1795.9 759.6 %all-reduce.16.cloned.1.call-start = ((), (), s32[]{:S(2)}) async-start(), calls=%async_computation.12 | async-start | bytes 25165824 | tf_op jit(solution)/shard_map/psum | solution.py:357
  (111 other events, 1311.0 us)
Sparse Core Ops, SparseCore 0:
  9.6 49.1 all-gather.14
  60.3 22.5 all-gather.16
  84.5 79.5 all-gather.18
  220.1 65.8 all-gather.20
  751.8 43.0 reduce-scatter.6
  1773.1 126.9 reduce-scatter.4
  1902.7 125.0 reduce-scatter.8
  2030.4 125.0 reduce-scatter.10
  2160.2 395.2 all-reduce.15
where the time goes:
time: 2590 us; the launch traced here: 2570 us
  waiting for transfers between devices  1220 us (47%)
  starting transfers between devices  492 us (19%)
  matrix products  362 us (14%)
  local copies, waits for them, and re-layouts  261 us (10%)
  blocking collectives  118 us (5%)
  other arithmetic  100 us (4%)
    ppermute x40, waiting for transfers between devices, from_behind(): return lax.ppermute(block, axis, route)  499 us
    ppermute x40, starting transfers between devices, from_behind(): return lax.ppermute(block, axis, route)  491 us
    psum x1, waiting for transfers between devices, shards(): lax.psum((owned_gain1, owned_shift1, owned_qkv, owned_qbias, owned_vbias,...  335 us
    reduce_scatter x1, waiting for transfers between devices, shards(): lax.psum_scatter(down_grad, 'fsdp', scatter_dimension=0, tiled=True)  128 us
    reduce_scatter x1, waiting for transfers between devices, shards(): lax.psum_scatter(up_grad, 'fsdp', scatter_dimension=0, tiled=True)  128 us
    dot_general x16, matrix products, pair_scores(): jnp.einsum('qhd,khd->hqk', query_pair.reshape(tok_rows, 2, HEAD_DIM), key...  108 us
    reduce_scatter x1, waiting for transfers between devices, shards(): lax.psum_scatter(qkv_weight_grad, 'fsdp', scatter_dimension=0, tiled=True)  104 us
    unnamed x193, local copies, waits for them, and re-layouts  70.9 us
  transfers between devices with their start and end apart: 49, of which 26 were waited for; matrix products, arithmetic and copies ran while one was open for 25% of the time, Pallas kernels for 0%

commit v1 on v0

v1 whole, which is shorter than its diff:
```python
import functools

import jax
import jax.numpy as jnp
from jax import lax
from jax.experimental import pallas as pl
from jax.experimental.pallas import tpu as pltpu
from jax.sharding import PartitionSpec as P

D = 1024
HEADS = 16
HEAD_DIM = 64
IMG = 1370

PAIR = 2 * HEAD_DIM
GROUP = HEADS // 2
BLOCK = 256
HALO = 1408
SLOTS = 63

EPSILON = 1e-06
NEG_BIG = -1e30
NEG_EDGE = -1e29

NT = (((1,), (1,)), ((), ()))


def from_behind(block, axis, distance):
    devices = range(lax.axis_size(axis))
    route = [(i - distance, i) for i in devices if i - distance in devices]
    return lax.ppermute(block, axis, route)


def normalize(values):
    center = jnp.mean(values, axis=-1, keepdims=True)
    centered = values - center
    spread = jnp.mean(centered * centered, axis=-1, keepdims=True)
    scale = lax.rsqrt(spread + EPSILON)
    return centered * scale, scale


def norm_back(cotangent, unit, scale, gain):
    scaled = cotangent * gain
    along = jnp.mean(scaled, axis=-1, keepdims=True)
    across = jnp.mean(scaled * unit, axis=-1, keepdims=True)
    return scale * (scaled - along - unit * across)


def matmul(left, right):
    return jnp.dot(left, right, preferred_element_type=jnp.float32)


def matmul_nt(left, right):
    return jnp.einsum("te,de->td", left, right, preferred_element_type=jnp.float32)


def matmul_tn(left, right):
    return jnp.einsum("td,te->de", left, right, preferred_element_type=jnp.float32)


def fold_rows(values, op):
    return op(values.reshape(values.shape[0] // 8, 8, values.shape[1]), axis=0)


def attend_kernel(meta, q_ref, k_ref, v_ref, o_ref, ot_ref, lse_ref, vt, scores):
    tiles = o_ref.shape[0] // BLOCK
    window = k_ref.shape[1]

    @pl.loop(0, window // BLOCK)
    def _(i):
        at = pl.ds(pl.multiple_of(i * BLOCK, BLOCK), BLOCK)
        vt[:, at] = v_ref[at, :].T

    @pl.loop(0, tiles)
    def _(t):
        start = meta[2 * t]
        count = meta[2 * t + 1]
        rows = pl.ds(pl.multiple_of(t * BLOCK, BLOCK), BLOCK)
        query = [q_ref[h, rows, :] for h in range(2)]

        def score(i, tops):
            at = pl.ds(pl.multiple_of(start + i * BLOCK, 128), BLOCK)
            keep = pl.ds(pl.multiple_of(i * BLOCK, BLOCK), BLOCK)
            new = []
            for h in range(2):
                part = lax.dot_general(
                    k_ref[h, at, :], query[h], NT, preferred_element_type=jnp.float32
                )
                scores[h, keep, :] = part
                new.append(jnp.maximum(tops[h], fold_rows(part, jnp.max)))
            return tuple(new)

        low = jnp.full((8, BLOCK), NEG_BIG, jnp.float32)
        tops = lax.fori_loop(0, count, score, (low, low))
        tops = [jnp.max(top, axis=0, keepdims=True) for top in tops]
        tops = [jnp.where(top < NEG_EDGE, 0.0, top) for top in tops]

        def mix(i, carry):
            at = pl.ds(pl.multiple_of(start + i * BLOCK, 128), BLOCK)
            keep = pl.ds(pl.multiple_of(i * BLOCK, BLOCK), BLOCK)
            new = []
            for h in range(2):
                total, mixed = carry[h]
                weights = jnp.exp(scores[h, keep, :] - tops[h])
                total = total + fold_rows(weights, jnp.sum)
                mixed = mixed + matmul(
                    vt[h * HEAD_DIM : (h + 1) * HEAD_DIM, at], weights.astype(jnp.bfloat16)
                )
                new.append((total, mixed))
            return tuple(new)

        zero = (jnp.zeros((8, BLOCK), jnp.float32), jnp.zeros((HEAD_DIM, BLOCK), jnp.float32))
        done = lax.fori_loop(0, count, mix, (zero, zero))
        outs = []
        for h in range(2):
            total = jnp.sum(done[h][0], axis=0, keepdims=True)
            total = jnp.where(total > 0, total, 1.0)
            lse_ref[h : h + 1, rows] = tops[h] + jnp.log(total)
            outs.append(done[h][1] / total)
        out = jnp.concatenate(outs, axis=0)
        ot_ref[:, rows] = out
        o_ref[rows, :] = out.T.astype(jnp.bfloat16)


def attend(meta, q_aug, k_aug, values):
    rows = q_aug.shape[1]
    window = k_aug.shape[1]
    deepest = (2 * IMG + 3 * BLOCK) // BLOCK * BLOCK
    vmem = pl.BlockSpec(memory_space=pltpu.VMEM)
    return pl.pallas_call(
        attend_kernel,
        out_shape=(
            jax.ShapeDtypeStruct((rows, PAIR), jnp.bfloat16),
            jax.ShapeDtypeStruct((PAIR, rows), jnp.float32),
            jax.ShapeDtypeStruct((8, rows), jnp.float32),
        ),
        in_specs=[pl.BlockSpec(memory_space=pltpu.SMEM), vmem, vmem, vmem],
        out_specs=(vmem, vmem, vmem),
        scratch_shapes=[
            pltpu.VMEM((PAIR, window), jnp.bfloat16),
            pltpu.VMEM((2, deepest, BLOCK), jnp.float32),
        ],
        cost_estimate=pl.CostEstimate(
            flops=4 * rows * 2 * IMG * PAIR, transcendentals=2 * rows * IMG, bytes_accessed=9 << 20
        ),
        name="attend",
    )(meta, q_aug, k_aug, values)


def attend_back_kernel(
    meta, q_ref, k_ref, v_ref, g_ref, ot_ref, lse_ref, dq_ref, dk_ref, dv_ref, kt
):
    tiles = dq_ref.shape[0] // BLOCK
    window = k_ref.shape[1]
    half = lax.broadcasted_iota(jnp.int32, (BLOCK, PAIR), 1) // HEAD_DIM

    @pl.loop(0, window // BLOCK)
    def _(i):
        at = pl.ds(pl.multiple_of(i * BLOCK, BLOCK), BLOCK)
        kt[:, at] = jnp.where(half == 0, k_ref[0, at, :], k_ref[1, at, :]).T
        dk_ref[at, :] = jnp.zeros((BLOCK, PAIR), jnp.float32)
        dv_ref[at, :] = jnp.zeros((BLOCK, PAIR), jnp.float32)

    @pl.loop(0, tiles)
    def _(t):
        start = meta[2 * t]
        count = meta[2 * t + 1]
        rows = pl.ds(pl.multiple_of(t * BLOCK, BLOCK), BLOCK)
        grad = g_ref[rows, :]
        blank = jnp.zeros_like(grad)
        query = [q_ref[h, rows, :] for h in range(2)]
        query_only = jnp.concatenate(
            [jnp.where(half == h, query[h], blank) for h in range(2)], axis=0
        )
        grads = [jnp.where(half == h, grad, blank) for h in range(2)]
        grads_both = jnp.concatenate(grads, axis=0)
        product = grad.astype(jnp.float32).T * ot_ref[:, rows]
        delta = [
            jnp.sum(product[h * HEAD_DIM : (h + 1) * HEAD_DIM], axis=0, keepdims=True)
            for h in range(2)
        ]
        lse = [lse_ref[h : h + 1, rows] for h in range(2)]

        def step(i, carry):
            at = pl.ds(pl.multiple_of(start + i * BLOCK, 128), BLOCK)
            value = v_ref[at, :]
            probs, slopes, new = [], [], []
            for h in range(2):
                part = lax.dot_general(
                    k_ref[h, at, :], query[h], NT, preferred_element_type=jnp.float32
                )
                weights = jnp.exp(part - lse[h])
                pull = lax.dot_general(value, grads[h], NT, preferred_element_type=jnp.float32)
                slope = (weights * (pull - delta[h])).astype(jnp.bfloat16)
                probs.append(weights.astype(jnp.bfloat16))
                slopes.append(slope)
                new.append(carry[h] + matmul(kt[h * HEAD_DIM : (h + 1) * HEAD_DIM, at], slope))
            dv_ref[at, :] += matmul(jnp.concatenate(probs, axis=1), grads_both)
            dk_ref[at, :] += matmul(jnp.concatenate(slopes, axis=1), query_only)
            return tuple(new)

        zero = jnp.zeros((HEAD_DIM, BLOCK), jnp.float32)
        done = lax.fori_loop(0, count, step, (zero, zero))
        dq = jnp.concatenate(done, axis=0) * (HEAD_DIM**-0.5)
        dq_ref[rows, :] = dq.T.astype(jnp.bfloat16)


def attend_back(meta, q_aug, k_aug, values, grad, out_t, lse):
    rows = q_aug.shape[1]
    window = k_aug.shape[1]
    vmem = pl.BlockSpec(memory_space=pltpu.VMEM)
    return pl.pallas_call(
        attend_back_kernel,
        out_shape=(
            jax.ShapeDtypeStruct((rows, PAIR), jnp.bfloat16),
            jax.ShapeDtypeStruct((window, PAIR), jnp.float32),
            jax.ShapeDtypeStruct((window, PAIR), jnp.float32),
        ),
        in_specs=[pl.BlockSpec(memory_space=pltpu.SMEM)] + [vmem] * 6,
        out_specs=(vmem, vmem, vmem),
        scratch_shapes=[pltpu.VMEM((PAIR, window), jnp.bfloat16)],
        cost_estimate=pl.CostEstimate(
            flops=10 * rows * 2 * IMG * PAIR, transcendentals=2 * rows * IMG, bytes_accessed=16 << 20
        ),
        name="attend_back",
    )(meta, q_aug, k_aug, values, grad, out_t, lse)


def shards(
    tokens,
    out_grad,
    norm1_gain,
    norm1_bias,
    w_qkv,
    q_bias,
    v_bias,
    w_out,
    out_bias,
    attn_scale,
    norm2_gain,
    norm2_bias,
    w_up,
    up_bias,
    w_down,
    down_bias,
    mlp_scale,
    image_ids,
    pad_mask,
):
    both = ("fsdp", "rep")
    owners = lax.axis_size("fsdp")
    replicas = lax.axis_size("rep")
    me = lax.axis_index("fsdp") * replicas + lax.axis_index("rep")
    tok_rows = tokens.shape[0]
    rows = GROUP * tok_rows
    groups = [list(range(g, g + GROUP)) for g in range(0, replicas, GROUP)]
    factor = HEAD_DIM ** (-0.5)

    small = (
        norm1_gain,
        norm1_bias,
        q_bias,
        v_bias,
        out_bias,
        attn_scale,
        norm2_gain,
        norm2_bias,
        down_bias,
        mlp_scale,
        up_bias,
    )
    vectors = lax.all_gather(jnp.concatenate(small), "fsdp", axis=0, tiled=False).astype(
        jnp.float32
    )
    parts = []
    place = 0
    for member in small:
        parts.append(vectors[:, place : place + member.shape[0]].reshape(-1))
        place += member.shape[0]
    (
        gain_first,
        shift_first,
        query_bias,
        value_bias,
        proj_bias,
        attn_gamma,
        gain_second,
        shift_second,
        final_bias,
        mlp_gamma,
        hidden_bias,
    ) = parts

    codes = lax.all_gather(
        jnp.where(pad_mask > 0, image_ids + 1, 0), both, axis=0, tiled=True
    )
    wide_qkv = lax.all_gather(w_qkv, "fsdp", axis=0, tiled=True)
    wide_out = lax.all_gather(w_out, "fsdp", axis=0, tiled=True)
    wide_up = lax.all_gather(w_up, "fsdp", axis=0, tiled=True)
    wide_down = lax.all_gather(w_down, "fsdp", axis=0, tiled=True)

    window = HALO + rows + HALO + BLOCK
    padded = jnp.concatenate(
        [jnp.zeros((HALO,), jnp.int32), codes, jnp.zeros((HALO + BLOCK,), jnp.int32)]
    )
    seen = lax.dynamic_slice_in_dim(padded, (me // GROUP) * rows, window, 0)
    spot = jnp.arange(window, dtype=jnp.int32)
    seen = jnp.where(spot < window - BLOCK, seen, 0)
    asked = seen[HALO : HALO + rows]
    tile_codes = asked.reshape(rows // BLOCK, BLOCK)
    first_code = jnp.min(jnp.where(tile_codes > 0, tile_codes, 1 << 30), axis=1)
    last_code = jnp.max(tile_codes, axis=1)
    begin = jnp.min(jnp.where(seen[None] == first_code[:, None], spot[None], window), axis=1)
    finish = jnp.max(jnp.where(seen[None] == last_code[:, None], spot[None] + 1, 0), axis=1)
    begin = begin // 128 * 128
    count = jnp.where(last_code > 0, (finish - begin + BLOCK - 1) // BLOCK, 0)
    meta = jnp.stack([begin, count], axis=1).reshape(-1)

    lane = jnp.arange(PAIR, dtype=jnp.int32)
    lane_half = lane // HEAD_DIM
    lane_slot = lane % HEAD_DIM
    key_slot = jnp.where(seen > 0, 1 + (seen - 1) % SLOTS, 0)
    ask_slot = key_slot[HALO : HALO + rows]
    key_marks = (key_slot[:, None] == lane_slot[None]).astype(jnp.bfloat16)
    ask_marks = jnp.where(
        (ask_slot[:, None] == lane_slot[None]) & (ask_slot[:, None] > 0), 0.0, NEG_BIG
    ).astype(jnp.bfloat16)

    inputs = tokens.astype(jnp.float32)
    unit_one, scale_one = normalize(inputs)
    act_one = (unit_one * gain_first + shift_first).astype(jnp.bfloat16)
    qkv_rows = matmul(act_one, wide_qkv)
    query = ((qkv_rows[:, :D] + query_bias) * factor).astype(jnp.bfloat16)
    keys = qkv_rows[:, D : 2 * D].astype(jnp.bfloat16)
    values = (qkv_rows[:, 2 * D :] + value_bias).astype(jnp.bfloat16)
    sent = jnp.stack(
        [member.reshape(tok_rows, GROUP, PAIR) for member in (query, keys, values)], axis=2
    )
    sent = sent.transpose(1, 0, 2, 3).reshape(GROUP, tok_rows, 3 * PAIR)

    def exchange(block):
        return lax.all_to_all(
            block, "rep", split_axis=0, concat_axis=0, tiled=True, axis_index_groups=groups
        )

    mine = exchange(sent).reshape(rows, 3 * PAIR)
    before = from_behind(mine[rows - HALO :, PAIR:], both, GROUP)
    after = from_behind(mine[:HALO, PAIR:], both, -GROUP)
    pad = jnp.zeros((BLOCK, 2 * PAIR), jnp.bfloat16)
    key_value = jnp.concatenate([before, mine[:, PAIR:], after, pad], axis=0)
    value_window = key_value[:, PAIR:]
    k_aug = jnp.stack(
        [jnp.where(lane_half[None] == h, key_value[:, :PAIR], key_marks) for h in range(2)]
    )
    q_aug = jnp.stack(
        [jnp.where(lane_half[None] == h, mine[:, :PAIR], ask_marks) for h in range(2)]
    )
    attn_mine, attn_t, lse = attend(meta, q_aug, k_aug, value_window)

    def to_tokens(block):
        back = exchange(block.reshape(GROUP, tok_rows, block.shape[-1]))
        return back.transpose(1, 0, 2)

    attn_low = to_tokens(attn_mine).reshape(tok_rows, D)
    proj = matmul(attn_low, wide_out) + proj_bias
    residual = inputs + attn_gamma * proj
    unit_two, scale_two = normalize(residual)
    act_two = (unit_two * gain_second + shift_second).astype(jnp.bfloat16)
    pre_act = matmul(act_two, wide_up) + hidden_bias
    phi_cdf = 0.5 * (1.0 + lax.erf(pre_act * (0.5**0.5)))
    hidden = (pre_act * phi_cdf).astype(jnp.bfloat16)
    slope = phi_cdf + pre_act * (jnp.exp(-0.5 * pre_act * pre_act) * 0.3989422804014327)
    branch = matmul(hidden, wide_down) + final_bias
    layer_out = (residual + mlp_gamma * branch).astype(jnp.bfloat16)

    upstream = out_grad.astype(jnp.float32)
    mlp_gamma_grad = jnp.sum(upstream * branch, axis=0)
    branch_grad = mlp_gamma * upstream
    final_bias_grad = jnp.sum(branch_grad, axis=0)
    branch_low = branch_grad.astype(jnp.bfloat16)
    down_grad = matmul_tn(hidden, branch_low).astype(jnp.bfloat16)
    pre_grad = matmul_nt(branch_low, wide_down) * slope
    hidden_bias_grad = jnp.sum(pre_grad, axis=0)
    pre_low = pre_grad.astype(jnp.bfloat16)
    up_grad = matmul_tn(act_two, pre_low).astype(jnp.bfloat16)
    act_two_grad = matmul_nt(pre_low, wide_up)
    gain_second_grad = jnp.sum(act_two_grad * unit_two, axis=0)
    shift_second_grad = jnp.sum(act_two_grad, axis=0)
    residual_grad = upstream + norm_back(act_two_grad, unit_two, scale_two, gain_second)
    attn_gamma_grad = jnp.sum(residual_grad * proj, axis=0)
    proj_grad = attn_gamma * residual_grad
    proj_bias_grad = jnp.sum(proj_grad, axis=0)
    proj_low = proj_grad.astype(jnp.bfloat16)
    out_weight_grad = matmul_tn(attn_low, proj_low).astype(jnp.bfloat16)
    attn_grad_low = matmul_nt(proj_low, wide_out).astype(jnp.bfloat16)

    grad_sent = attn_grad_low.reshape(tok_rows, GROUP, PAIR).transpose(1, 0, 2)
    grad_mine = exchange(grad_sent).reshape(rows, PAIR)
    dq, dk, dv = attend_back(meta, q_aug, k_aug, value_window, grad_mine, attn_t, lse)
    dkv = jnp.concatenate([dk, dv], axis=1)
    tail = dkv[:HALO].astype(jnp.bfloat16)
    head = dkv[HALO + rows : HALO + rows + HALO].astype(jnp.bfloat16)
    from_after = from_behind(tail, both, -GROUP).astype(jnp.float32)
    from_before = from_behind(head, both, GROUP).astype(jnp.float32)
    own = dkv[HALO : HALO + rows]
    gap = jnp.zeros((rows - HALO, 2 * PAIR), jnp.float32)
    own = (
        own
        + jnp.concatenate([from_before, gap], axis=0)
        + jnp.concatenate([gap, from_after], axis=0)
    )
    dqkv_mine = jnp.concatenate([dq, own.astype(jnp.bfloat16)], axis=1)
    dqkv = to_tokens(dqkv_mine).reshape(tok_rows, GROUP, 3, PAIR)
    dqkv = dqkv.transpose(0, 2, 1, 3).reshape(tok_rows, 3 * D)
    query_bias_grad = jnp.sum(dqkv[:, :D].astype(jnp.float32), axis=0)
    value_bias_grad = jnp.sum(dqkv[:, 2 * D :].astype(jnp.float32), axis=0)
    qkv_weight_grad = matmul_tn(act_one, dqkv).astype(jnp.bfloat16)
    act_one_grad = matmul_nt(dqkv, wide_qkv)
    gain_first_grad = jnp.sum(act_one_grad * unit_one, axis=0)
    shift_first_grad = jnp.sum(act_one_grad, axis=0)
    input_part = norm_back(act_one_grad, unit_one, scale_one, gain_first)
    tokens_grad = (residual_grad + input_part).astype(jnp.bfloat16)

    small_grads = (
        gain_first_grad,
        shift_first_grad,
        query_bias_grad,
        value_bias_grad,
        proj_bias_grad,
        attn_gamma_grad,
        gain_second_grad,
        shift_second_grad,
        final_bias_grad,
        mlp_gamma_grad,
        hidden_bias_grad,
    )
    packed = jnp.concatenate([member.reshape(owners, -1) for member in small_grads], axis=1)
    packed = lax.psum(packed, both)
    packed = lax.dynamic_slice_in_dim(packed, lax.axis_index("fsdp"), 1, 0)[0]
    small_out = []
    place = 0
    for member in small_grads:
        size = member.shape[0] // owners
        small_out.append(packed[place : place + size])
        place += size

    def reduced(partial):
        owned = lax.psum_scatter(partial, "fsdp", scatter_dimension=0, tiled=True)
        return lax.psum(owned, "rep").astype(jnp.float32)

    down_out = reduced(down_grad)
    up_out = reduced(up_grad)
    out_out = reduced(out_weight_grad)
    qkv_out = reduced(qkv_weight_grad)
    return (
        layer_out,
        tokens_grad,
        small_out[0],
        small_out[1],
        qkv_out,
        small_out[2],
        small_out[3],
        out_out,
        small_out[4],
        small_out[5],
        small_out[6],
        small_out[7],
        up_out,
        small_out[10],
        down_out,
        small_out[8],
        small_out[9],
    )


def solution(mesh):
    spread = P(("fsdp", "rep"), None)
    line = P("fsdp")
    plane = P("fsdp", None)
    return jax.shard_map(
        shards,
        mesh=mesh,
        in_specs=(
            spread,
            spread,
            line,
            line,
            plane,
            line,
            line,
            plane,
            line,
            line,
            line,
            line,
            plane,
            line,
            plane,
            line,
            line,
            P(("fsdp", "rep")),
            P(("fsdp", "rep")),
        ),
        out_specs=(
            spread,
            spread,
            line,
            line,
            plane,
            line,
            line,
            plane,
            line,
            line,
            line,
            line,
            plane,
            line,
            plane,
            line,
            line,
        ),
        check_vma=False,
    )
```

time: 2590 us -> 824 us (0.32)
  waiting for transfers between devices: 1220 us -> 280 us
  starting transfers between devices: 492 us -> 44.4 us
  matrix products: 362 us -> 80.9 us
  local copies, waits for them, and re-layouts: 261 us -> 24.7 us
  blocking collectives: 118 us -> 227 us
  Pallas kernels: 0 us -> 106 us
  other arithmetic: 100 us -> 36.3 us
    ppermute x40 -> x4, waiting for transfers between devices: 499 us -> 1.75 us  [from_behind(): return lax.ppermute(block, axis, route)]
    ppermute x40 -> x4, starting transfers between devices: 491 us -> 34.7 us  [from_behind(): return lax.ppermute(block, axis, route)]
    reduce_scatter x4, waiting for transfers between devices: 359 us -> 64.7 us  [reduced(): owned = lax.psum_scatter(partial, 'fsdp', scatter_dimension=0, tiled=True)]
    dot_general x56 -> x0, matrix products: 266 us -> none  [the longest x16 108 us: pair_scores(): jnp.einsum('qhd,khd->hqk', query_pair.reshape(tok_rows, 2, HEAD_DIM), key...]
    psum x1, waiting for transfers between devices: 335 us -> 159 us  [reduced(): return lax.psum(owned, 'rep').astype(jnp.float32)]
    pallas_call x0 -> x2, Pallas kernels: none -> 106 us  [the longest x1 65.2 us: attend_back(): pl.pallas_call(attend_back_kernel, out_shape=(jax.ShapeDtypeStruct((rows,...]
    all_to_all x0 -> x2, blocking collectives: none -> 67.6 us  [exchange(): lax.all_to_all(block, 'rep', split_axis=0, concat_axis=0, tiled=True, axi...]
    dynamic_update_slice x48 -> x0, local copies, waits for them, and re-layouts: 63.9 us -> none  [the longest x16 38.2 us: backward_pair(): lax.dynamic_update_slice_in_dim(value_grad, value_part, column, 1)]
  transfers between devices with their start and end apart: 49 -> 15, of which waited for: 26 -> 5; matrix products, arithmetic and copies ran while one was open for 25% -> 12% of each run, Pallas kernels for 0% -> 13%
where the time goes in v1:
time: 824 us; the launch traced here: 815 us
  waiting for transfers between devices  280 us (34%)
  blocking collectives  227 us (28%)
  Pallas kernels  106 us (13%)
  matrix products  80.9 us (10%)
  starting transfers between devices  44.4 us (5%)
  other arithmetic  36.3 us (4%)
  local copies, waits for them, and re-layouts  24.7 us (3%)
  between operations  15 us (2%)
    psum x1, waiting for transfers between devices, reduced(): return lax.psum(owned, 'rep').astype(jnp.float32)  159 us
    all_gather x1, blocking collectives, shards(): lax.all_gather(jnp.where(pad_mask > 0, image_ids + 1, 0), both, axis=0, t...  110 us
    all_to_all x2, blocking collectives, exchange(): lax.all_to_all(block, 'rep', split_axis=0, concat_axis=0, tiled=True, axi...  67.6 us
    pallas_call x1, Pallas kernels, attend_back(): pl.pallas_call(attend_back_kernel, out_shape=(jax.ShapeDtypeStruct((rows,...  65.2 us
    reduce_scatter x4, waiting for transfers between devices, reduced(): owned = lax.psum_scatter(partial, 'fsdp', scatter_dimension=0, tiled=True)  64.7 us
    psum x1, blocking collectives, shards(): packed = lax.psum(packed, both)  43.6 us
    pallas_call x1, Pallas kernels, attend(): pl.pallas_call(attend_kernel, out_shape=(jax.ShapeDtypeStruct((rows, PAIR...  40.4 us
    all_gather x1, waiting for transfers between devices, shards(): wide_qkv = lax.all_gather(w_qkv, 'fsdp', axis=0, tiled=True)  39.8 us
  transfers between devices with their start and end apart: 15, of which 5 were waited for; matrix products, arithmetic and copies ran while one was open for 12% of the time, Pallas kernels for 13%

profile of v1, /device:TPU:0, one launch (start us, length us, event | category | flops | bytes accessed | tf_op | source)
XLA Modules:
  0.0 814.6 jit_solution(4869024768214454979)
XLA Ops:
  7.2 0.7 all-gather.8.cloned.1.call-update
  8.1 0.7 all-gather.10.cloned.1.call-update
  8.8 0.7 all-gather.12.cloned.1.call-update
  12.0 6.2 all-gather.1
  18.5 0.3 fusion.25
  18.9 39.8 %all-gather.8.cloned.1.call-done = bf16[1024,3072]{1,0:T(8,128)(2,1)} async-done(((bf16[256,3072]{1,0:T(8,128)(2,1)}), bf16[1024,3072]{1,0:T(8,128)(2,1)}) %all-gather.8.cloned.1.call-update) | async-done | bytes 6291472 | tf_op jit(solution)/shard_map/all_gather | solution.py:297
  58.7 4.9 fusion.51
  63.6 1.0 slice.260
  64.6 0.4 fusion.31
  65.0 0.4 copy.68
  65.4 1.5 copy.67
  66.9 1.2 copy.66
  68.1 2.9 pad_maximum_fusion.1
  71.0 5.6 all-to-all-start
  76.6 0.5 all-gather.14.cloned.1.call-update
  77.3 109.7 %all-gather.2 = s32[32,1,384]{2,1,0:T(1,128)S(1)} all-gather(s32[1,1,384]{2,1,0:T(1,128)S(1)} %reshape.351), channel_id=1, replica_groups=mesh['fsdp'=4,'rep'=8] {'fsdp','rep'}, dimensions={0}, use_global_device_ids=true | all-gather | bytes 50688 | tf_op jit(solution)/shard_map/all_gather | solution.py:294
  187.7 0.6 reshape.326.meta
  188.4 3.0 copy.61
  191.5 1.3 collective-permute-start.1
  192.8 3.5 collective-permute-start
  196.3 2.2 fusion.38
  198.6 1.3 pad_maximum_fusion.3.q_ref
  199.9 7.8 maximum_maximum_fusion
  207.8 3.8 fusion.26
  211.6 1.9 pad_maximum_fusion.k_ref
  213.5 40.4 %attend.1 = (bf16[3072,128]{1,0:T(8,128)(2,1)}, f32[128,3072]{1,0:T(8,128)}, f32[8,3072]{1,0:T(8,128)}) custom-call(s32[24]{0:T(128)} %reshape.326.meta, bf16[2,3072,128]{2,1,0:T(8,128)(2,1)} %pad_maximum_fusion.3.q_ref, bf16[2,6144,128]{2,1,0:T(8,128)(2,1)} %pad_maximum_fusion.k_ref, bf16[6144,128]{1,0:T(8,128)(2,1)} %get-tuple-element.62.v_ref), custom_call_target="tpu_custom_call" | custom-call | flops 4309647360 | bytes 9437184 | tf_op jit(solution)/shard_map/attend/pallas_call | solution.py:130
  254.0 2.3 copy.62
  256.3 3.5 all-to-all-start.1
  260.0 13.0 %all-to-all-done.1 = bf16[8,384,128]{1,2,0:T(8,128)(2,1)S(1)} async-done(((bf16[8,384,128]{1,2,0:T(8,128)(2,1)}), bf16[8,384,128]{1,2,0:T(8,128)(2,1)S(1)}, u32[]{:S(2)}, u32[]{:S(2)}) %all-to-all-start.1) | async-done | bytes 786464 | tf_op jit(solution)/shard_map/all_to_all | solution.py:342
  273.0 3.8 fusion.53
  277.1 9.0 %multiply_convert_fusion = (bf16[384,4096]{1,0:T(8,128)(2,1)}, f32[384,4096]{1,0:T(8,128)}) fusion(f32[4096]{0:T(1024)S(1)} %bitcast.149, bf16[1024,4096]{1,0:T(8,128)(2,1)} %all-gather.12.cloned.1.call-done, f32[384,1024]{1,0:T(8,128)S(1)} %get-tuple-element.53, f32[1024]{0:T(1024)S(1)} %bitcast.164, f32[1024]{0:T(1024)S(1)} %bitcast.159, ...), kind=kOutput, calls=%fused_computation.8 | convolution fusion | flops 3232628736 | bytes 19426304 | tf_op jit(solution)/shard_map/dot_general | solution.py:50
  286.1 9.7 %fusion.58 = (f32[4096]{0:T(1024)S(1)}, bf16[384,4096]{1,0:T(8,128)(2,1)}) fusion(f32[384,4096]{1,0:T(8,128)} %get-tuple-element.95, bf16[4096,1024]{1,0:T(8,128)(2,1)} %all-gather.14.cloned.1.call-done, bf16[384,1024]{1,0:T(8,128)(2,1)} %param.20, f32[1024]{0:T(1024)S(1)} %bitcast.156), kind=kOutput, calls=%fused_computation.161 | convolution fusion | flops 3239702528 | bytes 18632704 | tf_op jit(solution)/shard_map/te,de->td/dot_general | solution.py:54
  295.9 6.9 multiply_reduce_fusion
  302.9 7.9 fusion.28
  310.8 2.6 convolution_convert_fusion.3
  313.7 10.3 %convolution_convert_fusion.1 = bf16[1024,4096]{1,0:T(8,128)(2,1)} fusion(bf16[384,4096]{1,0:T(8,128)(2,1)} %get-tuple-element.99, f32[384,1024]{1,0:T(8,128)} %copy-done.3, f32[1024]{0:T(1024)S(1)} %bitcast.165, f32[1024]{0:T(1024)S(1)} %bitcast.162, f32[384]{0:T(512)S(1)} %add_rsqrt_fusion, f32[384]{0:T(512)S(1)} %broadcast_multiply_fusion.4), kind=kOutput, calls=%fused_computation.2 | convolution fusion | flops 3227385856 | bytes 13118464 | tf_op jit(solution)/shard_map/td,te->de/dot_general | solution.py:58
  324.1 1.1 copy-done.26
  325.1 8.7 %convolution_convert_fusion = bf16[4096,1024]{1,0:T(8,128)(2,1)} fusion(bf16[384,4096]{1,0:T(8,128)(2,1)} %get-tuple-element.94, bf16[384,1024]{1,0:T(8,128)(2,1)S(1)} %copy-done.26, f32[1024]{0:T(1024)S(1)} %bitcast.158), kind=kOutput, calls=%fused_computation.1 | convolution fusion | flops 3226599424 | bytes 12324864 | tf_op jit(solution)/shard_map/td,te->de/dot_general | solution.py:58
  333.9 2.7 fusion.35
  336.7 16.7 %all_to_all.20 = bf16[8,384,128]{2,1,0:T(8,128)(2,1)} all-to-all(bf16[8,384,128]{2,1,0:T(8,128)(2,1)S(1)} %bitcast.136), channel_id=1, replica_groups={{0,1,2,3,4,5,6,7},{8,9,10,11,12,13,14,15},{16,17,18,19,20,21,22,23},{24..., dimensions={0} | all-to-all | bytes 1572864 | tf_op jit(solution)/shard_map/all_to_all | solution.py:342
  353.5 65.2 %attend_back.1 = (bf16[3072,128]{1,0:T(8,128)(2,1)}, f32[6144,128]{1,0:T(8,128)}, f32[6144,128]{1,0:T(8,128)}) custom-call(s32[24]{0:T(128)} %reshape.326.meta, bf16[2,3072,128]{2,1,0:T(8,128)(2,1)} %pad_maximum_fusion.3.q_ref, bf16[2,6144,128]{2,1,0:T(8,128)(2,1)} %pad_maximum_fusion.k_ref, bf16[6144,128]{1,0:T(8,128)(2,1)} %get-tuple-element.62.v_ref, ...), custom_call_target="tpu_custom_call" | custom-call | flops 10774118400 | bytes 16777216 | tf_op jit(solution)/shard_map/attend_back/pallas_call | solution.py:212
  418.7 2.4 constant_dynamic-update-slice_fusion.1
  421.1 0.6 copy-done.4
  422.3 1.3 collective-permute-start.3
  423.6 28.6 %collective-permute-start.2 = (bf16[1408,256]{1,0:T(8,128)(2,1)S(1)}, bf16[1408,256]{1,0:T(8,128)(2,1)S(1)}, u32[]{:S(2)}, u32[]{:S(2)}) collective-permute-start(bf16[1408,256]{1,0:T(8,128)(2,1)S(1)} %get-tuple-element.60), channel_id=1, source_target_pairs={{0,8},{1,9},{2,10},{3,11},{4,12},{5,13},{6,14},{7,15},{8,16},{9,17... | collective-permute-start | bytes 2162696 | tf_op jit(solution)/shard_map/ppermute | solution.py:31
  452.2 1.7 collective-permute-done.2
  454.0 0.5 fusion.6
  454.7 50.8 %all_to_all.21 = bf16[8,384,384]{2,1,0:T(8,128)(2,1)S(1)} all-to-all(bf16[8,384,384]{2,1,0:T(8,128)(2,1)S(1)} %bitcast.126), channel_id=1, replica_groups={{0,1,2,3,4,5,6,7},{8,9,10,11,12,13,14,15},{16,17,18,19,20,21,22,23},{24..., dimensions={0} | all-to-all | bytes 4718592 | tf_op jit(solution)/shard_map/all_to_all | solution.py:342
  505.6 1.4 copy.86
  507.0 2.9 copy.65
  509.8 7.4 convolution_convert_fusion.2
  517.4 64.6 %reduce-scatter.5.cloned.1.call-done = bf16[256,3072]{1,0:T(8,128)(2,1)} async-done(((bf16[1024,3072]{1,0:T(8,128)(2,1)}), bf16[256,3072]{1,0:T(8,128)(2,1)}) %reduce-scatter.5.cloned.1.call-update) | async-done | bytes 1572880 | tf_op jit(solution)/shard_map/reduce_scatter | solution.py:448
  582.1 1.6 copy-done.1
  583.7 6.9 fusion.24
  590.6 0.3 convert_reduce_fusion.1
  591.1 43.6 %psum.35 = f32[4,3584]{1,0:T(4,128)S(1)} all-reduce(f32[4,3584]{1,0:T(4,128)S(1)} %constant_dynamic-update-slice_fusion.2), channel_id=1, replica_groups=mesh['fsdp'=4,'rep'=8] {'fsdp','rep'}, use_global_device_ids=true, to_apply=%region_23.24 | all-reduce | flops 14336 | bytes 114688 | tf_op jit(solution)/shard_map/psum | solution.py:438
  634.7 0.7 dynamic-slice.8
  635.3 0.7 fusion.57
  636.0 3.4 fusion.23
  639.4 158.5 %all-reduce.5.cloned.1.call-done = (bf16[256,3072]{1,0:T(8,128)(2,1)}, bf16[256,1024]{1,0:T(8,128)(2,1)}, bf16[256,4096]{1,0:T(8,128)(2,1)}, bf16[1024,1024]{1,0:T(8,128)(2,1)}) async-done(((bf16[256,3072]{1,0:T(8,128)(2,1)}, bf16[256,1024]{1,0:T(8,128)(2,1)}, bf16[256,4096]{1,0:T(8,128)(2,1)}, bf16[1024,1024]{1,0:T(8,128)(2,1)}), (bf16[256,3072]{1,0:T(8,128)(2,1)}, bf16[256,1024]{1,0:T(8,128)(2,1)}, ...) | async-done | bytes 6291472 | tf_op jit(solution)/shard_map/psum | solution.py:449
  797.9 3.6 convert_element_type.106
  801.5 1.1 convert_element_type.108
  802.6 2.5 convert_element_type.110
  805.1 2.5 convert_element_type.112
  (160 shorter events, 6.2 us)
Async XLA Ops:
  7.2 51.5 %all-gather.8.cloned.1.call-start = ((), (), s32[]{:S(2)}) async-start(), calls=%async_computation.8 | async-start | bytes 7864320 | tf_op jit(solution)/shard_map/all_gather | solution.py:297
  7.9 1.6 copy-start.13
  7.9 1.9 copy-start.14
  7.9 2.1 copy-start.15
  8.0 2.3 copy-start.16
  8.0 2.5 copy-start.17
  8.0 2.7 copy-start.18
  8.0 2.9 copy-start.19
  8.0 3.1 copy-start.20
  8.0 3.3 copy-start.21
  8.0 3.5 copy-start.22
  8.0 3.8 copy-start.12
  8.0 10.3 %copy-start = (bf16[384,1024]{1,0:T(8,128)(2,1)S(1)}, bf16[384,1024]{1,0:T(8,128)(2,1)}, u32[]{:S(2)}) copy-start(bf16[384,1024]{1,0:T(8,128)(2,1)} %param.19) | copy-start | bytes 2359300
  8.0 251.9 %all-gather.10.cloned.1.call-start = ((), (), s32[]{:S(2)}) async-start(), calls=%async_computation.9 | async-start | bytes 2621440 | tf_op jit(solution)/shard_map/all_gather | solution.py:298
  8.8 268.3 %all-gather.12.cloned.1.call-start = ((), (), s32[]{:S(2)}) async-start(), calls=%async_computation.10 | async-start | bytes 10485760 | tf_op jit(solution)/shard_map/all_gather | solution.py:299
  71.0 117.4 %all-to-all-start = ((bf16[8,384,384]{1,2,0:T(8,128)(2,1)}), bf16[8,384,384]{1,2,0:T(8,128)(2,1)}, u32[]{:S(2)}, u32[]{:S(2)}) async-start(bf16[8,384,384]{1,2,0:T(8,128)(2,1)} %bitcast.8), calls=%async_computation | async-start | bytes 4718592 | tf_op jit(solution)/shard_map/all_to_all | solution.py:342
  76.6 0.7 copy-start.10
  76.6 0.7 copy-start.11
  76.6 209.6 %all-gather.14.cloned.1.call-start = ((), (), s32[]{:S(2)}) async-start(), calls=%async_computation.11 | async-start | bytes 10485760 | tf_op jit(solution)/shard_map/all_gather | solution.py:300
  191.5 8.4 %collective-permute-start.1 = (bf16[1408,256]{1,0:T(8,128)(2,1)S(1)}, bf16[1408,256]{1,0:T(8,128)(2,1)S(1)}, u32[]{:S(2)}, u32[]{:S(2)}) collective-permute-start(bf16[1408,256]{1,0:T(8,128)(2,1)S(1)} %get-tuple-element.66), channel_id=1, source_target_pairs={{8,0},{9,1},{10,2},{11,3},{12,4},{13,5},{14,6},{15,7},{16,8},{17,9... | collective-permute-start | bytes 2162696 | tf_op jit(solution)/shard_map/ppermute | solution.py:31
  192.8 7.1 collective-permute-start
  256.3 16.7 %all-to-all-start.1 = ((bf16[8,384,128]{1,2,0:T(8,128)(2,1)}), bf16[8,384,128]{1,2,0:T(8,128)(2,1)S(1)}, u32[]{:S(2)}, u32[]{:S(2)}) async-start(bf16[8,384,128]{1,2,0:T(8,128)(2,1)} %copy.62), calls=%async_computation.1 | async-start | bytes 1572864 | tf_op jit(solution)/shard_map/all_to_all | solution.py:342
  259.8 257.5 %reduce-scatter.7.cloned.1.call-start = ((), (), s32[]{:S(2)}) async-start(), calls=%async_computation.13 | async-start | bytes 2621440 | tf_op jit(solution)/shard_map/reduce_scatter | solution.py:448
  276.8 19.1 %copy-start.3 = (f32[384,1024]{1,0:T(8,128)}, f32[384,1024]{1,0:T(8,128)S(1)}, u32[]{:S(2)}) copy-start(f32[384,1024]{1,0:T(8,128)S(1)} %get-tuple-element.53) | copy-start | bytes 4718596
  286.1 9.7 %copy-start.23 = (bf16[1024,4096]{1,0:T(8,128)(2,1)S(1)}, bf16[1024,4096]{1,0:T(8,128)(2,1)}, u32[]{:S(2)}) copy-start(bf16[1024,4096]{1,0:T(8,128)(2,1)} %all-gather.12.cloned.1.call-done) | copy-start | bytes 25165828
  295.9 7.0 copy-start.7
  295.9 6.9 copy-start.24
  295.9 6.9 copy-start.25
  310.8 23.1 %copy-start.2 = (f32[384,1024]{1,0:T(8,128)}, f32[384,1024]{1,0:T(8,128)S(1)}, u32[]{:S(2)}) copy-start(f32[384,1024]{1,0:T(8,128)S(1)} %get-tuple-element.70) | copy-start | bytes 4718596
  313.4 203.9 %reduce-scatter.9.cloned.1.call-start = ((), (), s32[]{:S(2)}) async-start(), calls=%async_computation.14 | async-start | bytes 10485760 | tf_op jit(solution)/shard_map/reduce_scatter | solution.py:448
  324.0 1.1 copy-start.26
  324.0 193.4 %reduce-scatter.11.cloned.1.call-start = ((), (), s32[]{:S(2)}) async-start(), calls=%async_computation.15 | async-start | bytes 10485760 | tf_op jit(solution)/shard_map/reduce_scatter | solution.py:448
  333.8 248.2 %reduce-scatter.5.cloned.1.call-start = ((), (), s32[]{:S(2)}) async-start(), calls=%async_computation.12 | async-start | bytes 7864320 | tf_op jit(solution)/shard_map/reduce_scatter | solution.py:448
  418.7 2.9 copy-start.4
  422.3 29.9 %collective-permute-start.3 = (bf16[1408,256]{1,0:T(8,128)(2,1)S(1)}, bf16[1408,256]{1,0:T(8,128)(2,1)S(1)}, u32[]{:S(2)}, u32[]{:S(2)}) collective-permute-start(bf16[1408,256]{1,0:T(8,128)(2,1)S(1)} %get-tuple-element.61), channel_id=1, source_target_pairs={{8,0},{9,1},{10,2},{11,3},{12,4},{13,5},{14,6},{15,7},{16,8},{17,9... | collective-permute-start | bytes 2162696 | tf_op jit(solution)/shard_map/ppermute | solution.py:31
  423.6 30.8 %copy-start.8 = (bf16[3072,128]{1,0:T(8,128)(2,1)S(1)}, bf16[3072,128]{1,0:T(8,128)(2,1)}, u32[]{:S(2)}) copy-start(bf16[3072,128]{1,0:T(8,128)(2,1)} %get-tuple-element.26) | copy-start | bytes 2359300
  423.6 30.3 %collective-permute-start.2 = (bf16[1408,256]{1,0:T(8,128)(2,1)S(1)}, bf16[1408,256]{1,0:T(8,128)(2,1)S(1)}, u32[]{:S(2)}, u32[]{:S(2)}) collective-permute-start(bf16[1408,256]{1,0:T(8,128)(2,1)S(1)} %get-tuple-element.60), channel_id=1, source_target_pairs={{0,8},{1,9},{2,10},{3,11},{4,12},{5,13},{6,14},{7,15},{8,16},{9,17... | collective-permute-start | bytes 2162696 | tf_op jit(solution)/shard_map/ppermute | solution.py:31
  517.3 280.7 %all-reduce.5.cloned.1.call-start = ((), (), s32[]{:S(2)}) async-start(), calls=%async_computation.16 | async-start | bytes 12582912 | tf_op jit(solution)/shard_map/psum | solution.py:449
  582.0 1.7 copy-start.1
  797.9 3.6 copy-start.9
  797.9 4.7 copy-start.6
  802.6 2.5 copy-start.5
Sparse Core Ops, SparseCore 0:
  9.6 49.0 all-gather.7
  60.2 22.5 all-gather.9
  84.4 58.2 all-gather.11
  144.1 60.9 all-gather.13
  313.5 43.0 reduce-scatter.6
  359.1 71.4 reduce-scatter.8
  433.2 74.2 reduce-scatter.10
  517.4 64.5 reduce-scatter.4
  586.4 211.4 all-reduce.4

commit v2 on v1

--- a/solution.py
+++ b/solution.py
@@ -224,6 +224,297 @@
         ),
         name="attend_back",
     )(meta, q_aug, k_aug, values, grad, out_t, lse)
+
+
+CHUNK = 64
+LAG = 2
+MESH = pl.DeviceIdType.MESH
+STAGES = 6
+
+
+def reduce_kernel(
+    down_ref,
+    up_ref,
+    out_ref,
+    qkv_ref,
+    small_ref,
+    final,
+    small_final,
+    own,
+    from_core,
+    from_x,
+    from_y,
+    from_z,
+    small_own,
+    small_core,
+    small_x,
+    small_all,
+    load_sem,
+    core_sem,
+    x_sem,
+    y_sem,
+    z_sem,
+    zz_sem,
+    yy_sem,
+    small_sem,
+):
+    f = lax.axis_index("fsdp")
+    r = lax.axis_index("rep")
+    x, c = f // 2, f % 2
+    z, y = (r % GROUP) // 2, r % 2
+    base = r - r % GROUP
+    core_peer = (x * 2 + 1 - c, r)
+    x_peer = ((1 - x) * 2 + c, r)
+    y_peer = (f, base + z * 2 + 1 - y)
+    z_spots = [(z + step) % 4 for step in range(1, 4)]
+    z_peers = [(f, base + spot * 2 + y) for spot in z_spots]
+    plane = [(f, base + (r % GROUP + step) % GROUP) for step in range(1, GROUP)]
+    total = final.shape[0]
+
+    barrier = pltpu.get_barrier_semaphore()
+    for peer in [core_peer, x_peer] + plane:
+        pl.semaphore_signal(barrier, inc=1, device_id=peer, device_id_type=MESH)
+    pl.semaphore_wait(barrier, 2 + len(plane))
+
+    def remote(source, target, send, recv, peer):
+        return pltpu.make_async_remote_copy(
+            src_ref=source,
+            dst_ref=target,
+            send_sem=send,
+            recv_sem=recv,
+            device_id=peer,
+            device_id_type=MESH,
+        )
+
+    refs = (down_ref, up_ref, out_ref, qkv_ref)
+    spans = []
+    first = 0
+    for ref in refs:
+        height = ref.shape[0] // 4 // CHUNK
+        amount = height * (ref.shape[1] // D)
+        spans.append((ref, first, first + amount, height))
+        first += amount
+
+    def piece(ref, low, height, k, owner):
+        at = k - low
+        top = owner * (height * CHUNK) + (at % height) * CHUNK
+        left = (at // height) * D
+        return ref.at[pl.ds(pl.multiple_of(top, CHUNK), CHUNK), pl.ds(pl.multiple_of(left, D), D)]
+
+    def enter_copies(ref, low, height, k):
+        copies = []
+        for side in range(2):
+            copies.append(
+                remote(
+                    piece(ref, low, height, k, side * 2 + 1 - c),
+                    from_core.at[k, side],
+                    core_sem.at[0, k, side],
+                    core_sem.at[1, k, side],
+                    core_peer,
+                )
+            )
+            copies.append(
+                pltpu.make_async_copy(
+                    piece(ref, low, height, k, side * 2 + c), own.at[k, side], load_sem.at[k, side]
+                )
+            )
+        return copies
+
+    def enter(k):
+        for ref, low, high, height in spans:
+
+            @pl.when((k >= low) & (k < high))
+            def _():
+                for copy in enter_copies(ref, low, height, k):
+                    copy.start()
+
+    x_copy = lambda k: remote(
+        own.at[k, 1 - x], from_x.at[k], x_sem.at[0, k], x_sem.at[1, k], x_peer
+    )
+    half = CHUNK // 2
+    quarter = D // 4
+
+    def y_copy(k):
+        rows = pl.ds(pl.multiple_of((1 - y) * half, half), half)
+        return remote(
+            own.at[k, x, rows], from_y.at[k], y_sem.at[0, k], y_sem.at[1, k], y_peer
+        )
+
+    my_rows = pl.ds(pl.multiple_of(y * half, half), half)
+    my_lanes = pl.ds(pl.multiple_of(z * quarter, quarter), quarter)
+
+    def z_copies(k):
+        copies = []
+        for step in range(3):
+            lanes = pl.ds(pl.multiple_of(z_spots[step] * quarter, quarter), quarter)
+            copies.append(
+                remote(
+                    own.at[k, x, my_rows, lanes],
+                    from_z.at[k, step],
+                    z_sem.at[0, k, step],
+                    z_sem.at[1, k, step],
+                    z_peers[step],
+                )
+            )
+        return copies
+
+    def zz_copies(k):
+        here = final.at[k, my_rows, my_lanes]
+        return [
+            remote(here, here, zz_sem.at[0, k, step], zz_sem.at[1, k, step], z_peers[step])
+            for step in range(3)
+        ]
+
+    def yy_copy(k):
+        here = final.at[k, my_rows]
+        return remote(here, here, yy_sem.at[0, k], yy_sem.at[1, k], y_peer)
+
+    def core_sum(k):
+        for side in range(2):
+            target = own.at[k, side]
+            pltpu.make_async_copy(target, target, load_sem.at[k, side]).wait()
+            remote(
+                target,
+                from_core.at[k, side],
+                core_sem.at[0, k, side],
+                core_sem.at[1, k, side],
+                core_peer,
+            ).wait()
+        for side in range(2):
+            own[k, side] = (
+                own[k, side].astype(jnp.float32) + from_core[k, side].astype(jnp.float32)
+            ).astype(jnp.bfloat16)
+        x_copy(k).start()
+
+    def x_sum(k):
+        x_copy(k).wait()
+        own[k, x] = (own[k, x].astype(jnp.float32) + from_x[k].astype(jnp.float32)).astype(
+            jnp.bfloat16
+        )
+        y_copy(k).start()
+
+    def y_sum(k):
+        y_copy(k).wait()
+        own[k, x, my_rows] = (
+            own[k, x, my_rows].astype(jnp.float32) + from_y[k].astype(jnp.float32)
+        ).astype(jnp.bfloat16)
+        for copy in z_copies(k):
+            copy.start()
+
+    def z_sum(k):
+        for copy in z_copies(k):
+            copy.wait()
+        value = own[k, x, my_rows, my_lanes].astype(jnp.float32)
+        for step in range(3):
+            value = value + from_z[k, step].astype(jnp.float32)
+        final[k, my_rows, my_lanes] = value.astype(jnp.bfloat16)
+        for copy in zz_copies(k):
+            copy.start()
+
+    def z_join(k):
+        for copy in zz_copies(k):
+            copy.wait()
+        yy_copy(k).start()
+
+    def small_enter(side):
+        return remote(
+            small_ref.at[side * 2 + 1 - c],
+            small_core.at[side],
+            small_sem.at[0, side],
+            small_sem.at[1, side],
+            core_peer,
+        )
+
+    small_cross = remote(
+        small_own.at[1 - x], small_x, small_sem.at[0, 2], small_sem.at[1, 2], x_peer
+    )
+
+    def small_spread(step):
+        return remote(
+            small_own.at[2],
+            small_all.at[step - 1],
+            small_sem.at[0, 2 + step],
+            small_sem.at[1, 2 + step],
+            plane[step - 1],
+        )
+
+    for side in range(2):
+        small_enter(side).start()
+
+    steps = (enter, core_sum, x_sum, y_sum, z_sum, z_join, lambda k: yy_copy(k).wait())
+
+    @pl.loop(0, total + LAG * (len(steps) - 1))
+    def _(now):
+        @pl.when(now == 4)
+        def _():
+            for side in range(2):
+                small_enter(side).wait()
+            for side in range(2):
+                small_own[side] = small_ref[side * 2 + c] + small_core[side]
+            small_cross.start()
+
+        @pl.when(now == 8)
+        def _():
+            small_cross.wait()
+            small_own[2] = small_own[x] + small_x[...]
+            for step in range(1, GROUP):
+                small_spread(step).start()
+
+        for order, step in enumerate(steps):
+            k = now - order * LAG
+
+            @pl.when((k >= 0) & (k < total))
+            def _():
+                step(k)
+
+    for step in range(1, GROUP):
+        small_spread(step).wait()
+    value = small_own[2]
+    for step in range(1, GROUP):
+        value = value + small_all[step - 1]
+    small_final[...] = value
+
+
+def reduce_grads(weights, small):
+    chunks = sum(weight.size for weight in weights) // (4 * CHUNK * D)
+    tall = small.shape[1]
+    anywhere = pl.BlockSpec(memory_space=pl.ANY)
+    vmem = pl.BlockSpec(memory_space=pltpu.VMEM)
+    dma = pltpu.SemaphoreType.DMA
+    low = jnp.bfloat16
+    return pl.pallas_call(
+        reduce_kernel,
+        out_shape=(
+            jax.ShapeDtypeStruct((chunks, CHUNK, D), low),
+            jax.ShapeDtypeStruct((tall, 128), jnp.float32),
+        ),
+        in_specs=[anywhere] * 4 + [vmem],
+        out_specs=(vmem, vmem),
+        scratch_shapes=[
+            pltpu.VMEM((chunks, 2, CHUNK, D), low),
+            pltpu.VMEM((chunks, 2, CHUNK, D), low),
+            pltpu.VMEM((chunks, CHUNK, D), low),
+            pltpu.VMEM((chunks, CHUNK // 2, D), low),
+            pltpu.VMEM((chunks, 3, CHUNK // 2, D // 4), low),
+            pltpu.VMEM((3, tall, 128), jnp.float32),
+            pltpu.VMEM((2, tall, 128), jnp.float32),
+            pltpu.VMEM((tall, 128), jnp.float32),
+            pltpu.VMEM((GROUP - 1, tall, 128), jnp.float32),
+            dma((chunks, 2)),
+            dma((2, chunks, 2)),
+            dma((2, chunks)),
+            dma((2, chunks)),
+            dma((2, chunks, 3)),
+            dma((2, chunks, 3)),
+            dma((2, chunks)),
+            dma((2, GROUP + 2)),
+        ],
+        compiler_params=pltpu.CompilerParams(
+            collective_id=1, has_side_effects=True, vmem_limit_bytes=60 << 20
+        ),
+        cost_estimate=pl.CostEstimate(flops=0, transcendentals=0, bytes_accessed=200 << 20),
+        name="reduce_grads",
+    )(*weights, small)
 
 
 def shards(
@@ -250,7 +541,6 @@
     both = ("fsdp", "rep")
     owners = lax.axis_size("fsdp")
     replicas = lax.axis_size("rep")
-    me = lax.axis_index("fsdp") * replicas + lax.axis_index("rep")
     tok_rows = tokens.shape[0]
     rows = GROUP * tok_rows
     groups = [list(range(g, g + GROUP)) for g in range(0, replicas, GROUP)]
@@ -291,21 +581,22 @@
         hidden_bias,
     ) = parts
 
-    codes = lax.all_gather(
-        jnp.where(pad_mask > 0, image_ids + 1, 0), both, axis=0, tiled=True
-    )
+    codes = jnp.where(pad_mask > 0, image_ids + 1, 0)
+    codes = lax.all_gather(codes, "rep", axis=0, tiled=True, axis_index_groups=groups)
+    codes = [
+        from_behind(codes[rows - HALO :], both, GROUP),
+        codes,
+        from_behind(codes[:HALO], both, -GROUP),
+        jnp.zeros((BLOCK,), jnp.int32),
+    ]
     wide_qkv = lax.all_gather(w_qkv, "fsdp", axis=0, tiled=True)
     wide_out = lax.all_gather(w_out, "fsdp", axis=0, tiled=True)
     wide_up = lax.all_gather(w_up, "fsdp", axis=0, tiled=True)
     wide_down = lax.all_gather(w_down, "fsdp", axis=0, tiled=True)
 
     window = HALO + rows + HALO + BLOCK
-    padded = jnp.concatenate(
-        [jnp.zeros((HALO,), jnp.int32), codes, jnp.zeros((HALO + BLOCK,), jnp.int32)]
-    )
-    seen = lax.dynamic_slice_in_dim(padded, (me // GROUP) * rows, window, 0)
+    seen = jnp.concatenate(codes)
     spot = jnp.arange(window, dtype=jnp.int32)
-    seen = jnp.where(spot < window - BLOCK, seen, 0)
     asked = seen[HALO : HALO + rows]
     tile_codes = asked.reshape(rows // BLOCK, BLOCK)
     first_code = jnp.min(jnp.where(tile_codes > 0, tile_codes, 1 << 30), axis=1)
@@ -435,8 +726,14 @@
         hidden_bias_grad,
     )
     packed = jnp.concatenate([member.reshape(owners, -1) for member in small_grads], axis=1)
-    packed = lax.psum(packed, both)
-    packed = lax.dynamic_slice_in_dim(packed, lax.axis_index("fsdp"), 1, 0)[0]
+    packed = packed.reshape(owners, -1, 128)
+    grads, packed = reduce_grads((down_grad, up_grad, out_weight_grad, qkv_weight_grad), packed)
+    grads = grads.astype(jnp.float32)
+    if replicas > GROUP:
+        apart = [list(range(low, replicas, GROUP)) for low in range(GROUP)]
+        grads = lax.psum(grads, "rep", axis_index_groups=apart)
+        packed = lax.psum(packed, "rep", axis_index_groups=apart)
+    packed = packed.reshape(-1)
     small_out = []
     place = 0
     for member in small_grads:
@@ -444,14 +741,16 @@
         small_out.append(packed[place : place + size])
         place += size
 
-    def reduced(partial):
-        owned = lax.psum_scatter(partial, "fsdp", scatter_dimension=0, tiled=True)
-        return lax.psum(owned, "rep").astype(jnp.float32)
-
-    down_out = reduced(down_grad)
-    up_out = reduced(up_grad)
-    out_out = reduced(out_weight_grad)
-    qkv_out = reduced(qkv_weight_grad)
+    def joined(start, height, width):
+        deep, across = height // CHUNK, width // D
+        part = grads[start : start + deep * across]
+        part = part.reshape(across, deep, CHUNK, D).transpose(1, 2, 0, 3)
+        return part.reshape(height, width), start + deep * across
+
+    down_out, place = joined(0, *w_down.shape)
+    up_out, place = joined(place, *w_up.shape)
+    out_out, place = joined(place, *w_out.shape)
+    qkv_out, place = joined(place, *w_qkv.shape)
     return (
         layer_out,
         tokens_grad,

time: 824 us -> 700 us (0.85)
  Pallas kernels: 106 us -> 289 us
  waiting for transfers between devices: 280 us -> 103 us
  blocking collectives: 227 us -> 94.9 us
  local copies, waits for them, and re-layouts: 24.7 us -> 49.9 us
  other arithmetic: 36.3 us -> 26.1 us
    pallas_call x0 -> x1, Pallas kernels: none -> 176 us  [reduce_grads(): pl.pallas_call(reduce_kernel, out_shape=(jax.ShapeDtypeStruct((chunks, CH...]
    psum x1 -> x0, waiting for transfers between devices: 159 us -> none  [reduced(): return lax.psum(owned, 'rep').astype(jnp.float32)]
    reduce_scatter x4 -> x0, waiting for transfers between devices: 64.7 us -> none  [reduced(): owned = lax.psum_scatter(partial, 'fsdp', scatter_dimension=0, tiled=True)]
    all_to_all x2 -> x1, blocking collectives: 67.6 us -> 16.6 us  [exchange(): lax.all_to_all(block, 'rep', split_axis=0, concat_axis=0, tiled=True, axi...]
    psum x1 -> x0, blocking collectives: 43.6 us -> none  [shards(): packed = lax.psum(packed, both)]
    all_gather x1, blocking collectives: 110 us -> 72.1 us  [shards(): lax.all_gather(codes, 'rep', axis=0, tiled=True, axis_index_groups=groups)]
    all_to_all x2 -> x3, waiting for transfers between devices: 13 us -> 45.9 us  [exchange(): lax.all_to_all(block, 'rep', split_axis=0, concat_axis=0, tiled=True, axi...]
    ppermute x4 -> x6, waiting for transfers between devices: 1.75 us -> 14.8 us  [from_behind(): return lax.ppermute(block, axis, route)]
  transfers between devices with their start and end apart: 15 -> 13, of which waited for: 5 -> 6; matrix products, arithmetic and copies ran while one was open for 12% -> 10% of each run, Pallas kernels for 13% -> 6%
where the time goes in v2:
time: 700 us; the launch traced here: 697 us
  Pallas kernels  289 us (41%)
  waiting for transfers between devices  103 us (15%)
  blocking collectives  94.9 us (14%)
  matrix products  73.3 us (10%)
  local copies, waits for them, and re-layouts  49.9 us (7%)
  starting transfers between devices  45 us (6%)
  other arithmetic  26.1 us (4%)
  between operations  15 us (2%)
    pallas_call x1, Pallas kernels, reduce_grads(): pl.pallas_call(reduce_kernel, out_shape=(jax.ShapeDtypeStruct((chunks, CH...  176 us
    all_gather x1, blocking collectives, shards(): lax.all_gather(codes, 'rep', axis=0, tiled=True, axis_index_groups=groups)  72.1 us
    pallas_call x1, Pallas kernels, attend_back(): pl.pallas_call(attend_back_kernel, out_shape=(jax.ShapeDtypeStruct((rows,...  69.7 us
    all_to_all x3, waiting for transfers between devices, exchange(): lax.all_to_all(block, 'rep', split_axis=0, concat_axis=0, tiled=True, axi...  45.9 us
    pallas_call x1, Pallas kernels, attend(): pl.pallas_call(attend_kernel, out_shape=(jax.ShapeDtypeStruct((rows, PAIR...  43.2 us
    all_gather x1, waiting for transfers between devices, shards(): wide_qkv = lax.all_gather(w_qkv, 'fsdp', axis=0, tiled=True)  39.8 us
    ppermute x6, starting transfers between devices, from_behind(): return lax.ppermute(block, axis, route)  31.9 us
    dot_general x4, matrix products, matmul(): return jnp.dot(left, right, preferred_element_type=jnp.float32)  25.1 us
  transfers between devices with their start and end apart: 13, of which 6 were waited for; matrix products, arithmetic and copies ran while one was open for 10% of the time, Pallas kernels for 6%

profile of v2, /device:TPU:0, one launch (start us, length us, event | category | flops | bytes accessed | tf_op | source)
XLA Modules:
  0.0 696.6 jit_solution(9026082874502226817)
XLA Ops:
  7.2 0.7 all-gather.8.cloned.1.call-update
  8.1 0.7 all-gather.10.cloned.1.call-update
  8.8 0.7 all-gather.12.cloned.1.call-update
  12.0 6.2 all-gather.1
  18.9 39.8 %all-gather.8.cloned.1.call-done = bf16[1024,3072]{1,0:T(8,128)(2,1)} async-done(((bf16[256,3072]{1,0:T(8,128)(2,1)}), bf16[1024,3072]{1,0:T(8,128)(2,1)}) %all-gather.8.cloned.1.call-update) | async-done | bytes 6291472 | tf_op jit(solution)/shard_map/all_gather | solution.py:592
  58.7 4.9 fusion.48
  63.6 1.0 slice.296
  65.4 1.5 copy.75
  66.9 1.2 copy.76
  68.1 2.9 pad_maximum_fusion.1
  71.0 5.6 all-to-all-start
  77.3 72.1 %all-gather.2 = s32[8,1,384]{2,1,0:T(1,128)S(1)} all-gather(s32[1,1,384]{2,1,0:T(1,128)S(1)} %reshape.427), channel_id=1, replica_groups={{0,1,2,3,4,5,6,7},{8,9,10,11,12,13,14,15},{16,17,18,19,20,21,22,23},{24..., dimensions={0}, use_global_device_ids=true | all-gather | bytes 13824 | tf_op jit(solution)/shard_map/all_gather | solution.py:585
  149.3 1.3 collective-permute-start
  150.6 1.3 collective-permute-start.1
  152.2 2.2 collective-permute-done.1
  154.9 0.6 reshape.397.meta
  155.5 3.1 copy.67
  158.7 4.8 collective-permute-start.2
  163.5 1.5 collective-permute-start.3
  165.0 2.2 fusion.38
  167.3 1.3 pad_maximum_fusion.3.q_ref
  168.6 7.8 %maximum_maximum_fusion = bf16[6144,256]{1,0:T(8,128)(2,1)S(1)} fusion(bf16[1408,256]{1,0:T(8,128)(2,1)S(1)} %collective-permute-done.3, bf16[3072,256]{1,0:T(8,128)(2,1)S(1)} %slice.234, bf16[1408,256]{1,0:T(8,128)(2,1)S(1)} %collective-permute-done.2, bf16[6144]{0:T(1024)(128)(2,1)S(1)} %pad.11.clone), kind=kLoop, calls=%fused_computation.15 | loop fusion | flops 12582912 | bytes 6172672 | tf_op jit(solution)/shard_map/concatenate | solution.py:641
  176.4 3.8 fusion.26
  180.3 1.9 pad_maximum_fusion.k_ref
  182.2 43.2 %attend.1 = (bf16[3072,128]{1,0:T(8,128)(2,1)}, f32[128,3072]{1,0:T(8,128)}, f32[8,3072]{1,0:T(8,128)}) custom-call(s32[24]{0:T(128)} %reshape.397.meta, bf16[2,3072,128]{2,1,0:T(8,128)(2,1)} %pad_maximum_fusion.3.q_ref, bf16[2,6144,128]{2,1,0:T(8,128)(2,1)} %pad_maximum_fusion.k_ref, bf16[6144,128]{1,0:T(8,128)(2,1)} %get-tuple-element.64.v_ref), custom_call_target="tpu_custom_call" | custom-call | flops 4309647360 | bytes 9437184 | tf_op jit(solution)/shard_map/attend/pallas_call | solution.py:130
  225.4 2.3 copy.68
  227.7 3.5 all-to-all-start.1
  231.4 13.0 %all-to-all-done.1 = bf16[8,384,128]{1,2,0:T(8,128)(2,1)S(1)} async-done(((bf16[8,384,128]{1,2,0:T(8,128)(2,1)}), bf16[8,384,128]{1,2,0:T(8,128)(2,1)S(1)}, u32[]{:S(2)}, u32[]{:S(2)}) %all-to-all-start.1) | async-done | bytes 786464 | tf_op jit(solution)/shard_map/all_to_all | solution.py:633
  244.4 4.1 fusion.50
  248.9 9.1 %multiply_convert_fusion = (bf16[384,4096]{1,0:T(8,128)(2,1)}, f32[384,4096]{1,0:T(8,128)}) fusion(f32[4096]{0:T(1024)S(1)} %bitcast.182, bf16[1024,4096]{1,0:T(8,128)(2,1)} %all-gather.12.cloned.1.call-done, f32[384,1024]{1,0:T(8,128)S(1)} %get-tuple-element.53, f32[1024]{0:T(1024)S(1)} %bitcast.192, f32[1024]{0:T(1024)S(1)} %bitcast.194, ...), kind=kOutput, calls=%fused_computation.8 | convolution fusion | flops 3232628736 | bytes 19426304 | tf_op jit(solution)/shard_map/dot_general | solution.py:50
  258.0 10.0 %fusion.55 = (f32[4096]{0:T(1024)S(1)}, bf16[384,4096]{1,0:T(8,128)(2,1)}) fusion(f32[384,4096]{1,0:T(8,128)} %get-tuple-element.99, bf16[4096,1024]{1,0:T(8,128)(2,1)} %all-gather.14.cloned.1.call-done, bf16[384,1024]{1,0:T(8,128)(2,1)S(1)} %copy-done.27, f32[1024]{0:T(1024)S(1)} %bitcast.189), kind=kOutput, calls=%fused_computation.166 | convolution fusion | flops 3239702528 | bytes 18632704 | tf_op jit(solution)/shard_map/te,de->td/dot_general | solution.py:54
  268.0 5.9 multiply_reduce_fusion
  273.9 7.1 %fusion.28 = (f32[1024]{0:T(1024)S(1)}, f32[1024]{0:T(1024)S(1)}, bf16[384,1024]{1,0:T(8,128)(2,1)}, f32[1024]{0:T(1024)S(1)}, f32[1024]{0:T(1024)S(1)}, /*index=5*/f32[384,1024]{1,0:T(8,128)S(1)}) fusion(bf16[384,1024]{1,0:T(8,128)(2,1)S(1)} %copy-done.27, f32[1024]{0:T(1024)S(1)} %bitcast.198, f32[1024]{0:T(1024)S(1)} %bitcast.190, ...), kind=kOutput, calls=%fused_computation.49 | convolution fusion | flops 3229478912 | bytes 19437568 | tf_op jit(solution)/shard_map/dot_general | solution.py:50
  281.0 1.0 fusion.35
  282.3 16.6 %all_to_all.20 = bf16[8,384,128]{2,1,0:T(8,128)(2,1)} all-to-all(bf16[8,384,128]{2,1,0:T(8,128)(2,1)S(1)} %bitcast.167), channel_id=1, replica_groups={{0,1,2,3,4,5,6,7},{8,9,10,11,12,13,14,15},{16,17,18,19,20,21,22,23},{24..., dimensions={0} | all-to-all | bytes 1572864 | tf_op jit(solution)/shard_map/all_to_all | solution.py:633
  298.9 69.7 %attend_back.1 = (bf16[3072,128]{1,0:T(8,128)(2,1)}, f32[6144,128]{1,0:T(8,128)}, f32[6144,128]{1,0:T(8,128)}) custom-call(s32[24]{0:T(128)} %reshape.397.meta, bf16[2,3072,128]{2,1,0:T(8,128)(2,1)} %pad_maximum_fusion.3.q_ref, bf16[2,6144,128]{2,1,0:T(8,128)(2,1)} %pad_maximum_fusion.k_ref, bf16[6144,128]{1,0:T(8,128)(2,1)} %get-tuple-element.64.v_ref, ...), custom_call_target="tpu_custom_call" | custom-call | flops 10774118400 | bytes 16777216 | tf_op jit(solution)/shard_map/attend_back/pallas_call | solution.py:212
  368.6 2.3 constant_dynamic-update-slice_fusion.1
  370.9 0.5 copy-done.7
  372.1 21.6 %collective-permute-start.4 = (bf16[1408,256]{1,0:T(8,128)(2,1)S(1)}, bf16[1408,256]{1,0:T(8,128)(2,1)S(1)}, u32[]{:S(2)}, u32[]{:S(2)}) collective-permute-start(bf16[1408,256]{1,0:T(8,128)(2,1)S(1)} %get-tuple-element.62), channel_id=1, source_target_pairs={{0,8},{1,9},{2,10},{3,11},{4,12},{5,13},{6,14},{7,15},{8,16},{9,17... | collective-permute-start | bytes 2162696 | tf_op jit(solution)/shard_map/ppermute | solution.py:31
  393.7 1.4 collective-permute-start.5
  395.5 12.2 %collective-permute-done.5 = bf16[1408,256]{1,0:T(8,128)(2,1)S(1)} collective-permute-done((bf16[1408,256]{1,0:T(8,128)(2,1)S(1)}, bf16[1408,256]{1,0:T(8,128)(2,1)S(1)}, u32[]{:S(2)}, u32[]{:S(2)}) %collective-permute-start.5) | collective-permute-done | bytes 720928 | tf_op jit(solution)/shard_map/ppermute | solution.py:31
  408.2 1.7 pad_maximum_fusion.2
  409.9 3.8 all-to-all-start.3
  413.8 4.4 convolution_convert_fusion.3.out_ref
  418.2 6.9 convolution_convert_fusion.1.down_ref
  425.2 7.1 %convolution_convert_fusion.up_ref = bf16[1024,4096]{1,0:T(8,128)(2,1)} fusion(bf16[384,4096]{1,0:T(8,128)(2,1)S(1)} %copy-done.29, f32[384,1024]{1,0:T(8,128)S(1)} %copy-done.6, f32[1024]{0:T(1024)S(1)} %bitcast.193, f32[1024]{0:T(1024)S(1)} %bitcast.197, f32[384]{0:T(512)S(1)} %add_rsqrt_fusion, f32[384]{0:T(512)S(1)} %broadcast_multiply_fusion.4), kind=kOutput, calls=%fused_computation.1 | convolution fusion | flops 3227385856 | bytes 13118464 | tf_op jit(solution)/shard_map/td,te->de/dot_general | solution.py:58
  432.3 32.8 %all-to-all-done.3 = bf16[8,384,384]{2,1,0:T(8,128)(2,1)S(1)} async-done(((bf16[8,384,384]{2,1,0:T(8,128)(2,1)}), bf16[8,384,384]{2,1,0:T(8,128)(2,1)S(1)}, u32[]{:S(2)}, u32[]{:S(2)}) %all-to-all-start.3) | async-done | bytes 2359328 | tf_op jit(solution)/shard_map/all_to_all | solution.py:633
  465.1 2.8 copy.96
  467.9 3.2 copy.71
  471.5 5.9 convolution_convert_fusion.2.qkv_ref
  477.4 6.9 fusion.24
  484.4 0.7 reshape.418.small_ref
  485.1 176.4 %reduce_grads.1 = (bf16[48,64,1024]{2,1,0:T(8,128)(2,1)}, f32[28,128]{1,0:T(8,128)}) custom-call(bf16[4096,1024]{1,0:T(8,128)(2,1)} %convolution_convert_fusion.1.down_ref, bf16[1024,4096]{1,0:T(8,128)(2,1)} %convolution_convert_fusion.up_ref, bf16[1024,1024]{1,0:T(8,128)(2,1)} %convolution_convert_fusion.3.out_ref, ...), custom_call_target="tpu_custom_call" | custom-call | bytes 209715200 | tf_op jit(solution)/shard_map/reduce_grads/pallas_call | solution.py:485
  661.5 1.3 slice_bitcast_fusion.11
  662.8 1.4 slice_bitcast_fusion.12
  664.2 2.1 slice.250
  666.4 1.9 slice.249
  668.3 1.3 copy-done
  669.6 3.0 fusion.51
  672.6 2.2 copy.72
  674.8 4.5 copy.90
  679.3 2.9 copy.73
  682.3 5.9 copy.91
  688.1 1.5 fusion.23
  (162 shorter events, 8.2 us)
Async XLA Ops:
  7.2 51.5 %all-gather.8.cloned.1.call-start = ((), (), s32[]{:S(2)}) async-start(), calls=%async_computation.4 | async-start | bytes 7864320 | tf_op jit(solution)/shard_map/all_gather | solution.py:592
  7.9 1.6 copy-start.15
  7.9 1.9 copy-start.16
  7.9 2.1 copy-start.17
  8.0 2.3 copy-start.18
  8.0 2.5 copy-start.19
  8.0 2.7 copy-start.20
  8.0 2.9 copy-start.21
  8.0 3.1 copy-start.22
  8.0 3.3 copy-start.23
  8.0 3.5 copy-start.24
  8.0 3.8 copy-start.14
  8.0 10.3 %copy-start.1 = (bf16[384,1024]{1,0:T(8,128)(2,1)S(1)}, bf16[384,1024]{1,0:T(8,128)(2,1)}, u32[]{:S(2)}) copy-start(bf16[384,1024]{1,0:T(8,128)(2,1)} %param.19) | copy-start | bytes 2359300
  8.0 223.3 %all-gather.10.cloned.1.call-start = ((), (), s32[]{:S(2)}) async-start(), calls=%async_computation.5 | async-start | bytes 2621440 | tf_op jit(solution)/shard_map/all_gather | solution.py:593
  8.8 240.1 %all-gather.12.cloned.1.call-start = ((), (), s32[]{:S(2)}) async-start(), calls=%async_computation.6 | async-start | bytes 10485760 | tf_op jit(solution)/shard_map/all_gather | solution.py:594
  71.0 84.5 %all-to-all-start = ((bf16[8,384,384]{1,2,0:T(8,128)(2,1)}), bf16[8,384,384]{1,2,0:T(8,128)(2,1)}, u32[]{:S(2)}, u32[]{:S(2)}) async-start(bf16[8,384,384]{1,2,0:T(8,128)(2,1)} %bitcast.8), calls=%async_computation | async-start | bytes 4718592 | tf_op jit(solution)/shard_map/all_to_all | solution.py:633
  76.6 0.7 copy-start.12
  76.6 0.7 copy-start.13
  76.6 181.4 %all-gather.14.cloned.1.call-start = ((), (), s32[]{:S(2)}) async-start(), calls=%async_computation.7 | async-start | bytes 10485760 | tf_op jit(solution)/shard_map/all_gather | solution.py:595
  149.3 2.8 collective-permute-start
  150.6 3.8 collective-permute-start.1
  158.7 9.9 %collective-permute-start.2 = (bf16[1408,256]{1,0:T(8,128)(2,1)S(1)}, bf16[1408,256]{1,0:T(8,128)(2,1)S(1)}, u32[]{:S(2)}, u32[]{:S(2)}) collective-permute-start(bf16[1408,256]{1,0:T(8,128)(2,1)S(1)} %get-tuple-element.67), channel_id=1, source_target_pairs={{0,8},{1,9},{2,10},{3,11},{4,12},{5,13},{6,14},{7,15},{8,16},{9,17... | collective-permute-start | bytes 2162696 | tf_op jit(solution)/shard_map/ppermute | solution.py:31
  163.5 5.1 collective-permute-start.3
  227.7 16.7 %all-to-all-start.1 = ((bf16[8,384,128]{1,2,0:T(8,128)(2,1)}), bf16[8,384,128]{1,2,0:T(8,128)(2,1)S(1)}, u32[]{:S(2)}, u32[]{:S(2)}) async-start(bf16[8,384,128]{1,2,0:T(8,128)(2,1)} %copy.68), calls=%async_computation.1 | async-start | bytes 1572864 | tf_op jit(solution)/shard_map/all_to_all | solution.py:633
  244.4 4.1 copy-start.2
  248.5 25.4 %copy-start.5 = (f32[384,1024]{1,0:T(8,128)}, f32[384,1024]{1,0:T(8,128)S(1)}, u32[]{:S(2)}) copy-start(f32[384,1024]{1,0:T(8,128)S(1)} %get-tuple-element.53) | copy-start | bytes 4718596
  248.9 9.1 %copy-start.27 = (bf16[384,1024]{1,0:T(8,128)(2,1)S(1)}, bf16[384,1024]{1,0:T(8,128)(2,1)}, u32[]{:S(2)}) copy-start(bf16[384,1024]{1,0:T(8,128)(2,1)} %param.20) | copy-start | bytes 2359300
  258.0 10.0 %copy-start.25 = (bf16[1024,4096]{1,0:T(8,128)(2,1)S(1)}, bf16[1024,4096]{1,0:T(8,128)(2,1)}, u32[]{:S(2)}) copy-start(bf16[1024,4096]{1,0:T(8,128)(2,1)} %all-gather.12.cloned.1.call-done) | copy-start | bytes 25165828
  268.0 5.9 copy-start.10
  268.0 5.9 copy-start.26
  273.9 7.1 %copy-start.8 = (bf16[1024,1024]{1,0:T(8,128)(2,1)S(1)}, bf16[1024,1024]{1,0:T(8,128)(2,1)}, u32[]{:S(2)}) copy-start(bf16[1024,1024]{1,0:T(8,128)(2,1)} %all-gather.10.cloned.1.call-done) | copy-start | bytes 6291460
  281.0 1.2 copy-start.3
  368.6 2.8 copy-start.7
  372.1 23.4 %collective-permute-start.4 = (bf16[1408,256]{1,0:T(8,128)(2,1)S(1)}, bf16[1408,256]{1,0:T(8,128)(2,1)S(1)}, u32[]{:S(2)}, u32[]{:S(2)}) collective-permute-start(bf16[1408,256]{1,0:T(8,128)(2,1)S(1)} %get-tuple-element.62), channel_id=1, source_target_pairs={{0,8},{1,9},{2,10},{3,11},{4,12},{5,13},{6,14},{7,15},{8,16},{9,17... | collective-permute-start | bytes 2162696 | tf_op jit(solution)/shard_map/ppermute | solution.py:31
  393.7 14.5 %copy-start.11 = (bf16[3072,128]{1,0:T(8,128)(2,1)S(1)}, bf16[3072,128]{1,0:T(8,128)(2,1)}, u32[]{:S(2)}) copy-start(bf16[3072,128]{1,0:T(8,128)(2,1)} %get-tuple-element.28) | copy-start | bytes 2359300
  393.7 14.0 %collective-permute-start.5 = (bf16[1408,256]{1,0:T(8,128)(2,1)S(1)}, bf16[1408,256]{1,0:T(8,128)(2,1)S(1)}, u32[]{:S(2)}, u32[]{:S(2)}) collective-permute-start(bf16[1408,256]{1,0:T(8,128)(2,1)S(1)} %get-tuple-element.63), channel_id=1, source_target_pairs={{8,0},{9,1},{10,2},{11,3},{12,4},{13,5},{14,6},{15,7},{16,8},{17,9... | collective-permute-start | bytes 2162696 | tf_op jit(solution)/shard_map/ppermute | solution.py:31
  409.9 55.2 %all-to-all-start.3 = ((bf16[8,384,384]{2,1,0:T(8,128)(2,1)}), bf16[8,384,384]{2,1,0:T(8,128)(2,1)S(1)}, u32[]{:S(2)}, u32[]{:S(2)}) async-start(bf16[8,384,384]{2,1,0:T(8,128)(2,1)} %bitcast.154), calls=%async_computation.3 | async-start | bytes 4718592 | tf_op jit(solution)/shard_map/all_to_all | solution.py:633
  413.8 4.4 copy-start.28
  413.8 4.4 copy-start.30
  418.2 7.0 copy-start.6
  418.2 7.0 copy-start.29
  666.4 3.3 copy-start
  682.2 5.9 copy-start.4
  682.3 5.9 copy-start.9
Sparse Core Ops, SparseCore 0:
  9.6 49.0 all-gather.7
  60.2 22.5 all-gather.9
  84.4 58.2 all-gather.11
  144.1 66.1 all-gather.13

commit v3 on v2

--- a/solution.py
+++ b/solution.py
@@ -15,7 +15,6 @@
 PAIR = 2 * HEAD_DIM
 GROUP = HEADS // 2
 BLOCK = 256
-HALO = 1408
 SLOTS = 63
 
 EPSILON = 1e-06
@@ -62,21 +61,37 @@
     return op(values.reshape(values.shape[0] // 8, 8, values.shape[1]), axis=0)
 
 
-def attend_kernel(meta, q_ref, k_ref, v_ref, o_ref, ot_ref, lse_ref, vt, scores):
-    tiles = o_ref.shape[0] // BLOCK
-    window = k_ref.shape[1]
+def lane_marks():
+    lane = lax.broadcasted_iota(jnp.int32, (BLOCK, PAIR), 1)
+    return lane // HEAD_DIM, lane % HEAD_DIM > 0
+
+
+def asking(query, marks, half, usable):
+    wanted = jnp.where((marks.astype(jnp.float32) > 0) & usable, 0.0, NEG_BIG).astype(jnp.bfloat16)
+    return [jnp.where(half == h, query, wanted) for h in range(2)]
+
+
+def attend_kernel(meta, q_ref, k_ref, v_ref, m_ref, o_ref, ot_ref, lse_ref, vt, k_aug, scores):
+    rows_all = o_ref.shape[0]
+    tiles = rows_all // BLOCK
+    window = k_ref.shape[0]
+    halo = (window - BLOCK - rows_all) // 2
+    half, usable = lane_marks()
 
     @pl.loop(0, window // BLOCK)
     def _(i):
         at = pl.ds(pl.multiple_of(i * BLOCK, BLOCK), BLOCK)
         vt[:, at] = v_ref[at, :].T
+        for h in range(2):
+            k_aug[h, at, :] = jnp.where(half == h, k_ref[at, :], m_ref[at, :])
 
     @pl.loop(0, tiles)
     def _(t):
         start = meta[2 * t]
         count = meta[2 * t + 1]
         rows = pl.ds(pl.multiple_of(t * BLOCK, BLOCK), BLOCK)
-        query = [q_ref[h, rows, :] for h in range(2)]
+        spots = pl.ds(pl.multiple_of(halo + t * BLOCK, BLOCK), BLOCK)
+        query = asking(q_ref[rows, :], m_ref[spots, :], half, usable)
 
         def score(i, tops):
             at = pl.ds(pl.multiple_of(start + i * BLOCK, 128), BLOCK)
@@ -84,7 +99,7 @@
             new = []
             for h in range(2):
                 part = lax.dot_general(
-                    k_ref[h, at, :], query[h], NT, preferred_element_type=jnp.float32
+                    k_aug[h, at, :], query[h], NT, preferred_element_type=jnp.float32
                 )
                 scores[h, keep, :] = part
                 new.append(jnp.maximum(tops[h], fold_rows(part, jnp.max)))
@@ -122,9 +137,9 @@
         o_ref[rows, :] = out.T.astype(jnp.bfloat16)
 
 
-def attend(meta, q_aug, k_aug, values):
-    rows = q_aug.shape[1]
-    window = k_aug.shape[1]
+def attend(meta, query, keys, values, marks):
+    rows = query.shape[0]
+    window = keys.shape[0]
     deepest = (2 * IMG + 3 * BLOCK) // BLOCK * BLOCK
     vmem = pl.BlockSpec(memory_space=pltpu.VMEM)
     return pl.pallas_call(
@@ -134,30 +149,35 @@
             jax.ShapeDtypeStruct((PAIR, rows), jnp.float32),
             jax.ShapeDtypeStruct((8, rows), jnp.float32),
         ),
-        in_specs=[pl.BlockSpec(memory_space=pltpu.SMEM), vmem, vmem, vmem],
+        in_specs=[pl.BlockSpec(memory_space=pltpu.SMEM), vmem, vmem, vmem, vmem],
         out_specs=(vmem, vmem, vmem),
         scratch_shapes=[
             pltpu.VMEM((PAIR, window), jnp.bfloat16),
+            pltpu.VMEM((2, window, PAIR), jnp.bfloat16),
             pltpu.VMEM((2, deepest, BLOCK), jnp.float32),
         ],
         cost_estimate=pl.CostEstimate(
             flops=4 * rows * 2 * IMG * PAIR, transcendentals=2 * rows * IMG, bytes_accessed=9 << 20
         ),
         name="attend",
-    )(meta, q_aug, k_aug, values)
+    )(meta, query, keys, values, marks)
 
 
 def attend_back_kernel(
-    meta, q_ref, k_ref, v_ref, g_ref, ot_ref, lse_ref, dq_ref, dk_ref, dv_ref, kt
+    meta, q_ref, k_ref, v_ref, m_ref, g_ref, ot_ref, lse_ref, dq_ref, dk_ref, dv_ref, kt, k_aug
 ):
-    tiles = dq_ref.shape[0] // BLOCK
-    window = k_ref.shape[1]
-    half = lax.broadcasted_iota(jnp.int32, (BLOCK, PAIR), 1) // HEAD_DIM
+    rows_all = dq_ref.shape[0]
+    tiles = rows_all // BLOCK
+    window = k_ref.shape[0]
+    halo = (window - BLOCK - rows_all) // 2
+    half, usable = lane_marks()
 
     @pl.loop(0, window // BLOCK)
     def _(i):
         at = pl.ds(pl.multiple_of(i * BLOCK, BLOCK), BLOCK)
-        kt[:, at] = jnp.where(half == 0, k_ref[0, at, :], k_ref[1, at, :]).T
+        kt[:, at] = k_ref[at, :].T
+        for h in range(2):
+            k_aug[h, at, :] = jnp.where(half == h, k_ref[at, :], m_ref[at, :])
         dk_ref[at, :] = jnp.zeros((BLOCK, PAIR), jnp.float32)
         dv_ref[at, :] = jnp.zeros((BLOCK, PAIR), jnp.float32)
 
@@ -168,7 +188,8 @@
         rows = pl.ds(pl.multiple_of(t * BLOCK, BLOCK), BLOCK)
         grad = g_ref[rows, :]
         blank = jnp.zeros_like(grad)
-        query = [q_ref[h, rows, :] for h in range(2)]
+        spots = pl.ds(pl.multiple_of(halo + t * BLOCK, BLOCK), BLOCK)
+        query = asking(q_ref[rows, :], m_ref[spots, :], half, usable)
         query_only = jnp.concatenate(
             [jnp.where(half == h, query[h], blank) for h in range(2)], axis=0
         )
@@ -187,7 +208,7 @@
             probs, slopes, new = [], [], []
             for h in range(2):
                 part = lax.dot_general(
-                    k_ref[h, at, :], query[h], NT, preferred_element_type=jnp.float32
+                    k_aug[h, at, :], query[h], NT, preferred_element_type=jnp.float32
                 )
                 weights = jnp.exp(part - lse[h])
                 pull = lax.dot_general(value, grads[h], NT, preferred_element_type=jnp.float32)
@@ -205,9 +226,9 @@
         dq_ref[rows, :] = dq.T.astype(jnp.bfloat16)
 
 
-def attend_back(meta, q_aug, k_aug, values, grad, out_t, lse):
-    rows = q_aug.shape[1]
-    window = k_aug.shape[1]
+def attend_back(meta, query, keys, values, marks, grad, out_t, lse):
+    rows = query.shape[0]
+    window = keys.shape[0]
     vmem = pl.BlockSpec(memory_space=pltpu.VMEM)
     return pl.pallas_call(
         attend_back_kernel,
@@ -216,20 +237,364 @@
             jax.ShapeDtypeStruct((window, PAIR), jnp.float32),
             jax.ShapeDtypeStruct((window, PAIR), jnp.float32),
         ),
-        in_specs=[pl.BlockSpec(memory_space=pltpu.SMEM)] + [vmem] * 6,
+        in_specs=[pl.BlockSpec(memory_space=pltpu.SMEM)] + [vmem] * 7,
         out_specs=(vmem, vmem, vmem),
-        scratch_shapes=[pltpu.VMEM((PAIR, window), jnp.bfloat16)],
+        scratch_shapes=[
+            pltpu.VMEM((PAIR, window), jnp.bfloat16),
+            pltpu.VMEM((2, window, PAIR), jnp.bfloat16),
+        ],
         cost_estimate=pl.CostEstimate(
             flops=10 * rows * 2 * IMG * PAIR, transcendentals=2 * rows * IMG, bytes_accessed=16 << 20
         ),
         name="attend_back",
-    )(meta, q_aug, k_aug, values, grad, out_t, lse)
+    )(meta, query, keys, values, marks, grad, out_t, lse)
 
 
 CHUNK = 64
 LAG = 2
 MESH = pl.DeviceIdType.MESH
-STAGES = 6
+
+
+def split_index(f, r):
+    return f // 2, f % 2, (r % GROUP) // 2, r % 2
+
+
+def mixed_bits(left, right):
+    value = 0
+    for weight in (4, 2, 1):
+        value = value + weight * ((left // weight + right // weight) % 2)
+    return value
+
+
+def remote(source, target, send, recv, peer):
+    return pltpu.make_async_remote_copy(
+        src_ref=source,
+        dst_ref=target,
+        send_sem=send,
+        recv_sem=recv,
+        device_id=peer,
+        device_id_type=MESH,
+    )
+
+
+def greet(peers, optional=()):
+    barrier = pltpu.get_barrier_semaphore()
+    expected = len(peers)
+    for peer in peers:
+        pl.semaphore_signal(barrier, inc=1, device_id=peer, device_id_type=MESH)
+    for there, peer in optional:
+
+        @pl.when(there)
+        def _():
+            pl.semaphore_signal(barrier, inc=1, device_id=peer, device_id_type=MESH)
+
+        expected = expected + there.astype(jnp.int32)
+    pl.semaphore_wait(barrier, expected)
+
+
+def qkv_kernel(
+    replicas,
+    tokens_ref,
+    small_ref,
+    codes_ref,
+    w_ref,
+    act_ref,
+    q_out,
+    k_out,
+    v_out,
+    codes_out,
+    small_out,
+    w_buf,
+    stage,
+    bias,
+    own_sem,
+    x_sem,
+    core_sem,
+    relay_sem,
+    block_sem,
+    halo_sem,
+    code_sem,
+    edge_sem,
+    small_sem,
+):
+    f = lax.axis_index("fsdp")
+    r = lax.axis_index("rep")
+    x, c, z, y = split_index(f, r)
+    lo = r % GROUP
+    base = r - lo
+    tok_rows = tokens_ref.shape[0]
+    rows = GROUP * tok_rows
+    halo = (k_out.shape[0] - BLOCK - rows) // 2
+    half = GROUP // 2
+    share = w_ref.shape[0]
+    core_peer = (x * 2 + 1 - c, r)
+    x_peer = ((1 - x) * 2 + c, r)
+    fsdp_peers = [((f + step) % 4, r) for step in range(1, 4)]
+    plane = [(f, base + (lo + step) % GROUP) for step in range(1, GROUP)]
+    spot = f * replicas + r
+    has_next = spot + GROUP < 4 * replicas
+    has_prev = spot >= GROUP
+    after = lax.rem(spot + GROUP, 4 * replicas)
+    before = lax.rem(spot + 3 * replicas + (replicas - GROUP), 4 * replicas)
+    next_peer = (after // replicas, lax.rem(after, replicas))
+    prev_peer = (before // replicas, lax.rem(before, replicas))
+    greet(fsdp_peers + plane, [(has_next, next_peer), (has_prev, prev_peer)])
+
+    def small_copy(step):
+        return remote(
+            small_ref,
+            small_out.at[f],
+            small_sem.at[0, step - 1],
+            small_sem.at[1, step - 1],
+            fsdp_peers[step - 1],
+        )
+
+    def lanes(part):
+        return pl.ds(part * PAIR, PAIR)
+
+    def shard_rows(owner):
+        return pl.ds(pl.multiple_of(owner * share, share), share)
+
+    def columns(part, pair):
+        return w_ref.at[:, pl.ds(pl.multiple_of(part * D + pair * PAIR, PAIR), PAIR)]
+
+    def slot(e, owner, part):
+        return w_buf.at[e, shard_rows(owner), lanes(part)]
+
+    def x_copy(e, part):
+        pair = mixed_bits(lo, e)
+        return remote(
+            columns(part, pair), slot(e, f, part), x_sem.at[0, e, part], x_sem.at[1, e, part], x_peer
+        )
+
+    def core_copy(e, part):
+        pair = mixed_bits(lo, e)
+        return remote(
+            columns(part, pair),
+            slot(e, f, part),
+            core_sem.at[0, e, part],
+            core_sem.at[1, e, part],
+            core_peer,
+        )
+
+    def own_copy(e, part):
+        pair = mixed_bits(lo, e)
+        return pltpu.make_async_copy(columns(part, pair), slot(e, f, part), own_sem.at[e, part])
+
+    def relay_copy(e, part):
+        here = slot(e, (1 - x) * 2 + c, part)
+        return remote(here, here, relay_sem.at[0, e, part], relay_sem.at[1, e, part], core_peer)
+
+    def code_copy(step):
+        return remote(
+            codes_ref,
+            codes_out.at[half + lo],
+            code_sem.at[0, step - 1],
+            code_sem.at[1, step - 1],
+            plane[step - 1],
+        )
+
+    order = (4, 5, 6, 7, 2, 3, 1, 0)
+    for step in range(1, 4):
+        small_copy(step).start()
+    for e in order:
+        for part in range(3):
+            x_copy(e, part).start()
+            core_copy(e, part).start()
+            own_copy(e, part).start()
+    for step in range(1, GROUP):
+        code_copy(step).start()
+    codes_out[half + lo] = codes_ref[...]
+
+    k_out[2 * halo + rows :, :] = jnp.zeros((BLOCK, PAIR), jnp.bfloat16)
+    v_out[2 * halo + rows :, :] = jnp.zeros((BLOCK, PAIR), jnp.bfloat16)
+    for there, low, edge in ((has_prev, 0, 0), (has_next, halo + rows, half + GROUP)):
+
+        @pl.when(jnp.logical_not(there))
+        def _():
+            k_out[low : low + halo, :] = jnp.zeros((halo, PAIR), jnp.bfloat16)
+            v_out[low : low + halo, :] = jnp.zeros((halo, PAIR), jnp.bfloat16)
+            codes_out[edge : edge + half] = jnp.zeros((half, 8, PAIR), jnp.float32)
+
+    unit, scale = normalize(tokens_ref[...].astype(jnp.float32))
+    small_out[f] = small_ref[...]
+    for step in range(1, 4):
+        small_copy(step).wait()
+    table = [small_out[owner].astype(jnp.float32) for owner in range(4)]
+
+    def vector(line):
+        return jnp.concatenate(
+            [table[owner][line + row : line + row + 1] for owner in range(4) for row in range(2)],
+            axis=1,
+        )
+
+    for which, line in ((0, 4), (1, 6)):
+        bias[which] = jnp.concatenate(
+            [table[owner][line : line + 2] for owner in range(4)], axis=0
+        )
+    act_ref[...] = (unit * vector(0) + vector(2)).astype(jnp.bfloat16)
+
+    def block_copy(e, part):
+        pair = mixed_bits(lo, e)
+        into = (q_out, k_out, v_out)[part]
+        lead = lo * tok_rows + (0 if part == 0 else halo)
+        return remote(
+            stage.at[e, part],
+            into.at[pl.ds(pl.multiple_of(lead, 128), tok_rows), :],
+            block_sem.at[0, e, part],
+            block_sem.at[1, e, part],
+            (f, base + pair),
+        )
+
+    @pl.loop(0, GROUP)
+    def _(s):
+        e = jnp.where(s < 4, s + 4, jnp.where(s < 6, s - 2, 7 - s))
+        pair = mixed_bits(lo, e)
+        for part in range(3):
+            x_copy(e, part).wait_recv()
+            relay_copy(e, part).start()
+        for part in range(3):
+            own_copy(e, part).wait()
+            core_copy(e, part).wait_recv()
+            relay_copy(e, part).wait_recv()
+        result = matmul(act_ref[...], w_buf[e])
+        outs = (
+            (result[:, :PAIR] + bias[0, pl.ds(pair, 1), :]) * (HEAD_DIM**-0.5),
+            result[:, PAIR : 2 * PAIR],
+            result[:, 2 * PAIR :] + bias[1, pl.ds(pair, 1), :],
+        )
+        for part in range(3):
+            stage[e, part] = outs[part].astype(jnp.bfloat16)
+
+        @pl.when(s < GROUP - 1)
+        def _():
+            for part in range(3):
+                block_copy(e, part).start()
+
+        @pl.when(s == GROUP - 1)
+        def _():
+            for part, into in enumerate((q_out, k_out, v_out)):
+                lead = lo * tok_rows + (0 if part == 0 else halo)
+                into[pl.ds(pl.multiple_of(lead, 128), tok_rows), :] = outs[part].astype(
+                    jnp.bfloat16
+                )
+
+    def halo_copy(source, part, forward):
+        into = (k_out, v_out)[part]
+        lead = source * tok_rows
+        put = lead + halo - rows if forward else lead + halo + rows
+        return remote(
+            into.at[pl.ds(pl.multiple_of(halo + lead, 128), tok_rows), :],
+            into.at[pl.ds(pl.multiple_of(put, 128), tok_rows), :],
+            halo_sem.at[0, source, part],
+            halo_sem.at[1, source, part],
+            next_peer if forward else prev_peer,
+        )
+
+    def pass_on(source):
+        for there, forward, fits in (
+            (has_next, True, source >= half),
+            (has_prev, False, source < half),
+        ):
+
+            @pl.when(there & fits)
+            def _():
+                for part in range(2):
+                    halo_copy(source, part, forward).start()
+
+    pass_on(lo)
+    for e in (1, 2, 3, 4, 5, 6, 7):
+        for part in range(3):
+            block_copy(e, part).wait_recv()
+        pass_on(mixed_bits(lo, e))
+
+    for step in range(1, GROUP):
+        code_copy(step).wait()
+
+    def edge_copy(forward):
+        low, put = (GROUP, 0) if forward else (half, half + GROUP)
+        return remote(
+            codes_out.at[pl.ds(low, half)],
+            codes_out.at[pl.ds(put, half)],
+            edge_sem.at[0, int(forward)],
+            edge_sem.at[1, int(forward)],
+            next_peer if forward else prev_peer,
+        )
+
+    sides = ((has_next, has_prev, True), (has_prev, has_next, False))
+    for there, here, forward in sides:
+
+        @pl.when(there)
+        def _():
+            edge_copy(forward).start()
+
+    for e in range(GROUP):
+        for part in range(3):
+            x_copy(e, part).wait_send()
+            core_copy(e, part).wait_send()
+            relay_copy(e, part).wait_send()
+            if e > 0:
+                block_copy(e, part).wait_send()
+    for there, here, forward in sides:
+        sources = range(half, GROUP) if forward else range(half)
+
+        @pl.when(there)
+        def _():
+            edge_copy(forward).wait_send()
+            for source in sources:
+                for part in range(2):
+                    halo_copy(source, part, forward).wait_send()
+
+        @pl.when(here)
+        def _():
+            edge_copy(forward).wait_recv()
+            for source in sources:
+                for part in range(2):
+                    halo_copy(source, part, forward).wait_recv()
+
+
+def project(replicas, tokens, small, codes, w_qkv):
+    tok_rows = tokens.shape[0]
+    rows = GROUP * tok_rows
+    window = 2 * rows + BLOCK
+    low = jnp.bfloat16
+    vmem = pl.BlockSpec(memory_space=pltpu.VMEM)
+    dma = pltpu.SemaphoreType.DMA
+    shape = jax.ShapeDtypeStruct
+    return pl.pallas_call(
+        functools.partial(qkv_kernel, replicas),
+        out_shape=(
+            shape((tok_rows, D), low),
+            shape((rows, PAIR), low),
+            shape((window, PAIR), low),
+            shape((window, PAIR), low),
+            shape((2 * GROUP, 8, PAIR), jnp.float32),
+            shape((4,) + small.shape, low),
+        ),
+        in_specs=[vmem, vmem, vmem, pl.BlockSpec(memory_space=pl.ANY)],
+        out_specs=(vmem,) * 6,
+        scratch_shapes=[
+            pltpu.VMEM((GROUP, D, 3 * PAIR), low),
+            pltpu.VMEM((GROUP, 3, tok_rows, PAIR), low),
+            pltpu.VMEM((2, GROUP, PAIR), jnp.float32),
+            dma((GROUP, 3)),
+            dma((2, GROUP, 3)),
+            dma((2, GROUP, 3)),
+            dma((2, GROUP, 3)),
+            dma((2, GROUP, 3)),
+            dma((2, GROUP, 2)),
+            dma((2, GROUP - 1)),
+            dma((2, 2)),
+            dma((2, 3)),
+        ],
+        compiler_params=pltpu.CompilerParams(
+            collective_id=2, has_side_effects=True, vmem_limit_bytes=40 << 20
+        ),
+        cost_estimate=pl.CostEstimate(
+            flops=2 * tok_rows * D * 3 * D, transcendentals=0, bytes_accessed=60 << 20
+        ),
+        name="project",
+    )(tokens, small, codes, w_qkv)
 
 
 def reduce_kernel(
@@ -238,7 +603,10 @@
     out_ref,
     qkv_ref,
     small_ref,
-    final,
+    down_final,
+    up_final,
+    out_final,
+    qkv_final,
     small_final,
     own,
     from_core,
@@ -260,8 +628,7 @@
 ):
     f = lax.axis_index("fsdp")
     r = lax.axis_index("rep")
-    x, c = f // 2, f % 2
-    z, y = (r % GROUP) // 2, r % 2
+    x, c, z, y = split_index(f, r)
     base = r - r % GROUP
     core_peer = (x * 2 + 1 - c, r)
     x_peer = ((1 - x) * 2 + c, r)
@@ -269,30 +636,18 @@
     z_spots = [(z + step) % 4 for step in range(1, 4)]
     z_peers = [(f, base + spot * 2 + y) for spot in z_spots]
     plane = [(f, base + (r % GROUP + step) % GROUP) for step in range(1, GROUP)]
-    total = final.shape[0]
-
-    barrier = pltpu.get_barrier_semaphore()
-    for peer in [core_peer, x_peer] + plane:
-        pl.semaphore_signal(barrier, inc=1, device_id=peer, device_id_type=MESH)
-    pl.semaphore_wait(barrier, 2 + len(plane))
-
-    def remote(source, target, send, recv, peer):
-        return pltpu.make_async_remote_copy(
-            src_ref=source,
-            dst_ref=target,
-            send_sem=send,
-            recv_sem=recv,
-            device_id=peer,
-            device_id_type=MESH,
-        )
+    total = own.shape[0]
+
+    greet([core_peer, x_peer] + plane)
 
     refs = (down_ref, up_ref, out_ref, qkv_ref)
+    finals = (down_final, up_final, out_final, qkv_final)
     spans = []
     first = 0
-    for ref in refs:
-        height = ref.shape[0] // 4 // CHUNK
-        amount = height * (ref.shape[1] // D)
-        spans.append((ref, first, first + amount, height))
+    for ref, final in zip(refs, finals):
+        height = final.shape[0] // CHUNK
+        amount = height * (final.shape[1] // D)
+        spans.append((ref, first, first + amount, height, final))
         first += amount
 
     def piece(ref, low, height, k, owner):
@@ -321,7 +676,7 @@
         return copies
 
     def enter(k):
-        for ref, low, high, height in spans:
+        for ref, low, high, height, final in spans:
 
             @pl.when((k >= low) & (k < high))
             def _():
@@ -358,15 +713,19 @@
             )
         return copies
 
-    def zz_copies(k):
-        here = final.at[k, my_rows, my_lanes]
-        return [
-            remote(here, here, zz_sem.at[0, k, step], zz_sem.at[1, k, step], z_peers[step])
-            for step in range(3)
-        ]
-
-    def yy_copy(k):
-        here = final.at[k, my_rows]
+    def place(low, height, k, shift, tall, across, wide):
+        at = k - low
+        top = (at % height) * CHUNK + shift
+        left = (at // height) * D + across
+        return (
+            pl.ds(pl.multiple_of(top, tall), tall),
+            pl.ds(pl.multiple_of(left, wide), wide),
+        )
+
+    def zz_copy(k, step, here):
+        return remote(here, here, zz_sem.at[0, k, step], zz_sem.at[1, k, step], z_peers[step])
+
+    def yy_copy(k, here):
         return remote(here, here, yy_sem.at[0, k], yy_sem.at[1, k], y_peer)
 
     def core_sum(k):
@@ -407,14 +766,28 @@
         value = own[k, x, my_rows, my_lanes].astype(jnp.float32)
         for step in range(3):
             value = value + from_z[k, step].astype(jnp.float32)
-        final[k, my_rows, my_lanes] = value.astype(jnp.bfloat16)
-        for copy in zz_copies(k):
-            copy.start()
+        value = value.astype(jnp.bfloat16)
+        for ref, low, high, height, final in spans:
+
+            @pl.when((k >= low) & (k < high))
+            def _():
+                at = place(low, height, k, y * half, half, z * quarter, quarter)
+                final[at] = value
+                for step in range(3):
+                    zz_copy(k, step, final.at[at]).start()
 
     def z_join(k):
-        for copy in zz_copies(k):
-            copy.wait()
-        yy_copy(k).start()
+        for step in range(3):
+            zz_copy(k, step, from_z.at[k, step]).wait()
+        for ref, low, high, height, final in spans:
+
+            @pl.when((k >= low) & (k < high))
+            def _():
+                at = place(low, height, k, y * half, half, 0, D)
+                yy_copy(k, final.at[at]).start()
+
+    def y_join(k):
+        yy_copy(k, from_y.at[k]).wait()
 
     def small_enter(side):
         return remote(
@@ -441,7 +814,7 @@
     for side in range(2):
         small_enter(side).start()
 
-    steps = (enter, core_sum, x_sum, y_sum, z_sum, z_join, lambda k: yy_copy(k).wait())
+    steps = (enter, core_sum, x_sum, y_sum, z_sum, z_join, y_join)
 
     @pl.loop(0, total + LAG * (len(steps) - 1))
     def _(now):
@@ -484,12 +857,12 @@
     low = jnp.bfloat16
     return pl.pallas_call(
         reduce_kernel,
-        out_shape=(
-            jax.ShapeDtypeStruct((chunks, CHUNK, D), low),
-            jax.ShapeDtypeStruct((tall, 128), jnp.float32),
-        ),
+        out_shape=tuple(
+            jax.ShapeDtypeStruct((weight.shape[0] // 4, weight.shape[1]), low) for weight in weights
+        )
+        + (jax.ShapeDtypeStruct((tall, 128), jnp.float32),),
         in_specs=[anywhere] * 4 + [vmem],
-        out_specs=(vmem, vmem),
+        out_specs=(vmem,) * 5,
         scratch_shapes=[
             pltpu.VMEM((chunks, 2, CHUNK, D), low),
             pltpu.VMEM((chunks, 2, CHUNK, D), low),
@@ -559,9 +932,15 @@
         mlp_scale,
         up_bias,
     )
-    vectors = lax.all_gather(jnp.concatenate(small), "fsdp", axis=0, tiled=False).astype(
-        jnp.float32
+    sizes = [member.shape[0] for member in small]
+    packed = jnp.concatenate(small + (jnp.zeros((-sum(sizes) % 2048,), jnp.bfloat16),))
+    codes = jnp.where(pad_mask > 0, image_ids + 1, 0).astype(jnp.float32).reshape(-1, PAIR)
+    code_rows = codes.shape[0]
+    codes = jnp.concatenate([codes, jnp.zeros((8 - code_rows, PAIR), jnp.float32)], axis=0)
+    act_one, query, key_window, value_window, codes, vectors = project(
+        replicas, tokens, packed.reshape(-1, PAIR), codes, w_qkv
     )
+    vectors = vectors.reshape(4, -1).astype(jnp.float32)
     parts = []
     place = 0
     for member in small:
@@ -581,23 +960,17 @@
         hidden_bias,
     ) = parts
 
-    codes = jnp.where(pad_mask > 0, image_ids + 1, 0)
-    codes = lax.all_gather(codes, "rep", axis=0, tiled=True, axis_index_groups=groups)
-    codes = [
-        from_behind(codes[rows - HALO :], both, GROUP),
-        codes,
-        from_behind(codes[:HALO], both, -GROUP),
-        jnp.zeros((BLOCK,), jnp.int32),
-    ]
     wide_qkv = lax.all_gather(w_qkv, "fsdp", axis=0, tiled=True)
     wide_out = lax.all_gather(w_out, "fsdp", axis=0, tiled=True)
     wide_up = lax.all_gather(w_up, "fsdp", axis=0, tiled=True)
     wide_down = lax.all_gather(w_down, "fsdp", axis=0, tiled=True)
 
-    window = HALO + rows + HALO + BLOCK
-    seen = jnp.concatenate(codes)
+    window = key_window.shape[0]
+    halo = rows // 2
+    seen = codes[:, :code_rows].reshape(-1).astype(jnp.int32)
+    seen = jnp.concatenate([seen, jnp.zeros((BLOCK,), jnp.int32)])
     spot = jnp.arange(window, dtype=jnp.int32)
-    asked = seen[HALO : HALO + rows]
+    asked = seen[halo : halo + rows]
     tile_codes = asked.reshape(rows // BLOCK, BLOCK)
     first_code = jnp.min(jnp.where(tile_codes > 0, tile_codes, 1 << 30), axis=1)
     last_code = jnp.max(tile_codes, axis=1)
@@ -607,46 +980,19 @@
     count = jnp.where(last_code > 0, (finish - begin + BLOCK - 1) // BLOCK, 0)
     meta = jnp.stack([begin, count], axis=1).reshape(-1)
 
-    lane = jnp.arange(PAIR, dtype=jnp.int32)
-    lane_half = lane // HEAD_DIM
-    lane_slot = lane % HEAD_DIM
+    lane_slot = jnp.arange(PAIR, dtype=jnp.int32) % HEAD_DIM
     key_slot = jnp.where(seen > 0, 1 + (seen - 1) % SLOTS, 0)
-    ask_slot = key_slot[HALO : HALO + rows]
-    key_marks = (key_slot[:, None] == lane_slot[None]).astype(jnp.bfloat16)
-    ask_marks = jnp.where(
-        (ask_slot[:, None] == lane_slot[None]) & (ask_slot[:, None] > 0), 0.0, NEG_BIG
-    ).astype(jnp.bfloat16)
+    marks = (key_slot[:, None] == lane_slot[None]).astype(jnp.bfloat16)
 
     inputs = tokens.astype(jnp.float32)
     unit_one, scale_one = normalize(inputs)
-    act_one = (unit_one * gain_first + shift_first).astype(jnp.bfloat16)
-    qkv_rows = matmul(act_one, wide_qkv)
-    query = ((qkv_rows[:, :D] + query_bias) * factor).astype(jnp.bfloat16)
-    keys = qkv_rows[:, D : 2 * D].astype(jnp.bfloat16)
-    values = (qkv_rows[:, 2 * D :] + value_bias).astype(jnp.bfloat16)
-    sent = jnp.stack(
-        [member.reshape(tok_rows, GROUP, PAIR) for member in (query, keys, values)], axis=2
-    )
-    sent = sent.transpose(1, 0, 2, 3).reshape(GROUP, tok_rows, 3 * PAIR)
 
     def exchange(block):
         return lax.all_to_all(
             block, "rep", split_axis=0, concat_axis=0, tiled=True, axis_index_groups=groups
         )
 
-    mine = exchange(sent).reshape(rows, 3 * PAIR)
-    before = from_behind(mine[rows - HALO :, PAIR:], both, GROUP)
-    after = from_behind(mine[:HALO, PAIR:], both, -GROUP)
-    pad = jnp.zeros((BLOCK, 2 * PAIR), jnp.bfloat16)
-    key_value = jnp.concatenate([before, mine[:, PAIR:], after, pad], axis=0)
-    value_window = key_value[:, PAIR:]
-    k_aug = jnp.stack(
-        [jnp.where(lane_half[None] == h, key_value[:, :PAIR], key_marks) for h in range(2)]
-    )
-    q_aug = jnp.stack(
-        [jnp.where(lane_half[None] == h, mine[:, :PAIR], ask_marks) for h in range(2)]
-    )
-    attn_mine, attn_t, lse = attend(meta, q_aug, k_aug, value_window)
+    attn_mine, attn_t, lse = attend(meta, query, key_window, value_window, marks)
 
     def to_tokens(block):
         back = exchange(block.reshape(GROUP, tok_rows, block.shape[-1]))
@@ -687,19 +1033,15 @@
 
     grad_sent = attn_grad_low.reshape(tok_rows, GROUP, PAIR).transpose(1, 0, 2)
     grad_mine = exchange(grad_sent).reshape(rows, PAIR)
-    dq, dk, dv = attend_back(meta, q_aug, k_aug, value_window, grad_mine, attn_t, lse)
+    dq, dk, dv = attend_back(
+        meta, query, key_window, value_window, marks, grad_mine, attn_t, lse
+    )
     dkv = jnp.concatenate([dk, dv], axis=1)
-    tail = dkv[:HALO].astype(jnp.bfloat16)
-    head = dkv[HALO + rows : HALO + rows + HALO].astype(jnp.bfloat16)
-    from_after = from_behind(tail, both, -GROUP).astype(jnp.float32)
-    from_before = from_behind(head, both, GROUP).astype(jnp.float32)
-    own = dkv[HALO : HALO + rows]
-    gap = jnp.zeros((rows - HALO, 2 * PAIR), jnp.float32)
-    own = (
-        own
-        + jnp.concatenate([from_before, gap], axis=0)
-        + jnp.concatenate([gap, from_after], axis=0)
-    )
+    tail = dkv[:halo].astype(jnp.bfloat16)
+    head = dkv[halo + rows : halo + rows + halo].astype(jnp.bfloat16)
+    from_after = from_behind(tail, both, -GROUP)
+    from_before = from_behind(head, both, GROUP)
+    own = dkv[halo : halo + rows] + jnp.concatenate([from_before, from_after], axis=0)
     dqkv_mine = jnp.concatenate([dq, own.astype(jnp.bfloat16)], axis=1)
     dqkv = to_tokens(dqkv_mine).reshape(tok_rows, GROUP, 3, PAIR)
     dqkv = dqkv.transpose(0, 2, 1, 3).reshape(tok_rows, 3 * D)
@@ -727,8 +1069,8 @@
     )
     packed = jnp.concatenate([member.reshape(owners, -1) for member in small_grads], axis=1)
     packed = packed.reshape(owners, -1, 128)
-    grads, packed = reduce_grads((down_grad, up_grad, out_weight_grad, qkv_weight_grad), packed)
-    grads = grads.astype(jnp.float32)
+    *grads, packed = reduce_grads((down_grad, up_grad, out_weight_grad, qkv_weight_grad), packed)
+    grads = [grad.astype(jnp.float32) for grad in grads]
     if replicas > GROUP:
         apart = [list(range(low, replicas, GROUP)) for low in range(GROUP)]
         grads = lax.psum(grads, "rep", axis_index_groups=apart)
@@ -741,16 +1083,7 @@
         small_out.append(packed[place : place + size])
         place += size
 
-    def joined(start, height, width):
-        deep, across = height // CHUNK, width // D
-        part = grads[start : start + deep * across]
-        part = part.reshape(across, deep, CHUNK, D).transpose(1, 2, 0, 3)
-        return part.reshape(height, width), start + deep * across
-
-    down_out, place = joined(0, *w_down.shape)
-    up_out, place = joined(place, *w_up.shape)
-    out_out, place = joined(place, *w_out.shape)
-    qkv_out, place = joined(place, *w_qkv.shape)
+    down_out, up_out, out_out, qkv_out = grads
     return (
         layer_out,
         tokens_grad,

time: 700 us -> 622 us (0.89); the launches traced: 697 us -> 610 us
  blocking collectives: 94.9 us -> 0 us
  Pallas kernels: 289 us -> 349 us
  waiting for transfers between devices: 103 us -> 73.7 us
  local copies, waits for them, and re-layouts: 49.9 us -> 28.1 us
  starting transfers between devices: 45 us -> 52.1 us
    all_gather x2 -> x0, blocking collectives: 78.3 us -> none  [the longest x1 72.1 us: shards(): lax.all_gather(codes, 'rep', axis=0, tiled=True, axis_index_groups=groups)]
    pallas_call x1 -> x2, Pallas kernels: 176 us -> 249 us  [the longest x1 177 us: reduce_grads(): pl.pallas_call(reduce_kernel, out_shape=tuple((jax.ShapeDtypeStruct((weig...]
    all_gather x1, waiting for transfers between devices: 39.8 us -> 0.02 us  [shards(): wide_qkv = lax.all_gather(w_qkv, 'fsdp', axis=0, tiled=True)]
    all_to_all x1 -> x0, blocking collectives: 16.6 us -> none  [exchange(): lax.all_to_all(block, 'rep', split_axis=0, concat_axis=0, tiled=True, axi...]
    convert_element_type x1 -> x6, other arithmetic: 0.45 us -> 13.5 us  [the longest x4 9.83 us: shards(): grads = [grad.astype(jnp.float32) for grad in grads]]
    all_to_all x3, waiting for transfers between devices: 45.9 us -> 58.3 us  [exchange(): lax.all_to_all(block, 'rep', split_axis=0, concat_axis=0, tiled=True, axi...]
    another operation x6 -> x1, other arithmetic: 12.4 us -> 0.32 us  [the longest x2 5.77 us: shards(): jnp.stack([jnp.where(lane_half[None] == h, key_value[:, :PAIR], key_marks...]
    ppermute x6 -> x2, waiting for transfers between devices: 14.8 us -> 5.69 us  [from_behind(): return lax.ppermute(block, axis, route)]
  transfers between devices with their start and end apart: 13 -> 9, of which waited for: 6 -> 6; matrix products, arithmetic and copies ran while one was open for 10% -> 10% of each run, Pallas kernels for 6% -> 28%
where the time goes in v3:
time: 622 us; the launch traced here: 610 us
  Pallas kernels  349 us (56%)
  waiting for transfers between devices  73.7 us (12%)
  matrix products  72.6 us (12%)
  starting transfers between devices  52.1 us (8%)
  local copies, waits for them, and re-layouts  28.1 us (5%)
  other arithmetic  20.5 us (3%)
  between operations  14.6 us (2%)
    pallas_call x1, Pallas kernels, reduce_grads(): pl.pallas_call(reduce_kernel, out_shape=tuple((jax.ShapeDtypeStruct((weig...  177 us
    pallas_call x1, Pallas kernels, project(): pl.pallas_call(functools.partial(qkv_kernel, replicas), out_shape=(shape(...  72 us
    pallas_call x1, Pallas kernels, attend_back(): pl.pallas_call(attend_back_kernel, out_shape=(jax.ShapeDtypeStruct((rows,...  60.8 us
    all_to_all x3, waiting for transfers between devices, exchange(): lax.all_to_all(block, 'rep', split_axis=0, concat_axis=0, tiled=True, axi...  58.3 us
    pallas_call x1, Pallas kernels, attend(): pl.pallas_call(attend_kernel, out_shape=(jax.ShapeDtypeStruct((rows, PAIR...  39.2 us
    ppermute x2, starting transfers between devices, from_behind(): return lax.ppermute(block, axis, route)  33 us
    dot_general x4, matrix products, matmul_nt(): jnp.einsum('te,de->td', left, right, preferred_element_type=jnp.float32)  25.7 us
    dot_general x4, matrix products, matmul_tn(): jnp.einsum('td,te->de', left, right, preferred_element_type=jnp.float32)  25.3 us
  transfers between devices with their start and end apart: 9, of which 6 were waited for; matrix products, arithmetic and copies ran while one was open for 10% of the time, Pallas kernels for 28%

profile of v3, /device:TPU:0, one launch (start us, length us, event | category | flops | bytes accessed | tf_op | source)
XLA Modules:
  0.0 610.3 jit_solution(15230847106853013997)
XLA Ops:
  7.2 0.7 all-gather.5.cloned.1.call-update
  8.1 0.7 all-gather.7.cloned.1.call-update
  8.9 0.7 all-gather.9.cloned.1.call-update
  9.6 0.2 dynamic-update-slice.13
  9.9 0.2 dynamic-update-slice.14
  10.1 0.2 dynamic-update-slice.15
  10.5 0.2 dynamic-update-slice.17
  10.8 0.2 dynamic-update-slice.18
  11.2 0.2 dynamic-update-slice.20
  12.3 72.0 %project.1 = (bf16[384,1024]{1,0:T(8,128)(2,1)S(1)}, bf16[3072,128]{1,0:T(8,128)(2,1)S(1)}, bf16[6400,128]{1,0:T(8,128)(2,1)S(1)}, bf16[6400,128]{1,0:T(8,128)(2...) custom-call(bf16[384,1024]{1,0:T(8,128)(2,1)S(1)} %copy-done, bf16[32,128]{1,0:T(8,128)(2,1)S(1)} %bitcast.114, ...), custom_call_target="tpu_custom_call" | custom-call | flops 2415919104 | bytes 62914560 | tf_op jit(solution)/shard_map/project/pallas_call | solution.py:564
  84.3 1.2 copy-done.2
  85.5 1.2 copy-done.3
  86.7 0.9 copy-done.4
  88.1 0.3 select_reduce_fusion.1
  88.6 0.6 reshape.314.meta
  89.2 3.7 compare_convert_fusion.m_ref
  92.9 39.2 %attend.1 = (bf16[3072,128]{1,0:T(8,128)(2,1)}, f32[128,3072]{1,0:T(8,128)}, f32[8,3072]{1,0:T(8,128)}) custom-call(s32[24]{0:T(128)} %reshape.314.meta, bf16[3072,128]{1,0:T(8,128)(2,1)} %copy-done.4, bf16[6400,128]{1,0:T(8,128)(2,1)} %copy-done.2, bf16[6400,128]{1,0:T(8,128)(2,1)} %copy-done.3, bf16[6400,128]{1,0:T(8,128)(2,1)} %compare_convert_fusion.m_ref), custom_call_target="tpu_custom_call" | custom-call | flops 4309647360 | bytes 9437184 | tf_op jit(solution)/shard_map/attend/pallas_call | solution.py:145
  132.0 2.5 copy.49
  134.6 8.8 %all-to-all-start = ((bf16[8,384,128]{1,2,0:T(8,128)(2,1)}), bf16[8,384,128]{1,2,0:T(8,128)(2,1)S(1)}, u32[]{:S(2)}, u32[]{:S(2)}) async-start(bf16[8,384,128]{1,2,0:T(8,128)(2,1)} %copy.49), calls=%async_computation | async-start | bytes 1572864 | tf_op jit(solution)/shard_map/all_to_all | solution.py:991
  143.8 12.8 %all-to-all-done = bf16[8,384,128]{1,2,0:T(8,128)(2,1)S(1)} async-done(((bf16[8,384,128]{1,2,0:T(8,128)(2,1)}), bf16[8,384,128]{1,2,0:T(8,128)(2,1)S(1)}, u32[]{:S(2)}, u32[]{:S(2)}) %all-to-all-start) | async-done | bytes 786464 | tf_op jit(solution)/shard_map/all_to_all | solution.py:991
  156.6 4.2 fusion.32
  160.8 1.1 copy-done.8
  161.9 0.3 multiply_reduce_fusion.3
  162.3 9.4 %multiply_convert_fusion = (bf16[384,4096]{1,0:T(8,128)(2,1)}, f32[384,4096]{1,0:T(8,128)}) fusion(f32[4096]{0:T(1024)S(1)} %bitcast.130, bf16[1024,4096]{1,0:T(8,128)(2,1)} %all-gather.7.cloned.1.call-done, f32[384,1024]{1,0:T(8,128)} %copy-done.8, f32[1024]{0:T(1024)S(1)} %bitcast.137, f32[1024]{0:T(1024)S(1)} %bitcast.133, f32[384]{0:T(512)S(1)} %add_rsqrt_fusion.1, ...), kind=kOutput, calls=%fused_computation.8 | convolution fusion | flops 3232628736 | bytes 19426304 | tf_op jit(solution)/shard_map/dot_general | solution.py:49
  171.7 7.0 %all-gather.9.cloned.1.call-done = bf16[4096,1024]{1,0:T(8,128)(2,1)} async-done(((bf16[1024,1024]{1,0:T(8,128)(2,1)}), bf16[4096,1024]{1,0:T(8,128)(2,1)}) %all-gather.9.cloned.1.call-update) | async-done | bytes 8388624 | tf_op jit(solution)/shard_map/all_gather | solution.py:966
  178.7 10.1 %fusion.35 = (f32[4096]{0:T(1024)S(1)}, bf16[384,4096]{1,0:T(8,128)(2,1)}) fusion(f32[384,4096]{1,0:T(8,128)} %get-tuple-element.102, bf16[4096,1024]{1,0:T(8,128)(2,1)} %all-gather.9.cloned.1.call-done, bf16[384,1024]{1,0:T(8,128)(2,1)S(1)} %copy-done.31, f32[1024]{0:T(1024)S(1)} %bitcast.139), kind=kOutput, calls=%fused_computation.132 | convolution fusion | flops 3239702528 | bytes 18632704 | tf_op jit(solution)/shard_map/te,de->td/dot_general | solution.py:53
  188.8 6.9 %multiply_reduce_fusion = (f32[1024]{0:T(1024)S(1)}, f32[384]{0:T(512)S(1)}, f32[384]{0:T(512)S(1)}, f32[1024]{0:T(1024)S(1)}, f32[384,1024]{1,0:T(8,128)}) fusion(f32[384,1024]{1,0:T(8,128)S(1)} %copy-done.9, f32[384]{0:T(512)S(1)} %add_rsqrt_fusion.1, f32[384]{0:T(512)S(1)} %broadcast_multiply_fusion.5, f32[1024]{0:T(1024)S(1)} %bitcast.134, ...), kind=kOutput, calls=%fused_computation.39 | convolution fusion | flops 3224761344 | bytes 14698496 | tf_op jit(solution)/shard_map/te,de->td/dot_general | solution.py:53
  195.8 8.0 %fusion.20 = (f32[1024]{0:T(1024)S(1)}, f32[1024]{0:T(1024)S(1)}, bf16[384,1024]{1,0:T(8,128)(2,1)}, f32[1024]{0:T(1024)S(1)}, f32[1024]{0:T(1024)S(1)}, /*index=5*/f32[384,1024]{1,0:T(8,128)S(1)}) fusion(bf16[384,1024]{1,0:T(8,128)(2,1)S(1)} %copy-done.32, f32[1024]{0:T(1024)S(1)} %bitcast.142, f32[1024]{0:T(1024)S(1)} %bitcast.140, ...), kind=kOutput, calls=%fused_computation.38 | convolution fusion | flops 3229478912 | bytes 19437568 | tf_op jit(solution)/shard_map/dot_general | solution.py:49
  203.9 1.0 fusion.24
  204.9 1.0 copy.68
  205.9 5.5 all-to-all-start.1
  211.5 0.5 all-gather.11.cloned.1.call-update
  212.0 12.8 %all-to-all-done.1 = bf16[8,384,128]{2,1,0:T(8,128)(2,1)} async-done(((bf16[8,384,128]{2,1,0:T(8,128)(2,1)}), bf16[8,384,128]{2,1,0:T(8,128)(2,1)}, u32[]{:S(2)}, u32[]{:S(2)}) %all-to-all-start.1) | async-done | bytes 786464 | tf_op jit(solution)/shard_map/all_to_all | solution.py:991
  224.8 60.8 %attend_back.1 = (bf16[3072,128]{1,0:T(8,128)(2,1)}, f32[6400,128]{1,0:T(8,128)}, f32[6400,128]{1,0:T(8,128)}) custom-call(s32[24]{0:T(128)} %reshape.314.meta, bf16[3072,128]{1,0:T(8,128)(2,1)} %copy-done.4, bf16[6400,128]{1,0:T(8,128)(2,1)} %copy-done.2, bf16[6400,128]{1,0:T(8,128)(2,1)} %copy-done.3, bf16[6400,128]{1,0:T(8,128)(2,1)} %compare_convert_fusion.m_ref, ...), custom_call_target="tpu_custom_call" | custom-call | flops 10774118400 | bytes 16777216 | tf_op jit(solution)/shard_map/attend_back/pallas_call | solution.py:233
  285.6 2.3 constant_dynamic-update-slice_fusion.1
  288.0 0.6 copy-done.5
  288.5 0.3 constant_dynamic-update-slice_fusion
  288.8 0.3 convert.5
  289.2 31.6 %collective-permute-start = (bf16[1536,256]{1,0:T(8,128)(2,1)S(1)}, bf16[1536,256]{1,0:T(8,128)(2,1)S(1)}, u32[]{:S(2)}, u32[]{:S(2)}) collective-permute-start(bf16[1536,256]{1,0:T(8,128)(2,1)S(1)} %get-tuple-element.70), channel_id=1, source_target_pairs={{0,8},{1,9},{2,10},{3,11},{4,12},{5,13},{6,14},{7,15},{8,16},{9,17... | collective-permute-start | bytes 2359304 | tf_op jit(solution)/shard_map/ppermute | solution.py:30
  320.8 1.4 collective-permute-start.1
  322.2 0.4 collective-permute-done
  322.6 5.3 collective-permute-done.1
  327.9 0.4 fusion.5
  328.4 1.7 pad_maximum_fusion
  330.1 4.5 all-to-all-start.2
  334.8 3.8 convolution_convert_fusion.3.out_ref
  338.6 7.0 %convolution_convert_fusion.1.down_ref = bf16[4096,1024]{1,0:T(8,128)(2,1)} fusion(bf16[384,4096]{1,0:T(8,128)(2,1)S(1)} %copy-done.35, bf16[384,1024]{1,0:T(8,128)(2,1)S(1)} %copy-done.33, f32[1024]{0:T(1024)S(1)} %bitcast.141), kind=kOutput, calls=%fused_computation.2 | convolution fusion | flops 3226599424 | bytes 12324864 | tf_op jit(solution)/shard_map/td,te->de/dot_general | solution.py:57
  345.6 7.2 %convolution_convert_fusion.up_ref = bf16[1024,4096]{1,0:T(8,128)(2,1)} fusion(bf16[384,4096]{1,0:T(8,128)(2,1)S(1)} %copy-done.34, f32[384,1024]{1,0:T(8,128)S(1)} %copy-done.10, f32[1024]{0:T(1024)S(1)} %bitcast.138, f32[1024]{0:T(1024)S(1)} %bitcast.136, f32[384]{0:T(512)S(1)} %add_rsqrt_fusion.1, f32[384]{0:T(512)S(1)} %broadcast_multiply_fusion.5), kind=kOutput, calls=%fused_computation.1 | convolution fusion | flops 3227385856 | bytes 13118464 | tf_op jit(solution)/shard_map/td,te->de/dot_general | solution.py:57
  352.8 32.7 %all-to-all-done.2 = bf16[8,384,384]{2,1,0:T(8,128)(2,1)} async-done(((bf16[8,384,384]{2,1,0:T(8,128)(2,1)}), bf16[8,384,384]{2,1,0:T(8,128)(2,1)}, u32[]{:S(2)}, u32[]{:S(2)}) %all-to-all-start.2) | async-done | bytes 2359328 | tf_op jit(solution)/shard_map/all_to_all | solution.py:991
  385.5 4.5 copy.67
  390.0 4.5 copy.52
  394.5 1.7 convert_reduce_fusion.1
  396.2 7.6 %fusion.18 = (f32[1024]{0:T(1024)S(1)}, f32[384]{0:T(512)S(1)}, f32[384]{0:T(512)S(1)}, f32[1024]{0:T(1024)S(1)}, f32[384,1024]{1,0:T(8,128)}) fusion(bf16[384,1024]{1,0:T(8,128)(2,1)S(1)} %copy-done, f32[384]{0:T(512)S(1)} %add_rsqrt_fusion, f32[384]{0:T(512)S(1)} %broadcast_multiply_fusion.2, f32[1024]{0:T(1024)S(1)} %bitcast.131, ...), kind=kOutput, calls=%fused_computation.36 | convolution fusion | flops 2419848192 | bytes 11028480 | tf_op jit(solution)/shard_map/te,de->td/dot_general | solution.py:53
  404.0 0.7 reshape.333.small_ref
  404.7 7.3 %convolution_convert_fusion.2.qkv_ref = bf16[1024,3072]{1,0:T(8,128)(2,1)} fusion(bf16[384,1024]{1,0:T(8,128)(2,1)S(1)} %get-tuple-element.45, bf16[384,3072]{0,1:T(8,128)(2,1)} %bitcast.119), kind=kOutput, calls=%fused_computation.10 | convolution fusion | flops 2419064832 | bytes 9437184 | tf_op jit(solution)/shard_map/td,te->de/dot_general | solution.py:57
  411.9 176.8 %reduce_grads.1 = (bf16[1024,1024]{1,0:T(8,128)(2,1)}, bf16[256,4096]{1,0:T(8,128)(2,1)}, bf16[256,1024]{1,0:T(8,128)(2,1)}, bf16[256,3072]{1,0:T(8,128)(2,1)}, f32[28,128]{1,0:T(8,128)}) custom-call(bf16[4096,1024]{1,0:T(8,128)(2,1)} %convolution_convert_fusion.1.down_ref, bf16[1024,4096]{1,0:T(8,128)(2,1)} %convolution_convert_fusion.up_ref, ...), custom_call_target="tpu_custom_call" | custom-call | bytes 209715200 | tf_op jit(solution)/shard_map/reduce_grads/pallas_call | solution.py:858
  588.8 1.4 slice_bitcast_fusion.9
  590.2 1.3 slice_bitcast_fusion.8
  591.5 4.2 convert_element_type.114
  595.8 2.5 convert_element_type.115
  598.3 2.0 convert_element_type.112
  600.3 1.1 convert_element_type.113
  601.4 0.7 copy-done.11
  602.1 1.5 fusion.17
  (139 shorter events, 3.0 us)
Async XLA Ops:
  7.2 149.4 %all-gather.5.cloned.1.call-start = ((), (), s32[]{:S(2)}) async-start(), calls=%async_computation.3 | async-start | bytes 2621440 | tf_op jit(solution)/shard_map/all_gather | solution.py:964
  7.9 1.7 copy-start.15
  7.9 1.7 copy-start.16
  7.9 1.7 copy-start.18
  8.0 1.9 copy-start.19
  8.0 2.1 copy-start.20
  8.0 2.3 copy-start.21
  8.0 2.6 copy-start.22
  8.0 2.8 copy-start.23
  8.0 3.0 copy-start.24
  8.0 3.2 copy-start.25
  8.0 3.4 copy-start.26
  8.0 3.6 copy-start.27
  8.0 3.8 copy-start.17
  8.1 4.2 copy-start
  8.1 4.2 copy-start.1
  8.1 154.2 %all-gather.7.cloned.1.call-start = ((), (), s32[]{:S(2)}) async-start(), calls=%async_computation.4 | async-start | bytes 10485760 | tf_op jit(solution)/shard_map/all_gather | solution.py:965
  8.8 169.9 %all-gather.9.cloned.1.call-start = ((), (), s32[]{:S(2)}) async-start(), calls=%async_computation.5 | async-start | bytes 10485760 | tf_op jit(solution)/shard_map/all_gather | solution.py:966
  84.3 1.2 copy-start.2
  85.5 1.2 copy-start.3
  86.7 0.9 copy-start.4
  134.6 22.0 %all-to-all-start = ((bf16[8,384,128]{1,2,0:T(8,128)(2,1)}), bf16[8,384,128]{1,2,0:T(8,128)(2,1)S(1)}, u32[]{:S(2)}, u32[]{:S(2)}) async-start(bf16[8,384,128]{1,2,0:T(8,128)(2,1)} %copy.49), calls=%async_computation | async-start | bytes 1572864 | tf_op jit(solution)/shard_map/all_to_all | solution.py:991
  156.6 4.2 copy-start.6
  160.8 1.2 copy-start.8
  162.3 16.4 %copy-start.31 = (bf16[384,1024]{1,0:T(8,128)(2,1)S(1)}, bf16[384,1024]{1,0:T(8,128)(2,1)}, u32[]{:S(2)}) copy-start(bf16[384,1024]{1,0:T(8,128)(2,1)} %param.20) | copy-start | bytes 2359300
  178.7 10.1 %copy-start.9 = (f32[384,1024]{1,0:T(8,128)S(1)}, f32[384,1024]{1,0:T(8,128)}, u32[]{:S(2)}) copy-start(f32[384,1024]{1,0:T(8,128)} %copy-done.8) | copy-start | bytes 4718596
  178.7 10.1 %copy-start.29 = (bf16[1024,4096]{1,0:T(8,128)(2,1)S(1)}, bf16[1024,4096]{1,0:T(8,128)(2,1)}, u32[]{:S(2)}) copy-start(bf16[1024,4096]{1,0:T(8,128)(2,1)} %all-gather.7.cloned.1.call-done) | copy-start | bytes 25165828
  188.8 7.0 %copy-start.28 = (bf16[4096,1024]{1,0:T(8,128)(2,1)S(1)}, bf16[4096,1024]{1,0:T(8,128)(2,1)}, u32[]{:S(2)}) copy-start(bf16[4096,1024]{1,0:T(8,128)(2,1)} %all-gather.9.cloned.1.call-done) | copy-start | bytes 25165828
  188.8 6.9 %copy-start.32 = (bf16[384,1024]{1,0:T(8,128)(2,1)S(1)}, bf16[384,1024]{1,0:T(8,128)(2,1)}, u32[]{:S(2)}) copy-start(bf16[384,1024]{1,0:T(8,128)(2,1)} %param.20) | copy-start | bytes 2359300
  195.8 8.1 %copy-start.30 = (bf16[1024,1024]{1,0:T(8,128)(2,1)S(1)}, bf16[1024,1024]{1,0:T(8,128)(2,1)}, u32[]{:S(2)}) copy-start(bf16[1024,1024]{1,0:T(8,128)(2,1)} %all-gather.5.cloned.1.call-done) | copy-start | bytes 6291460
  205.9 18.9 %all-to-all-start.1 = ((bf16[8,384,128]{2,1,0:T(8,128)(2,1)}), bf16[8,384,128]{2,1,0:T(8,128)(2,1)}, u32[]{:S(2)}, u32[]{:S(2)}) async-start(bf16[8,384,128]{2,1,0:T(8,128)(2,1)} %bitcast.122), calls=%async_computation.1 | async-start | bytes 1572864 | tf_op jit(solution)/shard_map/all_to_all | solution.py:991
  211.5 184.7 %all-gather.11.cloned.1.call-start = ((), (), s32[]{:S(2)}) async-start(), calls=%async_computation.6 | async-start | bytes 7864320 | tf_op jit(solution)/shard_map/all_gather | solution.py:963
  285.6 2.9 copy-start.5
  289.2 33.4 %collective-permute-start = (bf16[1536,256]{1,0:T(8,128)(2,1)S(1)}, bf16[1536,256]{1,0:T(8,128)(2,1)S(1)}, u32[]{:S(2)}, u32[]{:S(2)}) collective-permute-start(bf16[1536,256]{1,0:T(8,128)(2,1)S(1)} %get-tuple-element.70), channel_id=1, source_target_pairs={{0,8},{1,9},{2,10},{3,11},{4,12},{5,13},{6,14},{7,15},{8,16},{9,17... | collective-permute-start | bytes 2359304 | tf_op jit(solution)/shard_map/ppermute | solution.py:30
  320.8 7.6 %copy-start.13 = (bf16[3072,128]{1,0:T(8,128)(2,1)S(1)}, bf16[3072,128]{1,0:T(8,128)(2,1)}, u32[]{:S(2)}) copy-start(bf16[3072,128]{1,0:T(8,128)(2,1)} %get-tuple-element.42) | copy-start | bytes 2359300
  320.8 7.1 %collective-permute-start.1 = (bf16[1536,256]{1,0:T(8,128)(2,1)S(1)}, bf16[1536,256]{1,0:T(8,128)(2,1)S(1)}, u32[]{:S(2)}, u32[]{:S(2)}) collective-permute-start(bf16[1536,256]{1,0:T(8,128)(2,1)S(1)} %get-tuple-element.71), channel_id=1, source_target_pairs={{8,0},{9,1},{10,2},{11,3},{12,4},{13,5},{14,6},{15,7},{16,8},{17,9... | collective-permute-start | bytes 2359304 | tf_op jit(solution)/shard_map/ppermute | solution.py:30
  330.1 55.5 %all-to-all-start.2 = ((bf16[8,384,384]{2,1,0:T(8,128)(2,1)}), bf16[8,384,384]{2,1,0:T(8,128)(2,1)}, u32[]{:S(2)}, u32[]{:S(2)}) async-start(bf16[8,384,384]{2,1,0:T(8,128)(2,1)} %bitcast.115), calls=%async_computation.2 | async-start | bytes 4718592 | tf_op jit(solution)/shard_map/all_to_all | solution.py:991
  334.8 3.9 copy-start.33
  334.8 3.9 copy-start.35
  338.6 7.0 %copy-start.10 = (f32[384,1024]{1,0:T(8,128)S(1)}, f32[384,1024]{1,0:T(8,128)}, u32[]{:S(2)}) copy-start(f32[384,1024]{1,0:T(8,128)} %copy-done.8) | copy-start | bytes 4718596
  338.6 7.0 %copy-start.34 = (bf16[384,4096]{1,0:T(8,128)(2,1)S(1)}, bf16[384,4096]{1,0:T(8,128)(2,1)}, u32[]{:S(2)}) copy-start(bf16[384,4096]{1,0:T(8,128)(2,1)} %get-tuple-element.106) | copy-start | bytes 9437188
  591.5 4.3 copy-start.7
  595.8 2.5 copy-start.12
  598.3 2.0 copy-start.14
  600.3 1.8 copy-start.11
Sparse Core Ops, SparseCore 0:
  9.6 36.6 all-gather.4
  47.8 73.1 all-gather.6
  122.5 56.1 all-gather.8
  213.5 70.4 all-gather.10

commit v4 on v3

v4 whole, which is shorter than its diff:
```python
import functools

import jax
import jax.numpy as jnp
from jax import lax
from jax.experimental import pallas as pl
from jax.experimental.pallas import tpu as pltpu
from jax.sharding import PartitionSpec as P

D = 1024
HEADS = 16
HEAD_DIM = 64
IMG = 1370

PAIR = 2 * HEAD_DIM
GROUP = HEADS // 2
BLOCK = 256
KEYS = 1536
SLOTS = 63

EPSILON = 1e-06
NEG_BIG = -1e30
NEG_EDGE = -1e29

NT = (((1,), (1,)), ((), ()))


def from_behind(block, axis, distance):
    devices = range(lax.axis_size(axis))
    route = [(i - distance, i) for i in devices if i - distance in devices]
    return lax.ppermute(block, axis, route)


def normalize(values):
    center = jnp.mean(values, axis=-1, keepdims=True)
    centered = values - center
    spread = jnp.mean(centered * centered, axis=-1, keepdims=True)
    scale = lax.rsqrt(spread + EPSILON)
    return centered * scale, scale


def norm_back(cotangent, unit, scale, gain):
    scaled = cotangent * gain
    along = jnp.mean(scaled, axis=-1, keepdims=True)
    across = jnp.mean(scaled * unit, axis=-1, keepdims=True)
    return scale * (scaled - along - unit * across)


def matmul(left, right):
    return jnp.dot(left, right, preferred_element_type=jnp.float32)


def fold_rows(values, op):
    return op(values.reshape(values.shape[0] // 8, 8, values.shape[1]), axis=0)


def lane_marks():
    lane = lax.broadcasted_iota(jnp.int32, (BLOCK, PAIR), 1)
    return lane // HEAD_DIM, lane % HEAD_DIM > 0


def asking(query, marks, half, usable):
    wanted = jnp.where((marks.astype(jnp.float32) > 0) & usable, 0.0, NEG_BIG).astype(jnp.bfloat16)
    return [jnp.where(half == h, query, wanted) for h in range(2)]


def attend_kernel(meta, q_ref, k_ref, v_ref, m_ref, o_ref, ot_ref, lse_ref, vt, k_aug, scores):
    rows_all = o_ref.shape[0]
    tiles = rows_all // BLOCK
    window = k_ref.shape[0]
    halo = (window - KEYS - rows_all) // 2
    half, usable = lane_marks()

    @pl.loop(0, window // BLOCK)
    def _(i):
        at = pl.ds(pl.multiple_of(i * BLOCK, BLOCK), BLOCK)
        vt[:, at] = v_ref[at, :].T
        for h in range(2):
            k_aug[h, at, :] = jnp.where(half == h, k_ref[at, :], m_ref[at, :])

    @pl.loop(0, tiles)
    def _(t):
        start = meta[2 * t]
        count = meta[2 * t + 1]
        rows = pl.ds(pl.multiple_of(t * BLOCK, BLOCK), BLOCK)
        spots = pl.ds(pl.multiple_of(halo + t * BLOCK, BLOCK), BLOCK)
        query = asking(q_ref[rows, :], m_ref[spots, :], half, usable)

        def score(i, tops):
            at = pl.ds(pl.multiple_of(start + i * KEYS, 128), KEYS)
            keep = pl.ds(pl.multiple_of(i * KEYS, KEYS), KEYS)
            new = []
            for h in range(2):
                part = lax.dot_general(
                    k_aug[h, at, :], query[h], NT, preferred_element_type=jnp.float32
                )
                scores[h, keep, :] = part
                new.append(jnp.maximum(tops[h], fold_rows(part, jnp.max)))
            return tuple(new)

        low = jnp.full((8, BLOCK), NEG_BIG, jnp.float32)
        tops = lax.fori_loop(0, count, score, (low, low))
        tops = [jnp.max(top, axis=0, keepdims=True) for top in tops]
        tops = [jnp.where(top < NEG_EDGE, 0.0, top) for top in tops]

        def mix(i, carry):
            at = pl.ds(pl.multiple_of(start + i * KEYS, 128), KEYS)
            keep = pl.ds(pl.multiple_of(i * KEYS, KEYS), KEYS)
            new = []
            for h in range(2):
                total, mixed = carry[h]
                weights = jnp.exp(scores[h, keep, :] - tops[h])
                total = total + fold_rows(weights, jnp.sum)
                mixed = mixed + matmul(
                    vt[h * HEAD_DIM : (h + 1) * HEAD_DIM, at], weights.astype(jnp.bfloat16)
                )
                new.append((total, mixed))
            return tuple(new)

        zero = (jnp.zeros((8, BLOCK), jnp.float32), jnp.zeros((HEAD_DIM, BLOCK), jnp.float32))
        done = lax.fori_loop(0, count, mix, (zero, zero))
        outs = []
        for h in range(2):
            total = jnp.sum(done[h][0], axis=0, keepdims=True)
            total = jnp.where(total > 0, total, 1.0)
            lse_ref[h : h + 1, rows] = tops[h] + jnp.log(total)
            outs.append(done[h][1] / total)
        out = jnp.concatenate(outs, axis=0)
        ot_ref[:, rows] = out
        o_ref[rows, :] = out.T.astype(jnp.bfloat16)


def attend(meta, query, keys, values, marks):
    rows = query.shape[0]
    window = keys.shape[0]
    deepest = (2 * IMG + 2 * BLOCK + KEYS) // KEYS * KEYS
    vmem = pl.BlockSpec(memory_space=pltpu.VMEM)
    return pl.pallas_call(
        attend_kernel,
        out_shape=(
            jax.ShapeDtypeStruct((rows, PAIR), jnp.bfloat16),
            jax.ShapeDtypeStruct((PAIR, rows), jnp.float32),
            jax.ShapeDtypeStruct((8, rows), jnp.float32),
        ),
        in_specs=[pl.BlockSpec(memory_space=pltpu.SMEM), vmem, vmem, vmem, vmem],
        out_specs=(vmem, vmem, vmem),
        scratch_shapes=[
            pltpu.VMEM((PAIR, window), jnp.bfloat16),
            pltpu.VMEM((2, window, PAIR), jnp.bfloat16),
            pltpu.VMEM((2, deepest, BLOCK), jnp.float32),
        ],
        cost_estimate=pl.CostEstimate(
            flops=4 * rows * 2 * IMG * PAIR, transcendentals=2 * rows * IMG, bytes_accessed=9 << 20
        ),
        name="attend",
    )(meta, query, keys, values, marks)


def attend_back_kernel(
    meta, q_ref, k_ref, v_ref, m_ref, g_ref, ot_ref, lse_ref, dq_ref, dk_out, dv_out, kt, k_aug, dk_ref, dv_ref
):
    rows_all = dq_ref.shape[0]
    tiles = rows_all // BLOCK
    window = k_ref.shape[0]
    halo = (window - KEYS - rows_all) // 2
    half, usable = lane_marks()

    @pl.loop(0, window // BLOCK)
    def _(i):
        at = pl.ds(pl.multiple_of(i * BLOCK, BLOCK), BLOCK)
        kt[:, at] = k_ref[at, :].T
        for h in range(2):
            k_aug[h, at, :] = jnp.where(half == h, k_ref[at, :], m_ref[at, :])
        dk_ref[at, :] = jnp.zeros((BLOCK, PAIR), jnp.float32)
        dv_ref[at, :] = jnp.zeros((BLOCK, PAIR), jnp.float32)

    @pl.loop(0, tiles)
    def _(t):
        start = meta[2 * t]
        count = meta[2 * t + 1]
        rows = pl.ds(pl.multiple_of(t * BLOCK, BLOCK), BLOCK)
        grad = g_ref[rows, :]
        blank = jnp.zeros_like(grad)
        spots = pl.ds(pl.multiple_of(halo + t * BLOCK, BLOCK), BLOCK)
        query = asking(q_ref[rows, :], m_ref[spots, :], half, usable)
        query_only = jnp.concatenate(
            [jnp.where(half == h, query[h], blank) for h in range(2)], axis=0
        )
        grads = [jnp.where(half == h, grad, blank) for h in range(2)]
        grads_both = jnp.concatenate(grads, axis=0)
        product = grad.astype(jnp.float32).T * ot_ref[:, rows]
        delta = [
            jnp.sum(product[h * HEAD_DIM : (h + 1) * HEAD_DIM], axis=0, keepdims=True)
            for h in range(2)
        ]
        lse = [lse_ref[h : h + 1, rows] for h in range(2)]

        def step(i, carry):
            at = pl.ds(pl.multiple_of(start + i * KEYS, 128), KEYS)
            value = v_ref[at, :]
            probs, slopes, new = [], [], []
            for h in range(2):
                part = lax.dot_general(
                    k_aug[h, at, :], query[h], NT, preferred_element_type=jnp.float32
                )
                weights = jnp.exp(part - lse[h])
                pull = lax.dot_general(value, grads[h], NT, preferred_element_type=jnp.float32)
                slope = (weights * (pull - delta[h])).astype(jnp.bfloat16)
                probs.append(weights.astype(jnp.bfloat16))
                slopes.append(slope)
                new.append(carry[h] + matmul(kt[h * HEAD_DIM : (h + 1) * HEAD_DIM, at], slope))
            dv_ref[at, :] += matmul(jnp.concatenate(probs, axis=1), grads_both)
            dk_ref[at, :] += matmul(jnp.concatenate(slopes, axis=1), query_only)
            return tuple(new)

        zero = jnp.zeros((HEAD_DIM, BLOCK), jnp.float32)
        done = lax.fori_loop(0, count, step, (zero, zero))
        dq = jnp.concatenate(done, axis=0) * (HEAD_DIM**-0.5)
        dq_ref[rows, :] = dq.T.astype(jnp.bfloat16)

    @pl.loop(0, window // BLOCK)
    def _(i):
        at = pl.ds(pl.multiple_of(i * BLOCK, BLOCK), BLOCK)
        dk_out[at, :] = dk_ref[at, :].astype(jnp.bfloat16)
        dv_out[at, :] = dv_ref[at, :].astype(jnp.bfloat16)


def attend_back(meta, query, keys, values, marks, grad, out_t, lse):
    rows = query.shape[0]
    window = keys.shape[0]
    vmem = pl.BlockSpec(memory_space=pltpu.VMEM)
    return pl.pallas_call(
        attend_back_kernel,
        out_shape=(
            jax.ShapeDtypeStruct((rows, PAIR), jnp.bfloat16),
            jax.ShapeDtypeStruct((window, PAIR), jnp.bfloat16),
            jax.ShapeDtypeStruct((window, PAIR), jnp.bfloat16),
        ),
        in_specs=[pl.BlockSpec(memory_space=pltpu.SMEM)] + [vmem] * 7,
        out_specs=(vmem, vmem, vmem),
        scratch_shapes=[
            pltpu.VMEM((PAIR, window), jnp.bfloat16),
            pltpu.VMEM((2, window, PAIR), jnp.bfloat16),
            pltpu.VMEM((window, PAIR), jnp.float32),
            pltpu.VMEM((window, PAIR), jnp.float32),
        ],
        cost_estimate=pl.CostEstimate(
            flops=10 * rows * 2 * IMG * PAIR, transcendentals=2 * rows * IMG, bytes_accessed=16 << 20
        ),
        name="attend_back",
    )(meta, query, keys, values, marks, grad, out_t, lse)


CHUNK = 64
LAG = 2
GIVE_AT = 3
TAKE_AT = 16
TAKE_BY = 1
LAST_TAKE = TAKE_AT + (GROUP - 1) * TAKE_BY
PAIR_BY = 2
WIDE_AT = 3
SHARED = (1, 2)
MESH = pl.DeviceIdType.MESH


def split_index(f, r):
    return f // 2, f % 2, (r % GROUP) // 2, r % 2


def mixed_bits(left, right):
    value = 0
    for weight in (4, 2, 1):
        value = value + weight * ((left // weight + right // weight) % 2)
    return value


def remote(source, target, send, recv, peer):
    return pltpu.make_async_remote_copy(
        src_ref=source,
        dst_ref=target,
        send_sem=send,
        recv_sem=recv,
        device_id=peer,
        device_id_type=MESH,
    )


def greet(peers, optional=()):
    barrier = pltpu.get_barrier_semaphore()
    expected = len(peers)
    for peer in peers:
        pl.semaphore_signal(barrier, inc=1, device_id=peer, device_id_type=MESH)
    for there, peer in optional:

        @pl.when(there)
        def _():
            pl.semaphore_signal(barrier, inc=1, device_id=peer, device_id_type=MESH)

        expected = expected + there.astype(jnp.int32)
    pl.semaphore_wait(barrier, expected)


def group_neighbours(f, r, replicas):
    spot = f * replicas + r
    after = lax.rem(spot + GROUP, 4 * replicas)
    before = lax.rem(spot + 3 * replicas + (replicas - GROUP), 4 * replicas)
    next_peer = (after // replicas, lax.rem(after, replicas))
    prev_peer = (before // replicas, lax.rem(before, replicas))
    return spot + GROUP < 4 * replicas, next_peer, spot >= GROUP, prev_peer


def qkv_kernel(
    replicas,
    tokens_ref,
    small_ref,
    codes_ref,
    w_ref,
    out_ref,
    up_ref,
    act_ref,
    q_out,
    k_out,
    v_out,
    codes_out,
    small_out,
    w_buf,
    out_full,
    up_full,
    stage,
    bias,
    own_sem,
    x_sem,
    y_sem,
    core_sem,
    relay_sem,
    block_sem,
    halo_sem,
    code_sem,
    edge_sem,
    small_sem,
    wide_sem,
):
    f = lax.axis_index("fsdp")
    r = lax.axis_index("rep")
    x, c, z, y = split_index(f, r)
    lo = r % GROUP
    base = r - lo
    tok_rows = tokens_ref.shape[0]
    rows = GROUP * tok_rows
    halo = (k_out.shape[0] - KEYS - rows) // 2
    half = GROUP // 2
    share = w_ref.shape[0]
    core_peer = (x * 2 + 1 - c, r)
    x_peer = ((1 - x) * 2 + c, r)
    y_peer = (f, base + z * 2 + 1 - y)
    fsdp_peers = [((f + step) % 4, r) for step in range(1, 4)]
    plane = [(f, base + (lo + step) % GROUP) for step in range(1, GROUP)]
    has_next, next_peer, has_prev, prev_peer = group_neighbours(f, r, replicas)
    greet(fsdp_peers + plane, [(has_next, next_peer), (has_prev, prev_peer)])

    def small_copy(step):
        return remote(
            small_ref,
            small_out.at[f],
            small_sem.at[0, step - 1],
            small_sem.at[1, step - 1],
            fsdp_peers[step - 1],
        )

    def lanes(part):
        return pl.ds(part * PAIR, PAIR)

    def shard_rows(owner):
        return pl.ds(pl.multiple_of(owner * share, share), share)

    def columns(part, pair):
        return w_ref.at[:, pl.ds(pl.multiple_of(part * D + pair * PAIR, PAIR), PAIR)]

    def slot(e, owner, part):
        return w_buf.at[e, shard_rows(owner), lanes(part)]

    across = (1 - x) * 2 + c
    wide_sets = 1 + up_ref.shape[0] // 64

    def wide_chunk(m, side, owner, mine):
        if m == 0:
            size, lead = out_ref.shape[0], 0
            own, full = out_ref, out_full
        else:
            size, lead = 64, 64 * (m - 1)
            own, full = up_ref, up_full
        if side is not None:
            size //= 2
            lead = lead + size * side
        if mine:
            return own.at[pl.ds(pl.multiple_of(lead, 32), size)]
        return full.at[pl.ds(pl.multiple_of(owner * own.shape[0] + lead, 32), size)]

    def wide_link(which, m, here, there, peer):
        return remote(here, there, wide_sem.at[0, which, m], wide_sem.at[1, which, m], peer)

    def wide_x(m):
        side = y if m in SHARED else None
        return wide_link(0, m, wide_chunk(m, side, f, True), wide_chunk(m, side, f, False), x_peer)

    def wide_y(m, side):
        here = wide_chunk(m, side, across, False)
        return wide_link(1, m, here, here, y_peer)

    def wide_core(m):
        return wide_link(
            2, m, wide_chunk(m, None, f, True), wide_chunk(m, None, f, False), core_peer
        )

    def wide_relay(m, side, which):
        here = wide_chunk(m, side, across, False)
        return wide_link(which, m, here, here, core_peer)

    def wide_pass(m):
        wide_x(m).wait_recv()
        if m in SHARED:
            wide_y(m, y).start()
        wide_relay(m, y if m in SHARED else None, 3).start()

    def wide_finish(m):
        wide_y(m, 1 - y).wait_recv()
        wide_relay(m, 1 - y, 4).start()

    def x_copy(e, part):
        pair = mixed_bits(lo, e)
        return remote(
            columns(part, pair), slot(e, f, part), x_sem.at[0, e, part], x_sem.at[1, e, part], x_peer
        )

    def y_copy(e, part):
        return remote(
            slot(e, across, part),
            slot(e + 1, across, part),
            y_sem.at[e, part],
            x_sem.at[1, e + 1, part],
            y_peer,
        )

    def arrival(e, part):
        here = slot(e, across, part)
        return remote(here, here, x_sem.at[0, e, part], x_sem.at[1, e, part], x_peer)

    def core_copy(e, part):
        pair = mixed_bits(lo, e)
        return remote(
            columns(part, pair),
            slot(e, f, part),
            core_sem.at[0, e, part],
            core_sem.at[1, e, part],
            core_peer,
        )

    def own_copy(e, part):
        pair = mixed_bits(lo, e)
        return pltpu.make_async_copy(columns(part, pair), slot(e, f, part), own_sem.at[e, part])

    def relay_copy(e, part):
        here = slot(e, across, part)
        return remote(here, here, relay_sem.at[0, e, part], relay_sem.at[1, e, part], core_peer)

    def code_copy(step):
        return remote(
            codes_ref,
            codes_out.at[half + lo],
            code_sem.at[0, step - 1],
            code_sem.at[1, step - 1],
            plane[step - 1],
        )

    order = (4, 5, 2, 3, 6, 7, 0, 1)
    for step in range(1, 4):
        small_copy(step).start()
    for e in order:
        for part in range(3):
            if e % 2 == 0:
                x_copy(e, part).start()
            core_copy(e, part).start()
            own_copy(e, part).start()
    for m in range(wide_sets):
        wide_x(m).start()
    for m in range(wide_sets):
        wide_core(m).start()
    for step in range(1, GROUP):
        code_copy(step).start()
    codes_out[half + lo] = codes_ref[...]

    k_out[2 * halo + rows :, :] = jnp.zeros((KEYS, PAIR), jnp.bfloat16)
    v_out[2 * halo + rows :, :] = jnp.zeros((KEYS, PAIR), jnp.bfloat16)
    for there, low, edge in ((has_prev, 0, 0), (has_next, halo + rows, half + GROUP)):

        @pl.when(jnp.logical_not(there))
        def _():
            k_out[low : low + halo, :] = jnp.zeros((halo, PAIR), jnp.bfloat16)
            v_out[low : low + halo, :] = jnp.zeros((halo, PAIR), jnp.bfloat16)
            codes_out[edge : edge + half] = jnp.zeros((half, 8, PAIR), jnp.float32)

    unit, scale = normalize(tokens_ref[...].astype(jnp.float32))
    small_out[f] = small_ref[...]
    for step in range(1, 4):
        small_copy(step).wait()
    table = [small_out[owner].astype(jnp.float32) for owner in range(4)]

    def vector(line):
        return jnp.concatenate(
            [table[owner][line + row : line + row + 1] for owner in range(4) for row in range(2)],
            axis=1,
        )

    for which, line in ((0, 4), (1, 6)):
        bias[which] = jnp.concatenate(
            [table[owner][line : line + 2] for owner in range(4)], axis=0
        )
    act_ref[...] = (unit * vector(0) + vector(2)).astype(jnp.bfloat16)

    def block_copy(e, part):
        pair = mixed_bits(lo, e)
        into = (q_out, k_out, v_out)[part]
        lead = lo * tok_rows + (0 if part == 0 else halo)
        return remote(
            stage.at[e, part],
            into.at[pl.ds(pl.multiple_of(lead, 128), tok_rows), :],
            block_sem.at[0, e, part],
            block_sem.at[1, e, part],
            (f, base + pair),
        )

    def nth(s):
        return jnp.where(s < 2, s + 4, jnp.where(s < 4, s, jnp.where(s < 6, s + 2, s - 6)))

    def halo_copy(source, part, forward):
        into = (k_out, v_out)[part]
        lead = source * tok_rows
        put = lead + halo - rows if forward else lead + halo + rows
        return remote(
            into.at[pl.ds(pl.multiple_of(halo + lead, 128), tok_rows), :],
            into.at[pl.ds(pl.multiple_of(put, 128), tok_rows), :],
            halo_sem.at[0, source, part],
            halo_sem.at[1, source, part],
            next_peer if forward else prev_peer,
        )

    def pass_on(source):
        for there, forward, fits in (
            (has_next, True, source >= half),
            (has_prev, False, source < half),
        ):

            @pl.when(there & fits)
            def _():
                for part in range(2):
                    halo_copy(source, part, forward).start()

    def pass_arrived(e):
        for part in range(3):
            block_copy(e, part).wait_recv()
        pass_on(mixed_bits(lo, e))

    @pl.loop(0, GROUP)
    def _(s):
        e = nth(s)
        pair = mixed_bits(lo, e)
        for part in range(3):
            arrival(e, part).wait_recv()
            relay_copy(e, part).start()

        @pl.when(e % 2 == 0)
        def _():
            for part in range(3):
                y_copy(e, part).start()

        for part in range(3):
            own_copy(e, part).wait()
            core_copy(e, part).wait_recv()
            relay_copy(e, part).wait_recv()
        result = matmul(act_ref[...], w_buf[e])
        outs = (
            (result[:, :PAIR] + bias[0, pl.ds(pair, 1), :]) * (HEAD_DIM**-0.5),
            result[:, PAIR : 2 * PAIR],
            result[:, 2 * PAIR :] + bias[1, pl.ds(pair, 1), :],
        )
        for part in range(3):
            stage[e, part] = outs[part].astype(jnp.bfloat16)

        @pl.when(e > 0)
        def _():
            for part in range(3):
                block_copy(e, part).start()

        @pl.when(e == 0)
        def _():
            for part, into in enumerate((q_out, k_out, v_out)):
                lead = lo * tok_rows + (0 if part == 0 else halo)
                into[pl.ds(pl.multiple_of(lead, 128), tok_rows), :] = outs[part].astype(
                    jnp.bfloat16
                )
            pass_on(lo)

        @pl.when(s >= GROUP // 2)
        def _():
            pass_arrived(nth(s - GROUP // 2))

        for m in range(wide_sets):
            if WIDE_AT + m < GROUP:
                pl.when(s == WIDE_AT + m)(functools.partial(wide_pass, m))


    for m in range(wide_sets):
        if WIDE_AT + m >= GROUP:
            wide_pass(m)
    pass_arrived(1)
    for m in SHARED:
        wide_finish(m)
    pass_arrived(6)
    pass_arrived(7)

    for step in range(1, GROUP):
        code_copy(step).wait()

    def edge_copy(forward):
        low, put = (GROUP, 0) if forward else (half, half + GROUP)
        return remote(
            codes_out.at[pl.ds(low, half)],
            codes_out.at[pl.ds(put, half)],
            edge_sem.at[0, int(forward)],
            edge_sem.at[1, int(forward)],
            next_peer if forward else prev_peer,
        )

    sides = ((has_next, has_prev, True), (has_prev, has_next, False))
    for there, here, forward in sides:

        @pl.when(there)
        def _():
            edge_copy(forward).start()

    for m in range(wide_sets):
        wide_x(m).wait_send()
        wide_core(m).wait()
        wide_relay(m, y if m in SHARED else None, 3).wait()
        if m in SHARED:
            wide_y(m, y).wait_send()
            wide_relay(m, 1 - y, 4).wait()
    for e in range(GROUP):
        for part in range(3):
            if e % 2 == 0:
                x_copy(e, part).wait_send()
                y_copy(e, part).wait_send()
            core_copy(e, part).wait_send()
            relay_copy(e, part).wait_send()
            if e > 0:
                block_copy(e, part).wait_send()
    for there, here, forward in sides:
        sources = range(half, GROUP) if forward else range(half)

        @pl.when(there)
        def _():
            edge_copy(forward).wait_send()
            for source in sources:
                for part in range(2):
                    halo_copy(source, part, forward).wait_send()

        @pl.when(here)
        def _():
            edge_copy(forward).wait_recv()
            for source in sources:
                for part in range(2):
                    halo_copy(source, part, forward).wait_recv()


def project(replicas, tokens, small, codes, w_qkv, w_out, w_up):
    tok_rows = tokens.shape[0]
    rows = GROUP * tok_rows
    window = 2 * rows + KEYS
    low = jnp.bfloat16
    vmem = pl.BlockSpec(memory_space=pltpu.VMEM)
    anywhere = pl.BlockSpec(memory_space=pl.ANY)
    dma = pltpu.SemaphoreType.DMA
    shape = jax.ShapeDtypeStruct
    return pl.pallas_call(
        functools.partial(qkv_kernel, replicas),
        out_shape=(
            shape((tok_rows, D), low),
            shape((rows, PAIR), low),
            shape((window, PAIR), low),
            shape((window, PAIR), low),
            shape((2 * GROUP, 8, PAIR), jnp.float32),
            shape((4,) + small.shape, low),
            shape((GROUP, D, 3 * PAIR), low),
            shape((4 * w_out.shape[0], w_out.shape[1]), low),
            shape((4 * w_up.shape[0], w_up.shape[1]), low),
        ),
        in_specs=[vmem] * 3 + [anywhere] * 3,
        out_specs=(vmem,) * 7 + (anywhere,) * 2,
        scratch_shapes=[
            pltpu.VMEM((GROUP, 3, tok_rows, PAIR), low),
            pltpu.VMEM((2, GROUP, PAIR), jnp.float32),
            dma((GROUP, 3)),
            dma((2, GROUP, 3)),
            dma((GROUP, 3)),
            dma((2, GROUP, 3)),
            dma((2, GROUP, 3)),
            dma((2, GROUP, 3)),
            dma((2, GROUP, 2)),
            dma((2, GROUP - 1)),
            dma((2, 2)),
            dma((2, 3)),
            dma((2, 5, 1 + w_up.shape[0] // 64)),
        ],
        compiler_params=pltpu.CompilerParams(
            collective_id=2, has_side_effects=True, vmem_limit_bytes=40 << 20
        ),
        cost_estimate=pl.CostEstimate(
            flops=2 * tok_rows * D * 3 * D, transcendentals=0, bytes_accessed=60 << 20
        ),
        name="project",
    )(tokens, small, codes, w_qkv, w_out, w_up)


def low(value):
    return value.astype(jnp.bfloat16)


def high(value):
    return value.astype(jnp.float32)


def span(start, size):
    return pl.ds(pl.multiple_of(start, size), size)


def make_pipe(place, own, source, load, from_core, from_x, from_y, from_near, from_far, final, sem):
    x, c, y, z_near, z_far = place["x"], place["c"], place["y"], place["z_near"], place["z_far"]
    depth = final.shape[1]
    half, mid, short = depth // 2, depth // 4, depth // 8
    my_half = span(y * half, half)
    my_mid = span(y * half + z_near * mid, mid)
    my_short = span(y * half + z_near * mid + z_far * short, short)

    def spot(side):
        return side if own.shape[1] == 2 else side * 2 + c

    def link(k, which, here, there, peer):
        return remote(here, there, sem.at[0, k, which], sem.at[1, k, which], place[peer])

    def core_copy(k, side):
        owner = side * 2 + 1 - c
        here = own.at[k, owner] if source is None else source(k, owner)
        return link(k, side, here, from_core.at[k, side], "core")

    def load_copy(k, side):
        return pltpu.make_async_copy(
            source(k, side * 2 + c), own.at[k, side], load.at[k, side]
        )

    def x_copy(k):
        return link(k, 2, own.at[k, spot(1 - x)], from_x.at[k], "x_peer")

    def y_copy(k):
        return link(k, 3, own.at[k, spot(x), span((1 - y) * half, half)], from_y.at[k], "y_peer")

    def near_copy(k):
        away = span(y * half + (1 - z_near) * mid, mid)
        return link(k, 4, own.at[k, spot(x), away], from_near.at[k], "near")

    def far_copy(k):
        away = span(y * half + z_near * mid + (1 - z_far) * short, short)
        return link(k, 5, own.at[k, spot(x), away], from_far.at[k], "far")

    def far_join_copy(k):
        here = final.at[k, my_short]
        return link(k, 6, here, here, "far")

    def near_join_copy(k):
        here = final.at[k, my_mid]
        return link(k, 7, here, here, "near")

    def y_join_copy(k):
        here = final.at[k, my_half]
        return link(k, 8, here, here, "y_peer")

    def enter(k):
        for side in range(2):
            core_copy(k, side).start()
            if source is not None:
                load_copy(k, side).start()

    def core_sum(k):
        for side in range(2):
            if source is not None:
                load_copy(k, side).wait()
            core_copy(k, side).wait()
            own[k, spot(side)] = low(high(own[k, spot(side)]) + high(from_core[k, side]))
        x_copy(k).start()

    def x_sum(k):
        x_copy(k).wait()
        own[k, spot(x)] = low(high(own[k, spot(x)]) + high(from_x[k]))
        y_copy(k).start()

    def y_sum(k):
        y_copy(k).wait()
        own[k, spot(x), my_half] = low(high(own[k, spot(x), my_half]) + high(from_y[k]))
        near_copy(k).start()

    def near_sum(k):
        near_copy(k).wait()
        own[k, spot(x), my_mid] = low(high(own[k, spot(x), my_mid]) + high(from_near[k]))
        far_copy(k).start()

    def far_sum(k):
        far_copy(k).wait()
        final[k, my_short] = low(high(own[k, spot(x), my_short]) + high(from_far[k]))
        far_join_copy(k).start()

    def far_join(k):
        far_join_copy(k).wait()
        near_join_copy(k).start()

    def near_join(k):
        near_join_copy(k).wait()
        y_join_copy(k).start()

    def y_join(k):
        y_join_copy(k).wait()

    return [enter, core_sum, x_sum, y_sum, near_sum, far_sum, far_join, near_join, y_join]


def run_pipe(steps, count, now):
    for where, step in enumerate(steps):
        k = now - where * LAG

        @pl.when((k >= 0) & (k < count))
        def _():
            step(k)


def pipe_shapes(count, held, depth, width, loads):
    low_type = jnp.bfloat16
    return [
        pltpu.VMEM((count, held, depth, width), low_type),
        pltpu.VMEM((count, 2, depth, width), low_type),
        pltpu.VMEM((count, depth, width), low_type),
        pltpu.VMEM((count, depth // 2, width), low_type),
        pltpu.VMEM((count, depth // 4, width), low_type),
        pltpu.VMEM((count, depth // 8, width), low_type),
        pltpu.VMEM((count, depth, width), low_type),
        pltpu.SemaphoreType.DMA((2, count, 9)),
    ] + ([pltpu.SemaphoreType.DMA((count, 2))] if loads else [])


def find_place():
    f = lax.axis_index("fsdp")
    r = lax.axis_index("rep")
    x, c, z, y = split_index(f, r)
    lo = r % GROUP
    base = r - lo
    z_near, z_far = z % 2, z // 2
    return {
        "f": f,
        "r": r,
        "x": x,
        "c": c,
        "y": y,
        "z_near": z_near,
        "z_far": z_far,
        "lo": lo,
        "base": base,
        "core": (x * 2 + 1 - c, r),
        "x_peer": ((1 - x) * 2 + c, r),
        "y_peer": (f, base + z * 2 + 1 - y),
        "near": (f, base + (z_far * 2 + 1 - z_near) * 2 + y),
        "far": (f, base + ((1 - z_far) * 2 + z_near) * 2 + y),
        "plane": [(f, base + (lo + step) % GROUP) for step in range(1, GROUP)],
    }


def erf(value):
    return lax.erf(value)


def middle_kernel(
    o_ref,
    tokens_ref,
    grad_ref,
    lines_ref,
    bias_ref,
    wo_ref,
    wo_own,
    wu_ref,
    wu_own,
    wd_own,
    half_ref,
    layer_out,
    residual_out,
    grad_out,
    small_out,
    up_final,
    rest,
    wo,
    wu,
    wd,
    attn,
    act,
    act_t,
    slim,
    x1,
    proj,
    branch,
    act_grad,
    pre,
    hidden,
    slope,
    pre_grad,
    attn_grad,
    proj_grad,
    sums,
    stage,
    own,
    from_core,
    from_x,
    from_y,
    from_near,
    from_far,
    final,
    sem,
    load_sem,
    attn_sem,
    grad_sem,
    down_x_sem,
    down_y_sem,
    down_core_sem,
    down_relay_sem,
    stage_sem,
):
    place = find_place()
    f, x, c, y, lo, base = (place[name] for name in ("f", "x", "c", "y", "lo", "base"))
    across = (1 - x) * 2 + c
    tok_rows = tokens_ref.shape[0]
    share = wo_own.shape[0]
    deep = wd_own.shape[0]
    sets = bias_ref.shape[0]
    tall = 128
    greet([place["core"], place["x_peer"]] + place["plane"])

    def shard_rows(owner, size):
        return span(owner * size, size)

    def attn_copy(e):
        pair = mixed_bits(lo, e)
        return remote(
            o_ref.at[span(pair * tok_rows, tok_rows), :],
            attn.at[:, span(lo * PAIR, PAIR)],
            attn_sem.at[0, e],
            attn_sem.at[1, e],
            (f, base + pair),
        )

    def grad_copy(e):
        pair = mixed_bits(lo, e)
        return remote(
            attn_grad.at[:, span(pair * PAIR, PAIR)],
            grad_out.at[span(lo * tok_rows, tok_rows), :],
            grad_sem.at[0, e],
            grad_sem.at[1, e],
            (f, base + pair),
        )

    def down_at(owner, i):
        return wd.at[span(owner * deep + i * tall, tall), :]

    def down_mine(i):
        return wd_own.at[span(i * tall, tall), :]

    def down_y(m, i):
        return remote(
            half_ref.at[m],
            down_at(across, i),
            down_y_sem.at[0, m],
            down_y_sem.at[1, m],
            place["y_peer"],
        )

    def down_core(i):
        return remote(
            down_mine(i),
            down_at(f, i),
            down_core_sem.at[0, i],
            down_core_sem.at[1, i],
            place["core"],
        )

    def down_relay(i, here):
        return remote(
            here,
            down_at(across, i),
            down_relay_sem.at[0, i],
            down_relay_sem.at[1, i],
            place["core"],
        )

    order = (4, 5, 6, 7, 2, 3, 1)
    for e in order:
        attn_copy(e).start()
    for m in range(sets // 2):
        i = 2 * m + y
        down_y(m, i).start()
        down_relay(i, half_ref.at[m]).start()
        pltpu.make_async_copy(half_ref.at[m], down_at(across, i), down_x_sem.at[m]).start()
    for i in range(sets):
        down_core(i).start()
    loads = [pltpu.make_async_copy(wd_own, wd.at[shard_rows(f, deep)], load_sem.at[0])]
    for owner in range(4):
        rows = pl.ds(owner * share, share)
        for which, (full, mine, into) in enumerate(((wo_ref, wo_own, wo), (wu_ref, wu_own, wu))):
            at = load_sem.at[1 + owner * 2 + which]
            loads.append((f == owner, full.at[rows], mine, into.at[rows], at))

    loads[0].start()
    for same, full, mine, into, at in loads[1:]:

        @pl.when(same)
        def _():
            pltpu.make_async_copy(mine, into, at).start()

        @pl.when(jnp.logical_not(same))
        def _():
            pltpu.make_async_copy(full, into, at).start()

    attn[:, span(lo * PAIR, PAIR)] = o_ref[span(lo * tok_rows, tok_rows), :]
    small_out[...] = jnp.zeros_like(small_out)
    sums[...] = jnp.zeros_like(sums)
    branch[...] = jnp.zeros_like(branch)
    act_grad[...] = jnp.zeros_like(act_grad)

    def line(which):
        return lines_ref[which : which + 1, :]

    def by_rows(step, body):
        @pl.loop(0, tok_rows // step)
        def _(b):
            body(span(b * step, step))

    def scale_grad(at):
        slim[at, :] = low(line(5) * high(grad_ref[at, :]))

    by_rows(64, scale_grad)

    for e in order:
        attn_copy(e).wait_recv()
    for same, full, mine, into, at in loads[1:]:
        pltpu.make_async_copy(full, into, at).wait()
    proj[...] = matmul(attn[...], wo[...])

    def enter_mlp(at):
        value = proj[at, :] + line(0)
        proj[at, :] = value
        value = high(tokens_ref[at, :]) + line(1) * value
        x1[at, :] = value
        unit, scale = normalize(value)
        act[at, :] = low(unit * line(2) + line(3))

    by_rows(64, enter_mlp)
    act_t[...] = act[...].T
    loads[0].wait()
    for m in range(sets // 2):
        i = 2 * m + y
        pltpu.make_async_copy(half_ref.at[m], down_at(across, i), down_x_sem.at[m]).wait()
        i = 2 * m + 1 - y
        down_y(m, i).wait_recv()
        down_relay(i, down_at(across, i)).start()
    steps = make_pipe(
        place, own, None, None, from_core, from_x, from_y, from_near, from_far, final, sem
    )
    finish_step = steps[-1]

    def settle(k):
        finish_step(k)
        i, side = k // 2, k % 2
        for owner in range(4):
            up_final[span(side * tall, tall), span(owner * deep + i * tall, tall)] = final[
                k, :, owner * tall : (owner + 1) * tall
            ]

    steps[-1] = settle
    count = 2 * sets

    def stage_copy(i, part):
        return pltpu.make_async_copy(
            stage.at[i % 2, part], rest.at[2 * i + part], stage_sem.at[i % 2, part]
        )

    @pl.loop(0, sets)
    def _(i):
        down_core(i).wait_recv()
        down_relay(i, down_at(across, i)).wait_recv()
        columns = [span(owner * deep + i * tall, tall) for owner in range(4)]
        w_in = jnp.concatenate([wu[:, at] for at in columns], axis=1)
        w_back = jnp.concatenate([wd[at, :] for at in columns], axis=0)
        pre[...] = matmul(act[...], w_in)

        def activate(at):
            value = pre[at, :] + bias_ref[pl.ds(i, 1), :]
            cdf = 0.5 * (1.0 + erf(value * (0.5**0.5)))
            hidden[at, :] = low(value * cdf)
            slope[at, :] = cdf + value * (jnp.exp(-0.5 * value * value) * 0.3989422804014327)

        by_rows(64, activate)
        pre[...] = lax.dot_general(slim[...], w_back, NT, preferred_element_type=jnp.float32)
        branch[...] += matmul(hidden[...], w_back)

        def descend(at):
            value = pre[at, :] * slope[at, :]
            pre[at, :] = value
            pre_grad[at, :] = low(value)

        by_rows(64, descend)
        total = jnp.sum(pre[...], axis=0, keepdims=True)
        for owner in range(4):
            small_out[owner, pl.ds(20 + i, 1), :] = total[:, owner * tall : (owner + 1) * tall]
        up_grad = low(matmul(act_t[...], pre_grad[...]))
        for side in range(2):
            for owner in range(4):
                top = owner * 2 * tall + side * tall
                own[2 * i + side, owner] = up_grad[top : top + tall]
        run_pipe(steps, count, 2 * i)
        act_grad[...] += lax.dot_general(
            pre_grad[...], w_in, NT, preferred_element_type=jnp.float32
        )

        @pl.when(i >= 2)
        def _():
            for part in range(2):
                stage_copy(i - 2, part).wait()

        down_grad = low(matmul(hidden[...].T, slim[...]))
        for part in range(2):
            for owner in range(4):
                stage[i % 2, part, owner] = down_grad[
                    owner * tall : (owner + 1) * tall, part * 4 * tall : (part + 1) * 4 * tall
                ]
            stage_copy(i, part).start()
        run_pipe(steps, count, 2 * i + 1)

    def leave_mlp(at):
        grad = high(grad_ref[at, :])
        out = branch[at, :] + line(4)
        layer_out[at, :] = low(x1[at, :] + line(5) * out)
        unit, scale = normalize(x1[at, :])
        back = act_grad[at, :]
        value = grad + norm_back(back, unit, scale, line(2))
        residual_out[at, :] = value
        scaled = line(1) * value
        proj_grad[at, :] = low(scaled)
        rows = (scaled, value * proj[at, :], back * unit, back, line(5) * grad, grad * out)
        for which, member in enumerate(rows):
            sums[which : which + 1, :] += jnp.sum(member, axis=0, keepdims=True)

    by_rows(64, leave_mlp)
    attn_grad[...] = low(
        lax.dot_general(proj_grad[...], wo[...], NT, preferred_element_type=jnp.float32)
    )
    for e in order:
        grad_copy(e).start()
    grad_out[span(lo * tok_rows, tok_rows), :] = attn_grad[:, span(lo * PAIR, PAIR)]
    for which in range(6):
        for owner in range(4):
            for row in range(2):
                at = (owner * 2 + row) * PAIR
                place_row = 8 + 2 * which + row
                small_out[owner, place_row : place_row + 1, :] = sums[
                    which : which + 1, at : at + PAIR
                ]
    for i in range(sets - 2, sets):
        for part in range(2):
            stage_copy(i, part).wait()

    def out_copy(side, part):
        return pltpu.make_async_copy(
            stage.at[side, part], rest.at[count + 2 * side + part], stage_sem.at[side, part]
        )

    act_t[...] = attn[...].T
    for owner in range(4):
        part_grad = low(matmul(act_t[owner * share : (owner + 1) * share, :], proj_grad[...]))
        for side in range(2):
            for part in range(2):
                stage[side, part, owner] = part_grad[
                    side * tall : (side + 1) * tall, part * 4 * tall : (part + 1) * 4 * tall
                ]
    for side in range(2):
        for part in range(2):
            out_copy(side, part).start()

    @pl.loop(count, count + LAG * (len(steps) - 1))
    def _(now):
        run_pipe(steps, count, now)

    for side in range(2):
        for part in range(2):
            out_copy(side, part).wait()
    for e in order:
        attn_copy(e).wait_send()
        grad_copy(e).wait()
    for m in range(sets // 2):
        down_y(m, 2 * m + y).wait_send()
    for i in range(sets):
        down_core(i).wait_send()
        down_relay(i, down_at(across, i)).wait_send()


def middle(mixed, tokens, out_grad, lines, bias, wide_out, w_out, wide_up, w_up, w_down, half):
    tok_rows = tokens.shape[0]
    rows = GROUP * tok_rows
    sets = bias.shape[0]
    count = 2 * sets
    wide = bias.shape[1]
    anywhere = pl.BlockSpec(memory_space=pl.ANY)
    vmem = pl.BlockSpec(memory_space=pltpu.VMEM)
    dma = pltpu.SemaphoreType.DMA
    shape = jax.ShapeDtypeStruct
    slight, full = jnp.bfloat16, jnp.float32
    return pl.pallas_call(
        middle_kernel,
        out_shape=(
            shape((tok_rows, D), slight),
            shape((tok_rows, D), full),
            shape((rows, PAIR), slight),
            shape((4, 28, PAIR), full),
            shape(w_up.shape, slight),
            shape((count + 4, 4, 128, wide), slight),
        ),
        in_specs=[vmem] * 5 + [anywhere] * 6,
        out_specs=(vmem,) * 5 + (anywhere,),
        scratch_shapes=[
            pltpu.VMEM(wide_out.shape, slight),
            pltpu.VMEM(wide_up.shape, slight),
            pltpu.VMEM((4 * w_down.shape[0], D), slight),
            pltpu.VMEM((tok_rows, D), slight),
            pltpu.VMEM((tok_rows, D), slight),
            pltpu.VMEM((D, tok_rows), slight),
            pltpu.VMEM((tok_rows, D), slight),
            pltpu.VMEM((tok_rows, D), full),
            pltpu.VMEM((tok_rows, D), full),
            pltpu.VMEM((tok_rows, D), full),
            pltpu.VMEM((tok_rows, D), full),
            pltpu.VMEM((tok_rows, wide), full),
            pltpu.VMEM((tok_rows, wide), slight),
            pltpu.VMEM((tok_rows, wide), full),
            pltpu.VMEM((tok_rows, wide), slight),
            pltpu.VMEM((tok_rows, D), slight),
            pltpu.VMEM((tok_rows, D), slight),
            pltpu.VMEM((8, D), full),
            pltpu.VMEM((2, 2, 4, 128, wide), slight),
        ]
        + pipe_shapes(count, 4, 128, wide, False)
        + [
            dma((9,)),
            dma((2, GROUP)),
            dma((2, GROUP)),
            dma((sets // 2,)),
            dma((2, sets // 2)),
            dma((2, sets)),
            dma((2, sets)),
            dma((2, 2)),
        ],
        compiler_params=pltpu.CompilerParams(
            collective_id=3, has_side_effects=True, vmem_limit_bytes=67043328
        ),
        cost_estimate=pl.CostEstimate(
            flops=40 * tok_rows * D * D, transcendentals=0, bytes_accessed=100 << 20
        ),
        name="middle",
    )(mixed, tokens, out_grad, lines, bias, wide_out, w_out, wide_up, w_up, w_down, half)


def finish_kernel(
    replicas,
    dq_ref,
    dk_ref,
    dv_ref,
    act_ref,
    pairs_ref,
    tokens_ref,
    residual_ref,
    gain_ref,
    small_ref,
    rest_ref,
    tokens_out,
    down_final,
    out_final,
    qkv_final,
    small_final,
    own,
    from_core,
    from_x,
    from_y,
    from_near,
    from_far,
    final,
    sem,
    load_sem,
    pair_own,
    pair_core,
    pair_x,
    pair_y,
    pair_near,
    pair_far,
    pair_final,
    pair_sem,
    halos,
    stage,
    arrived,
    w_buf,
    act_t,
    act_grad,
    small_work,
    small_own,
    small_core,
    small_x,
    small_all,
    halo_sem,
    block_sem,
    w_sem,
    small_sem,
):
    place = find_place()
    f, r, x, c, lo, base = (place[name] for name in ("f", "r", "x", "c", "lo", "base"))
    core_peer, x_peer, plane = place["core"], place["x_peer"], place["plane"]
    has_next, next_peer, has_prev, prev_peer = group_neighbours(f, r, replicas)
    total = own.shape[0]
    tok_rows = act_ref.shape[0]
    rows = GROUP * tok_rows
    halo = rows // 2
    half_group = GROUP // 2
    greet([core_peer, x_peer] + plane, [(has_next, next_peer), (has_prev, prev_peer)])

    def block(ref, source, lead=0):
        return ref.at[pl.ds(pl.multiple_of(lead + source * tok_rows, 128), tok_rows), :]

    def lanes(part):
        return pl.ds(part * PAIR, PAIR)

    def halo_copy(source, part, forward):
        ref = (dk_ref, dv_ref)[part]
        return remote(
            block(ref, source, halo + rows if forward else -halo),
            block(halos.at[part], source),
            halo_sem.at[0, source, part],
            halo_sem.at[1, source, part],
            next_peer if forward else prev_peer,
        )

    def block_copy(e, part):
        source = block(dq_ref, mixed_bits(lo, e)) if part == 0 else stage.at[e, part - 1]
        return remote(
            source,
            arrived.at[e, :, lanes(part)],
            block_sem.at[0, e, part],
            block_sem.at[1, e, part],
            (f, base + mixed_bits(lo, e)),
        )

    def nth(p):
        h = p // 2
        near = jnp.where(h == 0, 2, jnp.where(h == 1, 1, jnp.where(h == 2, 3, 0)))
        return jnp.where(p % 2 == 0, 4 + h, near)

    def w_copy(p):
        spot = p % 2
        return pltpu.make_async_copy(pairs_ref.at[nth(p)], w_buf.at[spot], w_sem.at[spot])

    for there, forward in ((has_next, True), (has_prev, False)):

        @pl.when(there)
        def _():
            for i in range(half_group):
                for part in range(2):
                    halo_copy(i if forward else i + half_group, part, forward).start()

        @pl.when(jnp.logical_not(there))
        def _():
            start = halo if forward else 0
            halos[:, start : start + halo, :] = jnp.zeros((2, halo, PAIR), jnp.bfloat16)

    order = (4, 2, 5, 1, 6, 3, 7)
    for e in order:
        block_copy(e, 0).start()
    arrived[0, :, lanes(0)] = dq_ref[pl.ds(pl.multiple_of(lo * tok_rows, 128), tok_rows), :]
    small_work[...] = small_ref[...]
    act_grad[...] = jnp.zeros_like(act_grad)
    act_t[...] = act_ref[...].T
    w_copy(0).start()

    def give(p):
        e = nth(p)
        source = mixed_bits(lo, e)
        for there, forward, fits in (
            (has_next, False, source >= half_group),
            (has_prev, True, source < half_group),
        ):

            @pl.when(there & fits)
            def _():
                for part in range(2):
                    halo_copy(source, part, forward).wait_recv()

        sums = []
        for part, ref in enumerate((dk_ref, dv_ref)):
            near = ref[pl.ds(pl.multiple_of(halo + source * tok_rows, 128), tok_rows), :]
            far = halos[part, pl.ds(pl.multiple_of(source * tok_rows, 128), tok_rows), :]
            sums.append(low(high(near) + high(far)))
            stage[e, part] = sums[part]

        @pl.when(e > 0)
        def _():
            for part in range(1, 3):
                block_copy(e, part).start()

        @pl.when(e == 0)
        def _():
            for part in range(1, 3):
                arrived[0, :, lanes(part)] = sums[part - 1]

    pair_steps = make_pipe(
        place,
        pair_own,
        None,
        None,
        pair_core,
        pair_x,
        pair_y,
        pair_near,
        pair_far,
        pair_final,
        pair_sem,
    )
    pair_enter = pair_steps.pop(0)

    def take(p):
        e = nth(p)
        j = mixed_bits(lo, e)

        @pl.when(p + 1 < GROUP)
        def _():
            w_copy(p + 1).start()

        @pl.when(e > 0)
        def _():
            for part in range(3):
                block_copy(e, part).wait_recv()

        w_copy(p).wait()
        grads = arrived[e]
        pair_own[j] = low(matmul(act_t[...], grads)).reshape(4, D // 4, 3 * PAIR)
        pair_enter(j)
        act_grad[...] += lax.dot_general(
            grads, w_buf[p % 2], NT, preferred_element_type=jnp.float32
        )
        sums = jnp.sum(high(grads), axis=0, keepdims=True)
        for line, part in ((4, 0), (6, 2)):
            small_work[j // 2, pl.ds(line + j % 2, 1), :] = sums[:, part * PAIR : (part + 1) * PAIR]

    def leave():
        unit, scale = normalize(high(tokens_ref[...]))
        grad = act_grad[...]
        back = norm_back(grad, unit, scale, gain_ref[...])
        tokens_out[...] = low(residual_ref[...] + back)
        for line, values in ((0, grad * unit), (2, grad)):
            sums = jnp.sum(values, axis=0, keepdims=True)
            for owner in range(4):
                for row in range(2):
                    at = (owner * 2 + row) * PAIR
                    small_work[owner, line + row : line + row + 1, :] = sums[:, at : at + PAIR]
        for side in range(2):
            small_enter(side).start()

    steps = make_pipe(
        place,
        own,
        lambda k, owner: rest_ref.at[k, owner],
        load_sem,
        from_core,
        from_x,
        from_y,
        from_near,
        from_far,
        final,
        sem,
    )
    finish_step = steps[-1]
    tall, wide = final.shape[1:]
    downs = down_final.shape[0] // tall * 2

    def settle(k):
        finish_step(k)

        @pl.when(k < downs)
        def _():
            down_final[span((k // 2) * tall, tall), span((k % 2) * wide, wide)] = final[k]

        @pl.when(k >= downs)
        def _():
            at = k - downs
            out_final[span((at // 2) * tall, tall), span((at % 2) * wide, wide)] = final[k]

    steps[-1] = settle

    def small_enter(side):
        return remote(
            small_work.at[side * 2 + 1 - c],
            small_core.at[side],
            small_sem.at[0, side],
            small_sem.at[1, side],
            core_peer,
        )

    small_cross = remote(
        small_own.at[1 - x], small_x, small_sem.at[0, 2], small_sem.at[1, 2], x_peer
    )

    def small_spread(step):
        return remote(
            small_own.at[2],
            small_all.at[step - 1],
            small_sem.at[0, 2 + step],
            small_sem.at[1, 2 + step],
            plane[step - 1],
        )

    def small_first():
        for side in range(2):
            small_enter(side).wait()
        for side in range(2):
            small_own[side] = small_work[side * 2 + c] + small_core[side]
        small_cross.start()

    def small_second():
        small_cross.wait()
        small_own[2] = small_own[x] + small_x[...]
        for step in range(1, GROUP):
            small_spread(step).start()

    def arrive(p):
        pair_steps[0](mixed_bits(lo, nth(p)))

    def cross(p):
        pair_steps[1](mixed_bits(lo, nth(p)))

    stop = max(total + LAG * (len(steps) - 1), LAST_TAKE + 5 + GROUP // PAIR_BY + LAG * 5)

    @pl.loop(0, stop)
    def _(now):
        @pl.when((now >= GIVE_AT) & (now < GIVE_AT + GROUP))
        def _():
            give(now - GIVE_AT)

        run_pipe(steps, total, now)

        for step, lag in ((take, 0), (arrive, 2), (cross, 4)):
            gone = now - TAKE_AT - lag

            @pl.when((gone >= 0) & (gone < TAKE_BY * GROUP) & (gone % TAKE_BY == 0))
            def _():
                step(gone // TAKE_BY)

        for event, at in (
            (leave, LAST_TAKE + 1),
            (small_first, LAST_TAKE + 5),
            (small_second, LAST_TAKE + 9),
        ):
            pl.when(now == at)(event)

        for where, step in enumerate(pair_steps[2:]):
            gone = now - LAST_TAKE - 5 - LAG * where

            @pl.when((gone >= 0) & (gone < GROUP // PAIR_BY))
            def _():
                for each in range(PAIR_BY):
                    step(PAIR_BY * gone + each)

    for step in range(1, GROUP):
        small_spread(step).wait()
    value = small_own[2]
    for step in range(1, GROUP):
        value = value + small_all[step - 1]
    small_final[...] = value
    for j in range(GROUP):
        for part in range(3):
            at = part * D + j * PAIR
            qkv_final[:, at : at + PAIR] = pair_final[j, :, part * PAIR : (part + 1) * PAIR]

    for e in order:
        for part in range(3):
            block_copy(e, part).wait_send()
    for there, forward in ((has_next, True), (has_prev, False)):

        @pl.when(there)
        def _():
            for i in range(half_group):
                for part in range(2):
                    halo_copy(i if forward else i + half_group, part, forward).wait_send()


def wrap_up(replicas, moved, act, pairs, tokens, residual, gain, small, rest, shapes):
    chunks = rest.shape[0]
    tok_rows = act.shape[0]
    tall = small.shape[1]
    anywhere = pl.BlockSpec(memory_space=pl.ANY)
    vmem = pl.BlockSpec(memory_space=pltpu.VMEM)
    dma = pltpu.SemaphoreType.DMA
    low = jnp.bfloat16
    shape = jax.ShapeDtypeStruct
    pair = 3 * PAIR
    return pl.pallas_call(
        functools.partial(finish_kernel, replicas),
        out_shape=(shape((tok_rows, D), low),)
        + tuple(shape(size, low) for size in shapes)
        + (shape((D // 4, 3 * D), low), shape((tall, PAIR), jnp.float32)),
        in_specs=[vmem] * 4 + [anywhere] + [vmem] * 4 + [anywhere],
        out_specs=(vmem,) * 5,
        scratch_shapes=pipe_shapes(chunks, 2, *rest.shape[2:], True)
        + pipe_shapes(GROUP, 4, D // 4, pair, False)
        + [
            pltpu.VMEM((2, GROUP * tok_rows, PAIR), low),
            pltpu.VMEM((GROUP, 2, tok_rows, PAIR), low),
            pltpu.VMEM((GROUP, tok_rows, pair), low),
            pltpu.VMEM((2, D, pair), low),
            pltpu.VMEM((D, tok_rows), low),
            pltpu.VMEM((tok_rows, D), jnp.float32),
            pltpu.VMEM((4, tall, PAIR), jnp.float32),
            pltpu.VMEM((3, tall, PAIR), jnp.float32),
            pltpu.VMEM((2, tall, PAIR), jnp.float32),
            pltpu.VMEM((tall, PAIR), jnp.float32),
            pltpu.VMEM((GROUP - 1, tall, PAIR), jnp.float32),
            dma((2, GROUP, 2)),
            dma((2, GROUP, 3)),
            dma((2,)),
            dma((2, GROUP + 2)),
        ],
        compiler_params=pltpu.CompilerParams(
            collective_id=1, has_side_effects=True, vmem_limit_bytes=67043328
        ),
        cost_estimate=pl.CostEstimate(
            flops=12 * tok_rows * D * D, transcendentals=0, bytes_accessed=200 << 20
        ),
        name="finish",
    )(*moved, act, pairs, tokens, residual, gain, small, rest)


def shards(
    tokens,
    out_grad,
    norm1_gain,
    norm1_bias,
    w_qkv,
    q_bias,
    v_bias,
    w_out,
    out_bias,
    attn_scale,
    norm2_gain,
    norm2_bias,
    w_up,
    up_bias,
    w_down,
    down_bias,
    mlp_scale,
    image_ids,
    pad_mask,
):
    both = ("fsdp", "rep")
    owners = lax.axis_size("fsdp")
    replicas = lax.axis_size("rep")
    tok_rows = tokens.shape[0]
    rows = GROUP * tok_rows
    groups = [list(range(g, g + GROUP)) for g in range(0, replicas, GROUP)]
    factor = HEAD_DIM ** (-0.5)

    small = (
        norm1_gain,
        norm1_bias,
        q_bias,
        v_bias,
        out_bias,
        attn_scale,
        norm2_gain,
        norm2_bias,
        down_bias,
        mlp_scale,
        up_bias,
    )
    sizes = [member.shape[0] for member in small]
    packed = jnp.concatenate(small + (jnp.zeros((-sum(sizes) % 2048,), jnp.bfloat16),))
    codes = jnp.where(pad_mask > 0, image_ids + 1, 0).astype(jnp.float32).reshape(-1, PAIR)
    code_rows = codes.shape[0]
    codes = jnp.concatenate([codes, jnp.zeros((8 - code_rows, PAIR), jnp.float32)], axis=0)
    act_one, query, key_window, value_window, codes, vectors, w_pairs, wide_out, wide_up = project(
        replicas, tokens, packed.reshape(-1, PAIR), codes, w_qkv, w_out, w_up
    )
    vectors = vectors.reshape(4, -1).astype(jnp.float32)
    parts = []
    place = 0
    for member in small:
        parts.append(vectors[:, place : place + member.shape[0]].reshape(-1))
        place += member.shape[0]
    (
        gain_first,
        shift_first,
        query_bias,
        value_bias,
        proj_bias,
        attn_gamma,
        gain_second,
        shift_second,
        final_bias,
        mlp_gamma,
        hidden_bias,
    ) = parts


    window = key_window.shape[0]
    halo = rows // 2
    seen = codes[:, :code_rows].reshape(-1).astype(jnp.int32)
    seen = jnp.concatenate([seen, jnp.zeros((KEYS,), jnp.int32)])
    spot = jnp.arange(window, dtype=jnp.int32)
    asked = seen[halo : halo + rows]
    tile_codes = asked.reshape(rows // BLOCK, BLOCK)
    first_code = jnp.min(jnp.where(tile_codes > 0, tile_codes, 1 << 30), axis=1)
    last_code = jnp.max(tile_codes, axis=1)
    begin = jnp.min(jnp.where(seen[None] == first_code[:, None], spot[None], window), axis=1)
    finish = jnp.max(jnp.where(seen[None] == last_code[:, None], spot[None] + 1, 0), axis=1)
    begin = begin // 128 * 128
    count = jnp.where(last_code > 0, (finish - begin + KEYS - 1) // KEYS, 0)
    meta = jnp.stack([begin, count], axis=1).reshape(-1)

    lane_slot = jnp.arange(PAIR, dtype=jnp.int32) % HEAD_DIM
    key_slot = jnp.where(seen > 0, 1 + (seen - 1) % SLOTS, 0)
    marks = (key_slot[:, None] == lane_slot[None]).astype(jnp.bfloat16)


    down_half = w_down.reshape(-1, 2, 128, D)
    down_half = lax.dynamic_index_in_dim(down_half, lax.axis_index("rep") % 2, 1, False)
    down_half, query = lax.optimization_barrier((down_half, query))
    down_half = lax.ppermute(down_half, "fsdp", [(f, (f + 2) % 4) for f in range(4)])
    attn_mine, attn_t, lse = attend(meta, query, key_window, value_window, marks)

    lines = jnp.stack(
        (proj_bias, attn_gamma, gain_second, shift_second, final_bias, mlp_gamma) + (gain_second,) * 2
    )
    wide_bias = hidden_bias.reshape(4, -1, PAIR).transpose(1, 0, 2).reshape(-1, 4 * PAIR)
    layer_out, residual_grad, grad_mine, packed, up_out, rest = middle(
        attn_mine,
        tokens,
        out_grad,
        lines,
        wide_bias,
        wide_out,
        w_out,
        wide_up,
        w_up,
        w_down,
        down_half,
    )
    dq, dk, dv = attend_back(
        meta, query, key_window, value_window, marks, grad_mine, attn_t, lse
    )
    tokens_grad, *grads, packed = wrap_up(
        replicas,
        (dq, dk, dv),
        act_one,
        w_pairs,
        tokens,
        residual_grad,
        gain_first.reshape(1, D),
        packed,
        rest,
        (w_down.shape, w_out.shape),
    )
    grads.insert(1, up_out)
    grads = [grad.astype(jnp.float32) for grad in grads]
    if replicas > GROUP:
        apart = [list(range(low, replicas, GROUP)) for low in range(GROUP)]
        grads = lax.psum(grads, "rep", axis_index_groups=apart)
        packed = lax.psum(packed, "rep", axis_index_groups=apart)
    packed = packed.reshape(-1)
    small_out = []
    place = 0
    for member in (norm1_gain, norm1_bias, q_bias, v_bias) + small[4:]:
        size = member.shape[0]
        small_out.append(packed[place : place + size])
        place += size

    down_out, up_out, out_out, qkv_out = grads
    return (
        layer_out,
        tokens_grad,
        small_out[0],
        small_out[1],
        qkv_out,
        small_out[2],
        small_out[3],
        out_out,
        small_out[4],
        small_out[5],
        small_out[6],
        small_out[7],
        up_out,
        small_out[10],
        down_out,
        small_out[8],
        small_out[9],
    )


def solution(mesh):
    spread = P(("fsdp", "rep"), None)
    line = P("fsdp")
    plane = P("fsdp", None)
    return jax.shard_map(
        shards,
        mesh=mesh,
        in_specs=(
            spread,
            spread,
            line,
            line,
            plane,
            line,
            line,
            plane,
            line,
            line,
            line,
            line,
            plane,
            line,
            plane,
            line,
            line,
            P(("fsdp", "rep")),
            P(("fsdp", "rep")),
        ),
        out_specs=(
            spread,
            spread,
            line,
            line,
            plane,
            line,
            line,
            plane,
            line,
            line,
            line,
            line,
            plane,
            line,
            plane,
            line,
            line,
        ),
        check_vma=False,
    )
```

time: 622 us -> 504 us (0.81); the launches traced: 610 us -> 503 us
  Pallas kernels: 349 us -> 461 us
  waiting for transfers between devices: 73.7 us -> 0.01 us
  matrix products: 72.6 us -> 0 us
  starting transfers between devices: 52.1 us -> 4.87 us
  between operations: 14.6 us -> 0.97 us
  local copies, waits for them, and re-layouts: 28.1 us -> 21.6 us
    pallas_call x1 -> x2, Pallas kernels: 177 us -> 302 us  [the longest x1 173 us: wrap_up(): pl.pallas_call(functools.partial(finish_kernel, replicas), out_shape=(sha...]
    dot_general x11 -> x0, matrix products: 72.6 us -> none  [the longest x4 25.7 us: matmul_nt(): jnp.einsum('te,de->td', left, right, preferred_element_type=jnp.float32)]
    all_to_all x3 -> x0, waiting for transfers between devices: 58.3 us -> none  [exchange(): lax.all_to_all(block, 'rep', split_axis=0, concat_axis=0, tiled=True, axi...]
    ppermute x2 -> x1, starting transfers between devices: 33 us -> 4.87 us  [shards(): lax.ppermute(down_half, 'fsdp', [(f, (f + 2) % 4) for f in range(4)])]
    pallas_call x1, Pallas kernels: 72 us -> 92.5 us  [project(): pl.pallas_call(functools.partial(qkv_kernel, replicas), out_shape=(shape(...]
    pallas_call x1, Pallas kernels: 60.8 us -> 41.1 us  [attend_back(): pl.pallas_call(attend_back_kernel, out_shape=(jax.ShapeDtypeStruct((rows,...]
    all_to_all x3 -> x0, starting transfers between devices: 18.9 us -> none  [exchange(): lax.all_to_all(block, 'rep', split_axis=0, concat_axis=0, tiled=True, axi...]
    pallas_call x1, Pallas kernels: 39.2 us -> 25.4 us  [attend(): pl.pallas_call(attend_kernel, out_shape=(jax.ShapeDtypeStruct((rows, PAIR...]
  transfers between devices with their start and end apart: 9 -> 1, of which waited for: 6 -> 0; matrix products, arithmetic and copies ran while one was open for 10% -> 2% of each run, Pallas kernels for 28% -> 5%
where the time goes in v4:
time: 504 us; the launch traced here: 503 us
  Pallas kernels  461 us (91%)
  local copies, waits for them, and re-layouts  21.6 us (4%)
  other arithmetic  15.1 us (3%)
    pallas_call x1, Pallas kernels, wrap_up(): pl.pallas_call(functools.partial(finish_kernel, replicas), out_shape=(sha...  173 us
    pallas_call x1, Pallas kernels, middle(): pl.pallas_call(middle_kernel, out_shape=(shape((tok_rows, D), slight), sh...  128 us
    pallas_call x1, Pallas kernels, project(): pl.pallas_call(functools.partial(qkv_kernel, replicas), out_shape=(shape(...  92.5 us
    pallas_call x1, Pallas kernels, attend_back(): pl.pallas_call(attend_back_kernel, out_shape=(jax.ShapeDtypeStruct((rows,...  41.1 us
    pallas_call x1, Pallas kernels, attend(): pl.pallas_call(attend_kernel, out_shape=(jax.ShapeDtypeStruct((rows, PAIR...  25.4 us
    unnamed x76, local copies, waits for them, and re-layouts  15.8 us
  transfers between devices with their start and end apart: 1, of which 0 were waited for; matrix products, arithmetic and copies ran while one was open for 2% of the time, Pallas kernels for 5%

profile of v4, /device:TPU:0, one launch (start us, length us, event | category | flops | bytes accessed | tf_op | source)
XLA Modules:
  0.0 503.1 jit_solution(17277506561328291791)
XLA Ops:
  0.7 0.0 copy-start.15
  0.7 0.0 copy-start.16
  0.7 0.0 copy-start.17
  0.7 0.0 copy-start.18
  0.7 0.0 copy-start.19
  0.7 0.0 copy-start.20
  0.7 0.0 copy-start.21
  0.7 0.0 copy-start.22
  0.8 0.0 copy-start
  0.8 0.0 copy-start.4
  0.8 0.8 convert_bitcast_fusion.1
  1.6 1.3 dynamic-slice_bitcast_fusion
  2.9 0.2 dynamic-update-slice
  3.2 0.0 copy-done.16
  3.2 0.2 dynamic-update-slice.1
  3.4 0.2 dynamic-update-slice.2
  3.6 0.2 dynamic-update-slice.3
  3.9 0.0 copy-done.19
  3.9 0.2 dynamic-update-slice.4
  4.1 0.2 dynamic-update-slice.5
  4.3 0.2 dynamic-update-slice.6
  4.5 0.0 copy-done.22
  4.5 0.2 dynamic-update-slice.7
  4.7 0.2 dynamic-update-slice.8
  5.0 0.2 dynamic-update-slice.9
  5.2 0.2 dynamic-update-slice.10
  5.4 0.2 dynamic-update-slice.11
  5.6 1.6 copy-done.2
  7.2 1.4 copy-done.3
  8.6 92.5 %project.1 = (bf16[384,1024]{1,0:T(8,128)(2,1)S(1)}, bf16[3072,128]{1,0:T(8,128)(2,1)S(1)}, bf16[7680,128]{1,0:T(8,128)(2,1)S(1)}, bf16[7680,128]{1,0:T(8,128)(2...) custom-call(bf16[384,1024]{1,0:T(8,128)(2,1)S(1)} %copy-done, ...), custom_call_target="tpu_custom_call" | custom-call | flops 2415919104 | bytes 62914560 | tf_op jit(solution)/shard_map/project/pallas_call | solution.py:684
  101.1 0.9 copy-done.1
  102.0 1.3 copy-done.5
  103.3 1.3 copy-done.6
  104.6 1.3 copy-done.7
  105.9 0.9 copy-done.8
  106.7 4.9 collective-permute-start
  111.6 0.2 fusion.5
  112.0 4.3 compare_convert_fusion.m_ref
  116.2 0.1 reduce_max.28
  116.3 0.6 copy.51
  116.9 0.6 copy.55
  117.6 0.1 reduce_max.29
  117.7 0.1 fusion.2
  117.8 0.4 select_reduce_fusion.1
  118.2 0.1 copy.40
  118.3 0.6 reshape.194.meta
  118.9 0.7 stack.9.lines_ref
  119.6 25.4 %attend.1 = (bf16[3072,128]{1,0:T(8,128)(2,1)}, f32[128,3072]{1,0:T(8,128)}, f32[8,3072]{1,0:T(8,128)}) custom-call(s32[24]{0:T(128)} %reshape.194.meta, bf16[3072,128]{1,0:T(8,128)(2,1)} %copy-done.8, bf16[7680,128]{1,0:T(8,128)(2,1)} %copy-done.6, bf16[7680,128]{1,0:T(8,128)(2,1)} %copy-done.7, bf16[7680,128]{1,0:T(8,128)(2,1)} %compare_convert_fusion.m_ref), custom_call_target="tpu_custom_call" | custom-call | flops 4309647360 | bytes 9437184 | tf_op jit(solution)/shard_map/attend/pallas_call | solution.py:138
  144.9 0.0 collective-permute-done.half_ref
  144.9 1.0 copy-done.25
  145.9 128.2 %middle.1 = (bf16[384,1024]{1,0:T(8,128)(2,1)}, f32[384,1024]{1,0:T(8,128)}, bf16[3072,128]{1,0:T(8,128)(2,1)}, f32[4,28,128]{2,1,0:T(8,128)}, bf16[256,4096]{1,...) custom-call(bf16[3072,128]{1,0:T(8,128)(2,1)} %get-tuple-element.50.o_ref, bf16[384,1024]{1,0:T(8,128)(2,1)} %tokens_ref.5, ...), custom_call_target="tpu_custom_call" | custom-call | flops 16106127360 | bytes 104857600 | tf_op jit(solution)/shard_map/middle/pallas_call | solution.py:1228
  274.1 41.1 %attend_back.1 = (bf16[3072,128]{1,0:T(8,128)(2,1)}, bf16[7680,128]{1,0:T(8,128)(2,1)}, bf16[7680,128]{1,0:T(8,128)(2,1)}) custom-call(s32[24]{0:T(128)} %reshape.194.meta, bf16[3072,128]{1,0:T(8,128)(2,1)} %copy-done.8, bf16[7680,128]{1,0:T(8,128)(2,1)} %copy-done.6, bf16[7680,128]{1,0:T(8,128)(2,1)} %copy-done.7, ...), custom_call_target="tpu_custom_call" | custom-call | flops 10774118400 | bytes 16777216 | tf_op jit(solution)/shard_map/attend_back/pallas_call | solution.py:232
  315.3 173.4 %finish.1 = (bf16[384,1024]{1,0:T(8,128)(2,1)}, bf16[1024,1024]{1,0:T(8,128)(2,1)}, bf16[256,1024]{1,0:T(8,128)(2,1)}, bf16[256,3072]{1,0:T(8,128)(2,1)}, f32[28,128]{1,0:T(8,128)}) custom-call(bf16[3072,128]{1,0:T(8,128)(2,1)} %get-tuple-element.59.dq_ref, bf16[7680,128]{1,0:T(8,128)(2,1)} %get-tuple-element.60.dk_ref, ...), custom_call_target="tpu_custom_call" | custom-call | flops 4831838208 | bytes 209715200 | tf_op jit(solution)/shard_map/finish/pallas_call | solution.py:1620
  488.7 0.0 copy-start.11
  488.7 1.4 slice_bitcast_fusion.8
  490.1 1.4 slice_bitcast_fusion.9
  491.5 2.1 convert_element_type.39
  493.6 2.0 convert_element_type.38
  495.7 0.2 copy-done.10
  495.9 2.5 convert_element_type.41
  498.3 2.5 convert_element_type.40
  500.8 0.9 copy.70
  501.7 0.5 copy-done.13
  502.3 0.9 copy.71
  (48 shorter events, 0.3 us)
Async XLA Ops:
  0.7 2.3 copy-start.15
  0.7 2.5 copy-start.16
  0.7 2.7 copy-start.17
  0.7 2.9 copy-start.18
  0.7 3.2 copy-start.19
  0.7 3.4 copy-start.20
  0.7 3.6 copy-start.21
  0.7 3.8 copy-start.22
  0.7 4.0 copy-start.23
  0.7 4.2 copy-start.24
  0.8 4.4 copy-start.14
  0.8 4.8 copy-start
  0.8 4.8 copy-start.4
  5.6 1.6 copy-start.2
  7.2 1.4 copy-start.3
  101.1 0.9 copy-start.1
  102.0 1.3 copy-start.5
  103.3 1.3 copy-start.6
  104.6 1.3 copy-start.7
  105.9 0.9 copy-start.8
  106.7 38.2 %collective-permute-start = (bf16[4,128,1024]{2,1,0:T(8,128)(2,1)S(1)}, bf16[4,128,1024]{2,1,0:T(8,128)(2,1)S(1)}, u32[]{:S(2)}, u32[]{:S(2)}) collective-permute-start(bf16[4,128,1024]{2,1,0:T(8,128)(2,1)S(1)} %dynamic-slice_bitcast_fusion), channel_id=1, source_target_pairs={{0,16},{8,24},{16,0},{24,8},{1,17},{9,25},{17,1},{25,9},{2,18},{10... | collective-permute-start | bytes 3145736 | tf_op jit(solution)/shard_map/ppermute | solution.py:1750
  144.9 1.0 copy-start.25
  488.7 5.0 copy-start.11
  493.6 2.2 copy-start.10
  495.8 2.5 copy-start.9
  498.3 2.5 copy-start.12
  500.8 1.4 copy-start.13

commit v5 on v4

--- a/solution.py
+++ b/solution.py
@@ -258,8 +258,6 @@
 TAKE_BY = 1
 LAST_TAKE = TAKE_AT + (GROUP - 1) * TAKE_BY
 PAIR_BY = 2
-WIDE_AT = 3
-SHARED = (1, 2)
 MESH = pl.DeviceIdType.MESH
 
 
@@ -323,9 +321,10 @@
     v_out,
     codes_out,
     small_out,
+    w_pairs,
+    out_across,
+    up_half,
     w_buf,
-    out_full,
-    up_full,
     stage,
     bias,
     own_sem,
@@ -339,6 +338,7 @@
     edge_sem,
     small_sem,
     wide_sem,
+    pair_sem,
 ):
     f = lax.axis_index("fsdp")
     r = lax.axis_index("rep")
@@ -380,51 +380,18 @@
         return w_buf.at[e, shard_rows(owner), lanes(part)]
 
     across = (1 - x) * 2 + c
-    wide_sets = 1 + up_ref.shape[0] // 64
-
-    def wide_chunk(m, side, owner, mine):
-        if m == 0:
-            size, lead = out_ref.shape[0], 0
-            own, full = out_ref, out_full
-        else:
-            size, lead = 64, 64 * (m - 1)
-            own, full = up_ref, up_full
-        if side is not None:
-            size //= 2
-            lead = lead + size * side
-        if mine:
-            return own.at[pl.ds(pl.multiple_of(lead, 32), size)]
-        return full.at[pl.ds(pl.multiple_of(owner * own.shape[0] + lead, 32), size)]
-
-    def wide_link(which, m, here, there, peer):
-        return remote(here, there, wide_sem.at[0, which, m], wide_sem.at[1, which, m], peer)
-
-    def wide_x(m):
-        side = y if m in SHARED else None
-        return wide_link(0, m, wide_chunk(m, side, f, True), wide_chunk(m, side, f, False), x_peer)
-
-    def wide_y(m, side):
-        here = wide_chunk(m, side, across, False)
-        return wide_link(1, m, here, here, y_peer)
-
-    def wide_core(m):
-        return wide_link(
-            2, m, wide_chunk(m, None, f, True), wide_chunk(m, None, f, False), core_peer
-        )
-
-    def wide_relay(m, side, which):
-        here = wide_chunk(m, side, across, False)
-        return wide_link(which, m, here, here, core_peer)
-
-    def wide_pass(m):
-        wide_x(m).wait_recv()
-        if m in SHARED:
-            wide_y(m, y).start()
-        wide_relay(m, y if m in SHARED else None, 3).start()
-
-    def wide_finish(m):
-        wide_y(m, 1 - y).wait_recv()
-        wide_relay(m, 1 - y, 4).start()
+    out_copy = remote(out_ref, out_across, wide_sem.at[0, 0], wide_sem.at[1, 0], x_peer)
+    up_tall = up_half.shape[0]
+    up_copy = remote(
+        up_ref.at[pl.ds(pl.multiple_of(y * up_tall, up_tall), up_tall)],
+        up_half,
+        wide_sem.at[0, 1],
+        wide_sem.at[1, 1],
+        x_peer,
+    )
+
+    def pair_store(e):
+        return pltpu.make_async_copy(w_buf.at[e], w_pairs.at[e], pair_sem.at[e])
 
     def x_copy(e, part):
         pair = mixed_bits(lo, e)
@@ -481,10 +448,8 @@
                 x_copy(e, part).start()
             core_copy(e, part).start()
             own_copy(e, part).start()
-    for m in range(wide_sets):
-        wide_x(m).start()
-    for m in range(wide_sets):
-        wide_core(m).start()
+    out_copy.start()
+    up_copy.start()
     for step in range(1, GROUP):
         code_copy(step).start()
     codes_out[half + lo] = codes_ref[...]
@@ -577,6 +542,7 @@
             own_copy(e, part).wait()
             core_copy(e, part).wait_recv()
             relay_copy(e, part).wait_recv()
+        pair_store(e).start()
         result = matmul(act_ref[...], w_buf[e])
         outs = (
             (result[:, :PAIR] + bias[0, pl.ds(pair, 1), :]) * (HEAD_DIM**-0.5),
@@ -604,19 +570,8 @@
         def _():
             pass_arrived(nth(s - GROUP // 2))
 
-        for m in range(wide_sets):
-            if WIDE_AT + m < GROUP:
-                pl.when(s == WIDE_AT + m)(functools.partial(wide_pass, m))
-
-
-    for m in range(wide_sets):
-        if WIDE_AT + m >= GROUP:
-            wide_pass(m)
-    pass_arrived(1)
-    for m in SHARED:
-        wide_finish(m)
-    pass_arrived(6)
-    pass_arrived(7)
+    for e in (1, 6, 7):
+        pass_arrived(e)
 
     for step in range(1, GROUP):
         code_copy(step).wait()
@@ -638,13 +593,10 @@
         def _():
             edge_copy(forward).start()
 
-    for m in range(wide_sets):
-        wide_x(m).wait_send()
-        wide_core(m).wait()
-        wide_relay(m, y if m in SHARED else None, 3).wait()
-        if m in SHARED:
-            wide_y(m, y).wait_send()
-            wide_relay(m, 1 - y, 4).wait()
+    out_copy.wait()
+    up_copy.wait()
+    for e in range(GROUP):
+        pair_store(e).wait()
     for e in range(GROUP):
         for part in range(3):
             if e % 2 == 0:
@@ -691,12 +643,13 @@
             shape((2 * GROUP, 8, PAIR), jnp.float32),
             shape((4,) + small.shape, low),
             shape((GROUP, D, 3 * PAIR), low),
-            shape((4 * w_out.shape[0], w_out.shape[1]), low),
-            shape((4 * w_up.shape[0], w_up.shape[1]), low),
+            shape(w_out.shape, low),
+            shape((w_up.shape[0] // 2, w_up.shape[1]), low),
         ),
         in_specs=[vmem] * 3 + [anywhere] * 3,
-        out_specs=(vmem,) * 7 + (anywhere,) * 2,
+        out_specs=(vmem,) * 6 + (anywhere,) * 3,
         scratch_shapes=[
+            pltpu.VMEM((GROUP, D, 3 * PAIR), low),
             pltpu.VMEM((GROUP, 3, tok_rows, PAIR), low),
             pltpu.VMEM((2, GROUP, PAIR), jnp.float32),
             dma((GROUP, 3)),
@@ -709,7 +662,8 @@
             dma((2, GROUP - 1)),
             dma((2, 2)),
             dma((2, 3)),
-            dma((2, 5, 1 + w_up.shape[0] // 64)),
+            dma((2, 2)),
+            dma((GROUP,)),
         ],
         compiler_params=pltpu.CompilerParams(
             collective_id=2, has_side_effects=True, vmem_limit_bytes=40 << 20
@@ -890,12 +844,13 @@
     grad_ref,
     lines_ref,
     bias_ref,
-    wo_ref,
     wo_own,
-    wu_ref,
+    wo_across,
     wu_own,
+    wu_half,
+    wu_other,
     wd_own,
-    half_ref,
+    wd_across,
     layer_out,
     residual_out,
     grad_out,
@@ -932,10 +887,7 @@
     load_sem,
     attn_sem,
     grad_sem,
-    down_x_sem,
-    down_y_sem,
-    down_core_sem,
-    down_relay_sem,
+    core_load_sem,
     stage_sem,
 ):
     place = find_place()
@@ -971,67 +923,36 @@
             (f, base + pair),
         )
 
-    def down_at(owner, i):
-        return wd.at[span(owner * deep + i * tall, tall), :]
-
-    def down_mine(i):
-        return wd_own.at[span(i * tall, tall), :]
-
-    def down_y(m, i):
+    share_half = share // 2
+    lead = across * share
+    moves = (
+        (wo_own, wo, f * share, share),
+        (wo_across, wo, lead, share),
+        (wu_own, wu, f * share, share),
+        (wu_half, wu, lead + y * share_half, share_half),
+        (wu_other, wu, lead + (1 - y) * share_half, share_half),
+        (wd_own, wd, f * deep, deep),
+        (wd_across, wd, across * deep, deep),
+    )
+
+    def local_copy(which):
+        source, into, top, size = moves[which]
+        target = into.at[pl.ds(pl.multiple_of(top, 128), size)]
+        return pltpu.make_async_copy(source, target, load_sem.at[which])
+
+    def core_copy(which):
+        source, into, top, size = moves[which]
+        target = into.at[pl.ds(pl.multiple_of(top, 128), size)]
         return remote(
-            half_ref.at[m],
-            down_at(across, i),
-            down_y_sem.at[0, m],
-            down_y_sem.at[1, m],
-            place["y_peer"],
-        )
-
-    def down_core(i):
-        return remote(
-            down_mine(i),
-            down_at(f, i),
-            down_core_sem.at[0, i],
-            down_core_sem.at[1, i],
-            place["core"],
-        )
-
-    def down_relay(i, here):
-        return remote(
-            here,
-            down_at(across, i),
-            down_relay_sem.at[0, i],
-            down_relay_sem.at[1, i],
-            place["core"],
+            source, target, core_load_sem.at[0, which], core_load_sem.at[1, which], place["core"]
         )
 
     order = (4, 5, 6, 7, 2, 3, 1)
     for e in order:
         attn_copy(e).start()
-    for m in range(sets // 2):
-        i = 2 * m + y
-        down_y(m, i).start()
-        down_relay(i, half_ref.at[m]).start()
-        pltpu.make_async_copy(half_ref.at[m], down_at(across, i), down_x_sem.at[m]).start()
-    for i in range(sets):
-        down_core(i).start()
-    loads = [pltpu.make_async_copy(wd_own, wd.at[shard_rows(f, deep)], load_sem.at[0])]
-    for owner in range(4):
-        rows = pl.ds(owner * share, share)
-        for which, (full, mine, into) in enumerate(((wo_ref, wo_own, wo), (wu_ref, wu_own, wu))):
-            at = load_sem.at[1 + owner * 2 + which]
-            loads.append((f == owner, full.at[rows], mine, into.at[rows], at))
-
-    loads[0].start()
-    for same, full, mine, into, at in loads[1:]:
-
-        @pl.when(same)
-        def _():
-            pltpu.make_async_copy(mine, into, at).start()
-
-        @pl.when(jnp.logical_not(same))
-        def _():
-            pltpu.make_async_copy(full, into, at).start()
-
+    for which in range(len(moves)):
+        core_copy(which).start()
+        local_copy(which).start()
     attn[:, span(lo * PAIR, PAIR)] = o_ref[span(lo * tok_rows, tok_rows), :]
     small_out[...] = jnp.zeros_like(small_out)
     sums[...] = jnp.zeros_like(sums)
@@ -1053,8 +974,9 @@
 
     for e in order:
         attn_copy(e).wait_recv()
-    for same, full, mine, into, at in loads[1:]:
-        pltpu.make_async_copy(full, into, at).wait()
+    for which in range(2):
+        local_copy(which).wait()
+        core_copy(which).wait_recv()
     proj[...] = matmul(attn[...], wo[...])
 
     def enter_mlp(at):
@@ -1067,13 +989,9 @@
 
     by_rows(64, enter_mlp)
     act_t[...] = act[...].T
-    loads[0].wait()
-    for m in range(sets // 2):
-        i = 2 * m + y
-        pltpu.make_async_copy(half_ref.at[m], down_at(across, i), down_x_sem.at[m]).wait()
-        i = 2 * m + 1 - y
-        down_y(m, i).wait_recv()
-        down_relay(i, down_at(across, i)).start()
+    for which in range(2, len(moves)):
+        local_copy(which).wait()
+        core_copy(which).wait_recv()
     steps = make_pipe(
         place, own, None, None, from_core, from_x, from_y, from_near, from_far, final, sem
     )
@@ -1097,8 +1015,6 @@
 
     @pl.loop(0, sets)
     def _(i):
-        down_core(i).wait_recv()
-        down_relay(i, down_at(across, i)).wait_recv()
         columns = [span(owner * deep + i * tall, tall) for owner in range(4)]
         w_in = jnp.concatenate([wu[:, at] for at in columns], axis=1)
         w_back = jnp.concatenate([wd[at, :] for at in columns], axis=0)
@@ -1207,14 +1123,12 @@
     for e in order:
         attn_copy(e).wait_send()
         grad_copy(e).wait()
-    for m in range(sets // 2):
-        down_y(m, 2 * m + y).wait_send()
-    for i in range(sets):
-        down_core(i).wait_send()
-        down_relay(i, down_at(across, i)).wait_send()
-
-
-def middle(mixed, tokens, out_grad, lines, bias, wide_out, w_out, wide_up, w_up, w_down, half):
+    for which in range(len(moves)):
+        core_copy(which).wait_send()
+
+
+def middle(mixed, tokens, out_grad, lines, bias, weights):
+    w_out, w_up, w_down = weights[0], weights[2], weights[5]
     tok_rows = tokens.shape[0]
     rows = GROUP * tok_rows
     sets = bias.shape[0]
@@ -1235,11 +1149,11 @@
             shape(w_up.shape, slight),
             shape((count + 4, 4, 128, wide), slight),
         ),
-        in_specs=[vmem] * 5 + [anywhere] * 6,
+        in_specs=[vmem] * 5 + [anywhere] * 7,
         out_specs=(vmem,) * 5 + (anywhere,),
         scratch_shapes=[
-            pltpu.VMEM(wide_out.shape, slight),
-            pltpu.VMEM(wide_up.shape, slight),
+            pltpu.VMEM((4 * w_out.shape[0], D), slight),
+            pltpu.VMEM((4 * w_up.shape[0], w_up.shape[1]), slight),
             pltpu.VMEM((4 * w_down.shape[0], D), slight),
             pltpu.VMEM((tok_rows, D), slight),
             pltpu.VMEM((tok_rows, D), slight),
@@ -1260,13 +1174,10 @@
         ]
         + pipe_shapes(count, 4, 128, wide, False)
         + [
-            dma((9,)),
+            dma((7,)),
             dma((2, GROUP)),
             dma((2, GROUP)),
-            dma((sets // 2,)),
-            dma((2, sets // 2)),
-            dma((2, sets)),
-            dma((2, sets)),
+            dma((2, 7)),
             dma((2, 2)),
         ],
         compiler_params=pltpu.CompilerParams(
@@ -1276,7 +1187,7 @@
             flops=40 * tok_rows * D * D, transcendentals=0, bytes_accessed=100 << 20
         ),
         name="middle",
-    )(mixed, tokens, out_grad, lines, bias, wide_out, w_out, wide_up, w_up, w_down, half)
+    )(mixed, tokens, out_grad, lines, bias, *weights)
 
 
 def finish_kernel(
@@ -1700,7 +1611,7 @@
     codes = jnp.where(pad_mask > 0, image_ids + 1, 0).astype(jnp.float32).reshape(-1, PAIR)
     code_rows = codes.shape[0]
     codes = jnp.concatenate([codes, jnp.zeros((8 - code_rows, PAIR), jnp.float32)], axis=0)
-    act_one, query, key_window, value_window, codes, vectors, w_pairs, wide_out, wide_up = project(
+    act_one, query, key_window, value_window, codes, vectors, w_pairs, out_across, up_half = project(
         replicas, tokens, packed.reshape(-1, PAIR), codes, w_qkv, w_out, w_up
     )
     vectors = vectors.reshape(4, -1).astype(jnp.float32)
@@ -1744,10 +1655,10 @@
     marks = (key_slot[:, None] == lane_slot[None]).astype(jnp.bfloat16)
 
 
-    down_half = w_down.reshape(-1, 2, 128, D)
-    down_half = lax.dynamic_index_in_dim(down_half, lax.axis_index("rep") % 2, 1, False)
-    down_half, query = lax.optimization_barrier((down_half, query))
-    down_half = lax.ppermute(down_half, "fsdp", [(f, (f + 2) % 4) for f in range(4)])
+    down_late, query = lax.optimization_barrier((w_down, query))
+    down_across = lax.ppermute(down_late, "fsdp", [(f, (f + 2) % 4) for f in range(4)])
+    swapped = [(r, r + 1 - 2 * (r % 2)) for r in range(replicas)]
+    up_other = lax.ppermute(up_half, "rep", swapped)
     attn_mine, attn_t, lse = attend(meta, query, key_window, value_window, marks)
 
     lines = jnp.stack(
@@ -1760,12 +1671,7 @@
         out_grad,
         lines,
         wide_bias,
-        wide_out,
-        w_out,
-        wide_up,
-        w_up,
-        w_down,
-        down_half,
+        (w_out, out_across, w_up, up_half, up_other, w_down, down_across),
     )
     dq, dk, dv = attend_back(
         meta, query, key_window, value_window, marks, grad_mine, attn_t, lse

time: 504 us -> 496 us (0.984)
  Pallas kernels: 461 us -> 430 us
  waiting for transfers between devices: 0.01 us -> 14.1 us
  local copies, waits for them, and re-layouts: 21.6 us -> 27.8 us
    pallas_call x1, Pallas kernels: 92.5 us -> 72.8 us  [project(): pl.pallas_call(functools.partial(qkv_kernel, replicas), out_shape=(shape(...]
    ppermute x1 -> x2, waiting for transfers between devices: 0.01 us -> 14.1 us  [the longest x1 14.1 us: shards(): lax.ppermute(down_late, 'fsdp', [(f, (f + 2) % 4) for f in range(4)])]
    pallas_call x1, Pallas kernels: 128 us -> 115 us  [middle(): pl.pallas_call(middle_kernel, out_shape=(shape((tok_rows, D), slight), sh...]
    pallas_call x1, Pallas kernels: 173 us -> 182 us  [wrap_up(): pl.pallas_call(functools.partial(finish_kernel, replicas), out_shape=(sha...]
    unnamed x76 -> x56, local copies, waits for them, and re-layouts: 15.8 us -> 23.3 us
  transfers between devices with their start and end apart: 1 -> 2, of which waited for: 0 -> 1; matrix products, arithmetic and copies ran while one was open for 2% -> 2% of each run, Pallas kernels for 5% -> 5%
where the time goes in v5:
time: 496 us; the launch traced here: 497 us
  Pallas kernels  430 us (87%)
  local copies, waits for them, and re-layouts  27.8 us (6%)
  other arithmetic  15 us (3%)
  waiting for transfers between devices  14.1 us (3%)
  starting transfers between devices  9.75 us (2%)
    pallas_call x1, Pallas kernels, wrap_up(): pl.pallas_call(functools.partial(finish_kernel, replicas), out_shape=(sha...  182 us
    pallas_call x1, Pallas kernels, middle(): pl.pallas_call(middle_kernel, out_shape=(shape((tok_rows, D), slight), sh...  115 us
    pallas_call x1, Pallas kernels, project(): pl.pallas_call(functools.partial(qkv_kernel, replicas), out_shape=(shape(...  72.8 us
    pallas_call x1, Pallas kernels, attend_back(): pl.pallas_call(attend_back_kernel, out_shape=(jax.ShapeDtypeStruct((rows,...  36.7 us
    unnamed x56, local copies, waits for them, and re-layouts  23.3 us
    pallas_call x1, Pallas kernels, attend(): pl.pallas_call(attend_kernel, out_shape=(jax.ShapeDtypeStruct((rows, PAIR...  22.9 us
    ppermute x1, waiting for transfers between devices, shards(): lax.ppermute(down_late, 'fsdp', [(f, (f + 2) % 4) for f in range(4)])  14.1 us
  transfers between devices with their start and end apart: 2, of which 1 were waited for; matrix products, arithmetic and copies ran while one was open for 2% of the time, Pallas kernels for 5%

profile of v5, /device:TPU:0, one launch (start us, length us, event | category | flops | bytes accessed | tf_op | source)
XLA Modules:
  0.0 497.4 jit_solution(6848760854698980344)
XLA Ops:
  0.7 0.7 convert_bitcast_fusion.1
  1.4 0.8 dynamic-update-slice
  2.2 0.8 dynamic-update-slice.1
  3.1 0.8 dynamic-update-slice.2
  3.9 0.8 dynamic-update-slice.3
  4.7 0.8 dynamic-update-slice.4
  5.6 0.8 dynamic-update-slice.5
  6.4 0.8 dynamic-update-slice.6
  7.2 0.8 dynamic-update-slice.7
  8.1 0.8 dynamic-update-slice.8
  8.9 0.8 dynamic-update-slice.9
  9.7 0.8 dynamic-update-slice.10
  10.6 0.2 dynamic-update-slice.11
  10.8 0.0 copy-start
  10.8 1.1 copy-done
  11.9 0.0 copy-start.2
  11.9 1.6 copy-done.2
  13.5 0.0 copy-start.3
  13.5 1.4 copy-done.3
  14.9 0.0 copy-start.5
  14.9 1.0 copy-done.5
  16.0 0.0 copy-start.15
  16.0 72.8 %project.1 = (bf16[384,1024]{1,0:T(8,128)(2,1)S(1)}, bf16[3072,128]{1,0:T(8,128)(2,1)S(1)}, bf16[7680,128]{1,0:T(8,128)(2,1)S(1)}, bf16[7680,128]{1,0:T(8,128)(2...) custom-call(bf16[384,1024]{1,0:T(8,128)(2,1)S(1)} %copy-done, ...), custom_call_target="tpu_custom_call" | custom-call | flops 2415919104 | bytes 62914560 | tf_op jit(solution)/shard_map/project/pallas_call | solution.py:636
  88.8 0.0 copy-start.1
  88.8 0.9 copy-done.1
  89.7 1.3 copy-done.6
  91.0 1.3 copy-done.7
  92.2 0.9 copy-done.8
  93.1 0.8 copy-done.9
  93.9 3.7 collective-permute-start
  97.7 0.0 copy-done.15
  97.7 6.0 %collective-permute-start.1 = (bf16[1024,1024]{1,0:T(8,128)(2,1)S(1)}, bf16[1024,1024]{1,0:T(8,128)(2,1)}, u32[]{:S(2)}, u32[]{:S(2)}) collective-permute-start(bf16[1024,1024]{1,0:T(8,128)(2,1)S(1)} %copy-done.15), channel_id=1, source_target_pairs={{0,16},{8,24},{16,0},{24,8},{1,17},{9,25},{17,1},{25,9},{2,18},{10... | collective-permute-start | bytes 6291464 | tf_op jit(solution)/shard_map/ppermute | solution.py:1659
  103.8 4.3 compare_convert_fusion.m_ref
  108.1 0.2 fusion.5
  108.3 0.1 reduce_max.28
  108.4 0.6 copy.47
  109.0 0.6 copy.51
  109.7 0.1 reduce_max.29
  109.8 0.1 fusion.2
  109.9 0.4 select_reduce_fusion.1
  110.3 0.1 copy.38
  110.4 0.6 reshape.191.meta
  111.0 0.7 stack.9.lines_ref
  111.7 22.9 %attend.1 = (bf16[3072,128]{1,0:T(8,128)(2,1)}, f32[128,3072]{1,0:T(8,128)}, f32[8,3072]{1,0:T(8,128)}) custom-call(s32[24]{0:T(128)} %reshape.191.meta, bf16[3072,128]{1,0:T(8,128)(2,1)} %copy-done.8, bf16[7680,128]{1,0:T(8,128)(2,1)} %copy-done.6, bf16[7680,128]{1,0:T(8,128)(2,1)} %copy-done.7, bf16[7680,128]{1,0:T(8,128)(2,1)} %compare_convert_fusion.m_ref), custom_call_target="tpu_custom_call" | custom-call | flops 4309647360 | bytes 9437184 | tf_op jit(solution)/shard_map/attend/pallas_call | solution.py:138
  134.6 0.0 copy-done.4
  134.6 0.0 collective-permute-done.wu_other
  134.6 14.1 %collective-permute-done.1.wd_across = bf16[1024,1024]{1,0:T(8,128)(2,1)} collective-permute-done((bf16[1024,1024]{1,0:T(8,128)(2,1)S(1)}, bf16[1024,1024]{1,0:T(8,128)(2,1)}, u32[]{:S(2)}, u32[]{:S(2)}) %collective-permute-start.1) | collective-permute-done | bytes 2097184 | tf_op jit(solution)/shard_map/ppermute | solution.py:1659
  148.7 115.5 %middle.1 = (bf16[384,1024]{1,0:T(8,128)(2,1)}, f32[384,1024]{1,0:T(8,128)}, bf16[3072,128]{1,0:T(8,128)(2,1)}, f32[4,28,128]{2,1,0:T(8,128)}, bf16[256,4096]{1,...) custom-call(bf16[3072,128]{1,0:T(8,128)(2,1)} %get-tuple-element.50.o_ref, bf16[384,1024]{1,0:T(8,128)(2,1)} %tokens_ref.5, ...), custom_call_target="tpu_custom_call" | custom-call | flops 16106127360 | bytes 104857600 | tf_op jit(solution)/shard_map/middle/pallas_call | solution.py:1142
  264.2 36.7 %attend_back.1 = (bf16[3072,128]{1,0:T(8,128)(2,1)}, bf16[7680,128]{1,0:T(8,128)(2,1)}, bf16[7680,128]{1,0:T(8,128)(2,1)}) custom-call(s32[24]{0:T(128)} %reshape.191.meta, bf16[3072,128]{1,0:T(8,128)(2,1)} %copy-done.8, bf16[7680,128]{1,0:T(8,128)(2,1)} %copy-done.6, bf16[7680,128]{1,0:T(8,128)(2,1)} %copy-done.7, ...), custom_call_target="tpu_custom_call" | custom-call | flops 10774118400 | bytes 16777216 | tf_op jit(solution)/shard_map/attend_back/pallas_call | solution.py:232
  300.9 182.0 %finish.1 = (bf16[384,1024]{1,0:T(8,128)(2,1)}, bf16[1024,1024]{1,0:T(8,128)(2,1)}, bf16[256,1024]{1,0:T(8,128)(2,1)}, bf16[256,3072]{1,0:T(8,128)(2,1)}, f32[28,128]{1,0:T(8,128)}) custom-call(bf16[3072,128]{1,0:T(8,128)(2,1)} %get-tuple-element.59.dq_ref, bf16[7680,128]{1,0:T(8,128)(2,1)} %get-tuple-element.60.dk_ref, ...), custom_call_target="tpu_custom_call" | custom-call | flops 4831838208 | bytes 209715200 | tf_op jit(solution)/shard_map/finish/pallas_call | solution.py:1531
  482.9 0.0 copy-start.12
  482.9 1.4 slice_bitcast_fusion.8
  484.4 1.4 slice_bitcast_fusion.9
  485.8 2.1 convert_element_type.39
  487.9 0.0 copy-done.12
  487.9 2.0 convert_element_type.38
  489.9 0.2 copy-done.11
  490.1 2.5 convert_element_type.41
  492.6 0.0 copy-done.10
  492.6 2.5 convert_element_type.40
  495.1 0.0 copy-done.13
  495.1 0.9 copy.66
  496.0 0.5 copy-done.14
  496.5 0.9 copy.67
  (29 shorter events, 0.2 us)
Async XLA Ops:
  10.8 1.1 copy-start
  11.9 1.6 copy-start.2
  13.5 1.4 copy-start.3
  14.9 1.0 copy-start.5
  16.0 81.7 %copy-start.15 = (bf16[1024,1024]{1,0:T(8,128)(2,1)S(1)}, bf16[1024,1024]{1,0:T(8,128)(2,1)}, u32[]{:S(2)}) copy-start(bf16[1024,1024]{1,0:T(8,128)(2,1)} %wd_own.1) | copy-start | bytes 6291460
  88.8 0.9 copy-start.1
  89.7 1.3 copy-start.6
  90.9 1.3 copy-start.7
  92.2 0.9 copy-start.8
  93.1 0.8 copy-start.9
  93.9 40.6 %copy-start.4 = (bf16[128,4096]{1,0:T(8,128)(2,1)}, bf16[128,4096]{1,0:T(8,128)(2,1)S(1)}, u32[]{:S(2)}) copy-start(bf16[128,4096]{1,0:T(8,128)(2,1)S(1)} %get-tuple-element.53.wu_half) | copy-start | bytes 3145732
  93.9 40.6 %collective-permute-start = (bf16[128,4096]{1,0:T(8,128)(2,1)S(1)}, bf16[128,4096]{1,0:T(8,128)(2,1)}, u32[]{:S(2)}, u32[]{:S(2)}) collective-permute-start(bf16[128,4096]{1,0:T(8,128)(2,1)S(1)} %get-tuple-element.53.wu_half), channel_id=1, source_target_pairs={{0,1},{1,0},{2,3},{3,2},{4,5},{5,4},{6,7},{7,6},{8,9},{9,8},{10,11... | collective-permute-start | bytes 3145736 | tf_op jit(solution)/shard_map/ppermute | solution.py:1661
  97.7 51.0 %collective-permute-start.1 = (bf16[1024,1024]{1,0:T(8,128)(2,1)S(1)}, bf16[1024,1024]{1,0:T(8,128)(2,1)}, u32[]{:S(2)}, u32[]{:S(2)}) collective-permute-start(bf16[1024,1024]{1,0:T(8,128)(2,1)S(1)} %copy-done.15), channel_id=1, source_target_pairs={{0,16},{8,24},{16,0},{24,8},{1,17},{9,25},{17,1},{25,9},{2,18},{10... | collective-permute-start | bytes 6291464 | tf_op jit(solution)/shard_map/ppermute | solution.py:1659
  482.9 5.0 %copy-start.12 = (bf16[256,3072]{1,0:T(8,128)(2,1)S(1)}, bf16[256,3072]{1,0:T(8,128)(2,1)}, u32[]{:S(2)}) copy-start(bf16[256,3072]{1,0:T(8,128)(2,1)} %get-tuple-element.69) | copy-start | bytes 4718596
  487.9 2.2 copy-start.11
  490.1 2.5 copy-start.10
  492.6 2.5 copy-start.13
  495.1 1.4 copy-start.14

commit v6 on v5

--- a/solution.py
+++ b/solution.py
@@ -253,11 +253,11 @@
 
 CHUNK = 64
 LAG = 2
-GIVE_AT = 3
-TAKE_AT = 16
+GIVE_AT = 4
+TAKE_AT = 20
 TAKE_BY = 1
 LAST_TAKE = TAKE_AT + (GROUP - 1) * TAKE_BY
-PAIR_BY = 2
+PAIR_BY = 1
 MESH = pl.DeviceIdType.MESH
 
 
@@ -468,19 +468,18 @@
     small_out[f] = small_ref[...]
     for step in range(1, 4):
         small_copy(step).wait()
-    table = [small_out[owner].astype(jnp.float32) for owner in range(4)]
+    table = [small_out[owner] for owner in range(4)]
 
     def vector(line):
-        return jnp.concatenate(
-            [table[owner][line + row : line + row + 1] for owner in range(4) for row in range(2)],
-            axis=1,
-        )
-
-    for which, line in ((0, 4), (1, 6)):
-        bias[which] = jnp.concatenate(
-            [table[owner][line : line + 2] for owner in range(4)], axis=0
-        )
-    act_ref[...] = (unit * vector(0) + vector(2)).astype(jnp.bfloat16)
+        return jnp.concatenate([rows_of[line : line + 1] for rows_of in table], axis=1)
+
+    for which, line in ((0, 2), (1, 3)):
+        for owner in range(4):
+            for side in range(2):
+                bias[which, 2 * owner + side : 2 * owner + side + 1, :] = table[owner][
+                    line : line + 1, side * PAIR : (side + 1) * PAIR
+                ]
+    act_ref[...] = (unit * vector(0) + vector(1)).astype(jnp.bfloat16)
 
     def block_copy(e, part):
         pair = mixed_bits(lo, e)
@@ -641,7 +640,7 @@
             shape((window, PAIR), low),
             shape((window, PAIR), low),
             shape((2 * GROUP, 8, PAIR), jnp.float32),
-            shape((4,) + small.shape, low),
+            shape((4,) + small.shape, jnp.float32),
             shape((GROUP, D, 3 * PAIR), low),
             shape(w_out.shape, low),
             shape((w_up.shape[0] // 2, w_up.shape[1]), low),
@@ -666,7 +665,7 @@
             dma((GROUP,)),
         ],
         compiler_params=pltpu.CompilerParams(
-            collective_id=2, has_side_effects=True, vmem_limit_bytes=40 << 20
+            collective_id=2, has_side_effects=True, vmem_limit_bytes=67043328
         ),
         cost_estimate=pl.CostEstimate(
             flops=2 * tok_rows * D * 3 * D, transcendentals=0, bytes_accessed=60 << 20
@@ -687,7 +686,9 @@
     return pl.ds(pl.multiple_of(start, size), size)
 
 
-def make_pipe(place, own, source, load, from_core, from_x, from_y, from_near, from_far, final, sem):
+def make_pipe(
+    place, own, source, load, from_core, from_x, from_y, from_near, from_far, final, sem, spread=True
+):
     x, c, y, z_near, z_far = place["x"], place["c"], place["y"], place["z_near"], place["z_far"]
     depth = final.shape[1]
     half, mid, short = depth // 2, depth // 4, depth // 8
@@ -777,7 +778,8 @@
 
     def near_join(k):
         near_join_copy(k).wait()
-        y_join_copy(k).start()
+        if spread:
+            y_join_copy(k).start()
 
     def y_join(k):
         y_join_copy(k).wait()
@@ -842,8 +844,7 @@
     o_ref,
     tokens_ref,
     grad_ref,
-    lines_ref,
-    bias_ref,
+    vectors_ref,
     wo_own,
     wo_across,
     wu_own,
@@ -874,6 +875,8 @@
     pre_grad,
     attn_grad,
     proj_grad,
+    lines_ref,
+    bias_ref,
     sums,
     stage,
     own,
@@ -888,6 +891,7 @@
     attn_sem,
     grad_sem,
     core_load_sem,
+    down_sem,
     stage_sem,
 ):
     place = find_place()
@@ -932,7 +936,19 @@
         (wu_half, wu, lead + y * share_half, share_half),
         (wu_other, wu, lead + (1 - y) * share_half, share_half),
         (wd_own, wd, f * deep, deep),
-        (wd_across, wd, across * deep, deep),
+        (wd_across.at[: deep // 2], wd, across * deep, deep // 2),
+        (wd_across.at[deep // 2 :], wd, across * deep + deep // 2 + y * (deep // 4), deep // 4),
+    )
+
+    def down_at(side):
+        top = across * deep + deep // 2 + side * (deep // 4)
+        return wd.at[span(top, deep // 4)]
+
+    y_copy = remote(
+        wd_across.at[deep // 2 :], down_at(y), down_sem.at[0], down_sem.at[1], place["y_peer"]
+    )
+    y_relay = remote(
+        down_at(1 - y), down_at(1 - y), down_sem.at[2], down_sem.at[3], place["core"]
     )
 
     def local_copy(which):
@@ -950,10 +966,21 @@
     order = (4, 5, 6, 7, 2, 3, 1)
     for e in order:
         attn_copy(e).start()
+    y_copy.start()
     for which in range(len(moves)):
         core_copy(which).start()
         local_copy(which).start()
     attn[:, span(lo * PAIR, PAIR)] = o_ref[span(lo * tok_rows, tok_rows), :]
+    table = [vectors_ref[owner] for owner in range(4)]
+    for which in range(6):
+        lines_ref[which : which + 1, :] = jnp.concatenate(
+            [rows_of[4 + which : 5 + which] for rows_of in table], axis=1
+        )
+    for i in range(sets):
+        at, side = 10 + i // 2, i % 2 * tall
+        bias_ref[i : i + 1, :] = jnp.concatenate(
+            [rows_of[at : at + 1, side : side + tall] for rows_of in table], axis=1
+        )
     small_out[...] = jnp.zeros_like(small_out)
     sums[...] = jnp.zeros_like(sums)
     branch[...] = jnp.zeros_like(branch)
@@ -989,23 +1016,28 @@
 
     by_rows(64, enter_mlp)
     act_t[...] = act[...].T
+    y_copy.wait_recv()
+    y_relay.start()
     for which in range(2, len(moves)):
         local_copy(which).wait()
         core_copy(which).wait_recv()
+    y_relay.wait_recv()
     steps = make_pipe(
-        place, own, None, None, from_core, from_x, from_y, from_near, from_far, final, sem
+        place, own, None, None, from_core, from_x, from_y, from_near, from_far, final, sem, False
     )
-    finish_step = steps[-1]
+    steps.pop()
+    wait_near = steps.pop()
 
     def settle(k):
-        finish_step(k)
+        wait_near(k)
         i, side = k // 2, k % 2
+        mine = span(y * (tall // 2), tall // 2)
         for owner in range(4):
-            up_final[span(side * tall, tall), span(owner * deep + i * tall, tall)] = final[
-                k, :, owner * tall : (owner + 1) * tall
+            up_final[side, :, span(owner * deep + i * tall, tall)] = final[
+                k, mine, owner * tall : (owner + 1) * tall
             ]
 
-    steps[-1] = settle
+    steps.append(settle)
     count = 2 * sets
 
     def stage_copy(i, part):
@@ -1123,17 +1155,19 @@
     for e in order:
         attn_copy(e).wait_send()
         grad_copy(e).wait()
+    y_copy.wait_send()
+    y_relay.wait_send()
     for which in range(len(moves)):
         core_copy(which).wait_send()
 
 
-def middle(mixed, tokens, out_grad, lines, bias, weights):
+def middle(mixed, tokens, out_grad, vectors, weights):
     w_out, w_up, w_down = weights[0], weights[2], weights[5]
     tok_rows = tokens.shape[0]
     rows = GROUP * tok_rows
-    sets = bias.shape[0]
+    sets = w_down.shape[0] // 128
     count = 2 * sets
-    wide = bias.shape[1]
+    wide = 4 * 128
     anywhere = pl.BlockSpec(memory_space=pl.ANY)
     vmem = pl.BlockSpec(memory_space=pltpu.VMEM)
     dma = pltpu.SemaphoreType.DMA
@@ -1146,10 +1180,10 @@
             shape((tok_rows, D), full),
             shape((rows, PAIR), slight),
             shape((4, 28, PAIR), full),
-            shape(w_up.shape, slight),
+            shape((2, w_up.shape[0] // 4, w_up.shape[1]), slight),
             shape((count + 4, 4, 128, wide), slight),
         ),
-        in_specs=[vmem] * 5 + [anywhere] * 7,
+        in_specs=[vmem] * 4 + [anywhere] * 7,
         out_specs=(vmem,) * 5 + (anywhere,),
         scratch_shapes=[
             pltpu.VMEM((4 * w_out.shape[0], D), slight),
@@ -1170,14 +1204,17 @@
             pltpu.VMEM((tok_rows, D), slight),
             pltpu.VMEM((tok_rows, D), slight),
             pltpu.VMEM((8, D), full),
+            pltpu.VMEM((sets, wide), full),
+            pltpu.VMEM((8, D), full),
             pltpu.VMEM((2, 2, 4, 128, wide), slight),
         ]
         + pipe_shapes(count, 4, 128, wide, False)
         + [
-            dma((7,)),
+            dma((8,)),
             dma((2, GROUP)),
             dma((2, GROUP)),
-            dma((2, 7)),
+            dma((2, 8)),
+            dma((4,)),
             dma((2, 2)),
         ],
         compiler_params=pltpu.CompilerParams(
@@ -1187,7 +1224,7 @@
             flops=40 * tok_rows * D * D, transcendentals=0, bytes_accessed=100 << 20
         ),
         name="middle",
-    )(mixed, tokens, out_grad, lines, bias, *weights)
+    )(mixed, tokens, out_grad, vectors, *weights)
 
 
 def finish_kernel(
@@ -1380,7 +1417,9 @@
     def leave():
         unit, scale = normalize(high(tokens_ref[...]))
         grad = act_grad[...]
-        back = norm_back(grad, unit, scale, gain_ref[...])
+        back = norm_back(
+            grad, unit, scale, jnp.concatenate([gain_ref[owner, :1] for owner in range(4)], axis=1)
+        )
         tokens_out[...] = low(residual_ref[...] + back)
         for line, values in ((0, grad * unit), (2, grad)):
             sums = jnp.sum(values, axis=0, keepdims=True)
@@ -1606,35 +1645,18 @@
         mlp_scale,
         up_bias,
     )
-    sizes = [member.shape[0] for member in small]
-    packed = jnp.concatenate(small + (jnp.zeros((-sum(sizes) % 2048,), jnp.bfloat16),))
+    share = norm1_gain.shape[0]
+    lines = list(small[:-1]) + list(up_bias.reshape(-1, share))
+    line_at = lax.broadcasted_iota(jnp.int32, (-(-len(lines) // 8) * 8, share), 0)
+    packed = jnp.zeros(line_at.shape, jnp.float32)
+    for at, member in enumerate(lines):
+        packed = jnp.where(line_at == at, member.astype(jnp.float32)[None], packed)
     codes = jnp.where(pad_mask > 0, image_ids + 1, 0).astype(jnp.float32).reshape(-1, PAIR)
     code_rows = codes.shape[0]
     codes = jnp.concatenate([codes, jnp.zeros((8 - code_rows, PAIR), jnp.float32)], axis=0)
     act_one, query, key_window, value_window, codes, vectors, w_pairs, out_across, up_half = project(
-        replicas, tokens, packed.reshape(-1, PAIR), codes, w_qkv, w_out, w_up
+        replicas, tokens, packed, codes, w_qkv, w_out, w_up
     )
-    vectors = vectors.reshape(4, -1).astype(jnp.float32)
-    parts = []
-    place = 0
-    for member in small:
-        parts.append(vectors[:, place : place + member.shape[0]].reshape(-1))
-        place += member.shape[0]
-    (
-        gain_first,
-        shift_first,
-        query_bias,
-        value_bias,
-        proj_bias,
-        attn_gamma,
-        gain_second,
-        shift_second,
-        final_bias,
-        mlp_gamma,
-        hidden_bias,
-    ) = parts
-
-
     window = key_window.shape[0]
     halo = rows // 2
     seen = codes[:, :code_rows].reshape(-1).astype(jnp.int32)
@@ -1655,24 +1677,25 @@
     marks = (key_slot[:, None] == lane_slot[None]).astype(jnp.bfloat16)
 
 
-    down_late, query = lax.optimization_barrier((w_down, query))
+    deep = w_down.shape[0]
+    side = deep // 2 + lax.axis_index("rep") % 2 * (deep // 4)
+    down_most = jnp.concatenate(
+        [w_down[: deep // 2], lax.dynamic_slice_in_dim(w_down, side, deep // 4, 0)], axis=0
+    )
+    down_late, query = lax.optimization_barrier((down_most, query))
     down_across = lax.ppermute(down_late, "fsdp", [(f, (f + 2) % 4) for f in range(4)])
     swapped = [(r, r + 1 - 2 * (r % 2)) for r in range(replicas)]
     up_other = lax.ppermute(up_half, "rep", swapped)
     attn_mine, attn_t, lse = attend(meta, query, key_window, value_window, marks)
 
-    lines = jnp.stack(
-        (proj_bias, attn_gamma, gain_second, shift_second, final_bias, mlp_gamma) + (gain_second,) * 2
-    )
-    wide_bias = hidden_bias.reshape(4, -1, PAIR).transpose(1, 0, 2).reshape(-1, 4 * PAIR)
     layer_out, residual_grad, grad_mine, packed, up_out, rest = middle(
         attn_mine,
         tokens,
         out_grad,
-        lines,
-        wide_bias,
+        vectors,
         (w_out, out_across, w_up, up_half, up_other, w_down, down_across),
     )
+    up_theirs = lax.ppermute(up_out, "rep", swapped)
     dq, dk, dv = attend_back(
         meta, query, key_window, value_window, marks, grad_mine, attn_t, lse
     )
@@ -1683,11 +1706,13 @@
         w_pairs,
         tokens,
         residual_grad,
-        gain_first.reshape(1, D),
+        vectors,
         packed,
         rest,
         (w_down.shape, w_out.shape),
     )
+    half = jnp.arange(2).reshape(1, 2, 1, 1) == lax.axis_index("rep") % 2
+    up_out = jnp.where(half, up_out[:, None], up_theirs[:, None]).reshape(w_up.shape)
     grads.insert(1, up_out)
     grads = [grad.astype(jnp.float32) for grad in grads]
     if replicas > GROUP:

time: 496 us -> 475 us (0.958)
  local copies, waits for them, and re-layouts: 27.8 us -> 7.01 us
  waiting for transfers between devices: 14.1 us -> 2.81 us
  other arithmetic: 15 us -> 24.5 us
    unnamed x56 -> x22, local copies, waits for them, and re-layouts: 23.3 us -> 3.64 us
    ppermute x1, waiting for transfers between devices: 14.1 us -> 2.8 us  [shards(): lax.ppermute(down_late, 'fsdp', [(f, (f + 2) % 4) for f in range(4)])]
    pallas_call x1, Pallas kernels: 182 us -> 171 us  [wrap_up(): pl.pallas_call(functools.partial(finish_kernel, replicas), out_shape=(sha...]
    convert_element_type x0 -> x11, other arithmetic: none -> 7.4 us  [shards(): packed = jnp.where(line_at == at, member.astype(jnp.float32)[None], packed)]
  transfers between devices with their start and end apart: 2 -> 3, of which waited for: 1 -> 1; matrix products, arithmetic and copies ran while one was open for 2% -> 3% of each run, Pallas kernels for 5% -> 49%
where the time goes in v6:
time: 475 us; the launch traced here: 474 us
  Pallas kernels  427 us (90%)
  other arithmetic  24.5 us (5%)
  starting transfers between devices  11.9 us (3%)
  local copies, waits for them, and re-layouts  7.01 us (1%)
    pallas_call x1, Pallas kernels, wrap_up(): pl.pallas_call(functools.partial(finish_kernel, replicas), out_shape=(sha...  171 us
    pallas_call x1, Pallas kernels, middle(): pl.pallas_call(middle_kernel, out_shape=(shape((tok_rows, D), slight), sh...  116 us
    pallas_call x1, Pallas kernels, project(): pl.pallas_call(functools.partial(qkv_kernel, replicas), out_shape=(shape(...  76.7 us
    pallas_call x1, Pallas kernels, attend_back(): pl.pallas_call(attend_back_kernel, out_shape=(jax.ShapeDtypeStruct((rows,...  38.9 us
    pallas_call x1, Pallas kernels, attend(): pl.pallas_call(attend_kernel, out_shape=(jax.ShapeDtypeStruct((rows, PAIR...  24.1 us
    convert_element_type x4, other arithmetic, shards(): grads = [grad.astype(jnp.float32) for grad in grads]  10.4 us
  transfers between devices with their start and end apart: 3, of which 1 were waited for; matrix products, arithmetic and copies ran while one was open for 3% of the time, Pallas kernels for 49%

profile of v6, /device:TPU:0, one launch (start us, length us, event | category | flops | bytes accessed | tf_op | source)
XLA Modules:
  0.0 474.4 jit_solution(561419069981879966)
XLA Ops:
  0.7 0.7 convert_element_type.89
  1.4 0.7 convert_element_type.88
  2.1 0.7 convert_element_type.87
  2.7 0.7 convert_element_type.86
  3.4 0.7 convert_element_type.85
  4.0 0.7 convert_element_type.84
  4.7 0.7 convert_element_type.83
  5.3 0.7 convert_element_type.82
  6.0 0.7 convert_element_type.81
  6.7 0.7 convert_element_type.80
  7.3 0.8 slice_convert_fusion.4
  8.1 0.7 convert_bitcast_fusion
  8.9 0.6 concatenate.9.codes_ref
  9.4 0.7 select_select_fusion.small_ref
  10.2 76.7 %project.1 = (bf16[384,1024]{1,0:T(8,128)(2,1)}, bf16[3072,128]{1,0:T(8,128)(2,1)}, bf16[7680,128]{1,0:T(8,128)(2,1)}, bf16[7680,128]{1,0:T(8,128)(2,1)}, f32[16...) custom-call(bf16[384,1024]{1,0:T(8,128)(2,1)} %tokens_ref.5, ...), custom_call_target="tpu_custom_call" | custom-call | flops 2415919104 | bytes 62914560 | tf_op jit(solution)/shard_map/project/pallas_call | solution.py:635
  86.9 0.0 copy-start
  86.9 0.0 slice-start
  86.9 3.8 collective-permute-start
  90.7 0.0 copy-done
  90.7 0.0 copy-start.6
  90.7 0.0 slice-done
  90.8 0.1 pad_maximum_fusion
  90.9 6.1 %collective-permute-start.1 = (bf16[768,1024]{1,0:T(8,128)(2,1)S(1)}, bf16[768,1024]{1,0:T(8,128)(2,1)S(1)}, u32[]{:S(2)}, u32[]{:S(2)}) collective-permute-start(bf16[768,1024]{1,0:T(8,128)(2,1)S(1)} %pad_maximum_fusion), channel_id=1, source_target_pairs={{0,16},{8,24},{16,0},{24,8},{1,17},{9,25},{17,1},{25,9},{2,18},{10... | collective-permute-start | bytes 4718600 | tf_op jit(solution)/shard_map/ppermute | solution.py:1686
  97.0 0.0 copy-done.6
  97.0 4.3 compare_convert_fusion.m_ref
  101.3 0.1 broadcast_in_dim.184
  101.4 0.7 broadcast_in_dim.185
  102.0 0.2 fusion.6
  102.3 0.1 reduce_max.28
  102.3 0.1 reduce_max.29
  102.5 0.1 fusion.3
  102.6 0.4 select_reduce_fusion.1
  103.0 0.1 copy.38
  103.1 0.6 reshape.224.meta
  103.7 24.1 %attend.1 = (bf16[3072,128]{1,0:T(8,128)(2,1)}, f32[128,3072]{1,0:T(8,128)}, f32[8,3072]{1,0:T(8,128)}) custom-call(s32[24]{0:T(128)} %reshape.224.meta, bf16[3072,128]{1,0:T(8,128)(2,1)} %get-tuple-element.47.q_ref, bf16[7680,128]{1,0:T(8,128)(2,1)} %get-tuple-element.48.k_ref, bf16[7680,128]{1,0:T(8,128)(2,1)} %get-tuple-element.49.v_ref, ...), custom_call_target="tpu_custom_call" | custom-call | flops 4309647360 | bytes 9437184 | tf_op jit(solution)/shard_map/attend/pallas_call | solution.py:138
  127.8 0.0 collective-permute-done.wu_other
  127.8 2.8 collective-permute-done.1.wd_across
  130.6 0.0 copy-start.9
  130.6 1.1 copy-done.9
  131.8 116.2 %middle.1 = (bf16[384,1024]{1,0:T(8,128)(2,1)}, f32[384,1024]{1,0:T(8,128)}, bf16[3072,128]{1,0:T(8,128)(2,1)}, f32[4,28,128]{2,1,0:T(8,128)}, bf16[2,64,4096]{2...) custom-call(bf16[3072,128]{1,0:T(8,128)(2,1)} %get-tuple-element.50.o_ref, bf16[384,1024]{1,0:T(8,128)(2,1)} %tokens_ref.5, ...), custom_call_target="tpu_custom_call" | custom-call | flops 16106127360 | bytes 104857600 | tf_op jit(solution)/shard_map/middle/pallas_call | solution.py:1176
  247.9 2.0 collective-permute-start.2
  250.0 38.9 %attend_back.1 = (bf16[3072,128]{1,0:T(8,128)(2,1)}, bf16[7680,128]{1,0:T(8,128)(2,1)}, bf16[7680,128]{1,0:T(8,128)(2,1)}) custom-call(s32[24]{0:T(128)} %reshape.224.meta, bf16[3072,128]{1,0:T(8,128)(2,1)} %get-tuple-element.47.q_ref, bf16[7680,128]{1,0:T(8,128)(2,1)} %get-tuple-element.48.k_ref, bf16[7680,128]{1,0:T(8,128)(2,1)} %get-tuple-element.49.v_ref, ...), custom_call_target="tpu_custom_call" | custom-call | flops 10774118400 | bytes 16777216 | tf_op jit(solution)/shard_map/attend_back/pallas_call | solution.py:232
  288.9 171.4 %finish.1 = (bf16[384,1024]{1,0:T(8,128)(2,1)}, bf16[1024,1024]{1,0:T(8,128)(2,1)}, bf16[256,1024]{1,0:T(8,128)(2,1)}, bf16[256,3072]{1,0:T(8,128)(2,1)}, f32[28,128]{1,0:T(8,128)}) custom-call(bf16[3072,128]{1,0:T(8,128)(2,1)} %get-tuple-element.59.dq_ref, bf16[7680,128]{1,0:T(8,128)(2,1)} %get-tuple-element.60.dk_ref, ...), custom_call_target="tpu_custom_call" | custom-call | flops 4831838208 | bytes 209715200 | tf_op jit(solution)/shard_map/finish/pallas_call | solution.py:1570
  460.3 0.0 copy-start.2
  460.3 2.2 convert_element_type.95
  462.6 0.0 copy-done.2
  462.6 0.0 copy-start.1
  462.6 2.0 convert_element_type.94
  464.6 0.2 copy-done.1
  464.8 0.0 copy-start.7
  464.8 0.0 copy-start.3
  464.8 0.0 copy-start.8
  464.8 2.5 convert_element_type.97
  467.3 0.0 copy-done.7
  467.3 0.6 slice_bitcast_fusion
  467.8 0.6 slice_bitcast_fusion.1
  468.5 0.0 collective-permute-done.2
  468.5 0.0 copy-done.3
  468.5 0.0 copy-done.8
  468.5 3.6 fusion
  472.1 0.0 copy-done.4
  472.1 0.9 copy.41
  473.0 0.5 copy-done.5
  473.5 0.9 copy.42
  (19 shorter events, 0.2 us)
Async XLA Ops:
  86.9 3.8 copy-start
  86.9 3.9 slice-start
  86.9 40.9 %collective-permute-start = (bf16[128,4096]{1,0:T(8,128)(2,1)}, bf16[128,4096]{1,0:T(8,128)(2,1)}, u32[]{:S(2)}, u32[]{:S(2)}) collective-permute-start(bf16[128,4096]{1,0:T(8,128)(2,1)} %get-tuple-element.53.wu_half), channel_id=1, source_target_pairs={{0,1},{1,0},{2,3},{3,2},{4,5},{5,4},{6,7},{7,6},{8,9},{9,8},{10,11... | collective-permute-start | bytes 3145736 | tf_op jit(solution)/shard_map/ppermute | solution.py:1688
  90.7 6.3 %copy-start.6 = (f32[16,8,128]{2,1,0:T(8,128)S(1)}, f32[16,8,128]{2,1,0:T(8,128)}, u32[]{:S(2)}) copy-start(f32[16,8,128]{2,1,0:T(8,128)} %get-tuple-element.45) | copy-start | bytes 196612
  90.9 39.8 %collective-permute-start.1 = (bf16[768,1024]{1,0:T(8,128)(2,1)S(1)}, bf16[768,1024]{1,0:T(8,128)(2,1)S(1)}, u32[]{:S(2)}, u32[]{:S(2)}) collective-permute-start(bf16[768,1024]{1,0:T(8,128)(2,1)S(1)} %pad_maximum_fusion), channel_id=1, source_target_pairs={{0,16},{8,24},{16,0},{24,8},{1,17},{9,25},{17,1},{25,9},{2,18},{10... | collective-permute-start | bytes 4718600 | tf_op jit(solution)/shard_map/ppermute | solution.py:1686
  130.6 1.1 copy-start.9
  247.9 220.5 %collective-permute-start.2 = (bf16[2,64,4096]{2,1,0:T(8,128)(2,1)}, bf16[2,64,4096]{2,1,0:T(8,128)(2,1)}, u32[]{:S(2)}, u32[]{:S(2)}) collective-permute-start(bf16[2,64,4096]{2,1,0:T(8,128)(2,1)} %get-tuple-element.71), channel_id=1, source_target_pairs={{0,1},{1,0},{2,3},{3,2},{4,5},{5,4},{6,7},{7,6},{8,9},{9,8},{10,11... | collective-permute-start | bytes 3145736 | tf_op jit(solution)/shard_map/ppermute | solution.py:1698
  460.3 2.3 copy-start.2
  462.6 2.2 copy-start.1
  464.8 2.5 copy-start.7
  464.8 3.7 copy-start.3
  464.8 3.7 copy-start.8
  468.5 3.7 copy-start.4
  472.1 1.4 copy-start.5

commit v7 on v6

--- a/solution.py
+++ b/solution.py
@@ -1648,12 +1648,13 @@
     share = norm1_gain.shape[0]
     lines = list(small[:-1]) + list(up_bias.reshape(-1, share))
     line_at = lax.broadcasted_iota(jnp.int32, (-(-len(lines) // 8) * 8, share), 0)
-    packed = jnp.zeros(line_at.shape, jnp.float32)
+    packed = jnp.zeros(line_at.shape, jnp.bfloat16)
     for at, member in enumerate(lines):
-        packed = jnp.where(line_at == at, member.astype(jnp.float32)[None], packed)
+        packed = jnp.where(line_at == at, member[None], packed)
+    packed = packed.astype(jnp.float32)
     codes = jnp.where(pad_mask > 0, image_ids + 1, 0).astype(jnp.float32).reshape(-1, PAIR)
     code_rows = codes.shape[0]
-    codes = jnp.concatenate([codes, jnp.zeros((8 - code_rows, PAIR), jnp.float32)], axis=0)
+    codes = jnp.pad(codes, ((0, 8 - code_rows), (0, 0)))
     act_one, query, key_window, value_window, codes, vectors, w_pairs, out_across, up_half = project(
         replicas, tokens, packed, codes, w_qkv, w_out, w_up
     )

time: 475 us -> 472 us (level)
  other arithmetic: 24.5 us -> 17.9 us
    convert_element_type x11 -> x1, other arithmetic: 7.4 us -> 1.5 us  [shards(): packed = packed.astype(jnp.float32)]
  transfers between devices with their start and end apart: 3 -> 3, of which waited for: 1 -> 1; matrix products, arithmetic and copies ran while one was open for 3% -> 3% of each run, Pallas kernels for 49% -> 51%
where the time goes in v7:
time: 472 us; the launch traced here: 471 us
  Pallas kernels  431 us (91%)
  other arithmetic  17.9 us (4%)
  starting transfers between devices  11.7 us (2%)
  local copies, waits for them, and re-layouts  7.85 us (2%)
    pallas_call x1, Pallas kernels, wrap_up(): pl.pallas_call(functools.partial(finish_kernel, replicas), out_shape=(sha...  171 us
    pallas_call x1, Pallas kernels, middle(): pl.pallas_call(middle_kernel, out_shape=(shape((tok_rows, D), slight), sh...  116 us
    pallas_call x1, Pallas kernels, project(): pl.pallas_call(functools.partial(qkv_kernel, replicas), out_shape=(shape(...  76.7 us
    pallas_call x1, Pallas kernels, attend_back(): pl.pallas_call(attend_back_kernel, out_shape=(jax.ShapeDtypeStruct((rows,...  41.1 us
    pallas_call x1, Pallas kernels, attend(): pl.pallas_call(attend_kernel, out_shape=(jax.ShapeDtypeStruct((rows, PAIR...  25.4 us
    convert_element_type x4, other arithmetic, shards(): grads = [grad.astype(jnp.float32) for grad in grads]  10.4 us
  transfers between devices with their start and end apart: 3, of which 1 were waited for; matrix products, arithmetic and copies ran while one was open for 3% of the time, Pallas kernels for 51%

profile of v7, /device:TPU:0, one launch (start us, length us, event | category | flops | bytes accessed | tf_op | source)
XLA Modules:
  0.0 470.8 jit_solution(1407391875713638302)
XLA Ops:
  0.7 0.8 fusion.7
  1.6 0.7 convert_bitcast_fusion
  2.3 0.6 pad.5.codes_ref
  2.9 1.5 select_convert_fusion.small_ref
  4.4 76.7 %project.1 = (bf16[384,1024]{1,0:T(8,128)(2,1)}, bf16[3072,128]{1,0:T(8,128)(2,1)}, bf16[7680,128]{1,0:T(8,128)(2,1)}, bf16[7680,128]{1,0:T(8,128)(2,1)}, f32[16...) custom-call(bf16[384,1024]{1,0:T(8,128)(2,1)} %tokens_ref.5, ...), custom_call_target="tpu_custom_call" | custom-call | flops 2415919104 | bytes 62914560 | tf_op jit(solution)/shard_map/project/pallas_call | solution.py:635
  81.1 0.0 copy-start
  81.1 0.0 slice-start
  81.1 3.8 collective-permute-start
  84.9 0.0 copy-done
  84.9 0.0 copy-start.6
  85.0 0.0 slice-done
  85.0 0.1 pad_maximum_fusion
  85.1 6.1 %collective-permute-start.1 = (bf16[768,1024]{1,0:T(8,128)(2,1)S(1)}, bf16[768,1024]{1,0:T(8,128)(2,1)S(1)}, u32[]{:S(2)}, u32[]{:S(2)}) collective-permute-start(bf16[768,1024]{1,0:T(8,128)(2,1)S(1)} %pad_maximum_fusion), channel_id=1, source_target_pairs={{0,16},{8,24},{16,0},{24,8},{1,17},{9,25},{17,1},{25,9},{2,18},{10... | collective-permute-start | bytes 4718600 | tf_op jit(solution)/shard_map/ppermute | solution.py:1687
  91.2 0.0 copy-done.6
  91.3 4.3 compare_convert_fusion.m_ref
  95.5 0.1 broadcast_in_dim.179
  95.6 0.7 broadcast_in_dim.180
  96.3 0.2 fusion.6
  96.5 0.1 reduce_max.28
  96.6 0.1 reduce_max.29
  96.7 0.1 fusion.3
  96.8 0.4 select_reduce_fusion.1
  97.2 0.1 copy.38
  97.3 0.6 reshape.212.meta
  97.9 25.4 %attend.1 = (bf16[3072,128]{1,0:T(8,128)(2,1)}, f32[128,3072]{1,0:T(8,128)}, f32[8,3072]{1,0:T(8,128)}) custom-call(s32[24]{0:T(128)} %reshape.212.meta, bf16[3072,128]{1,0:T(8,128)(2,1)} %get-tuple-element.47.q_ref, bf16[7680,128]{1,0:T(8,128)(2,1)} %get-tuple-element.48.k_ref, bf16[7680,128]{1,0:T(8,128)(2,1)} %get-tuple-element.49.v_ref, ...), custom_call_target="tpu_custom_call" | custom-call | flops 4309647360 | bytes 9437184 | tf_op jit(solution)/shard_map/attend/pallas_call | solution.py:138
  123.3 0.0 collective-permute-done.wu_other
  123.3 1.5 collective-permute-done.1.wd_across
  124.9 0.0 copy-start.9
  124.9 1.1 copy-done.9
  126.0 116.3 %middle.1 = (bf16[384,1024]{1,0:T(8,128)(2,1)}, f32[384,1024]{1,0:T(8,128)}, bf16[3072,128]{1,0:T(8,128)(2,1)}, f32[4,28,128]{2,1,0:T(8,128)}, bf16[2,64,4096]{2...) custom-call(bf16[3072,128]{1,0:T(8,128)(2,1)} %get-tuple-element.50.o_ref, bf16[384,1024]{1,0:T(8,128)(2,1)} %tokens_ref.5, ...), custom_call_target="tpu_custom_call" | custom-call | flops 16106127360 | bytes 104857600 | tf_op jit(solution)/shard_map/middle/pallas_call | solution.py:1176
  242.3 1.8 collective-permute-start.2
  244.1 41.1 %attend_back.1 = (bf16[3072,128]{1,0:T(8,128)(2,1)}, bf16[7680,128]{1,0:T(8,128)(2,1)}, bf16[7680,128]{1,0:T(8,128)(2,1)}) custom-call(s32[24]{0:T(128)} %reshape.212.meta, bf16[3072,128]{1,0:T(8,128)(2,1)} %get-tuple-element.47.q_ref, bf16[7680,128]{1,0:T(8,128)(2,1)} %get-tuple-element.48.k_ref, bf16[7680,128]{1,0:T(8,128)(2,1)} %get-tuple-element.49.v_ref, ...), custom_call_target="tpu_custom_call" | custom-call | flops 10774118400 | bytes 16777216 | tf_op jit(solution)/shard_map/attend_back/pallas_call | solution.py:232
  285.2 171.4 %finish.1 = (bf16[384,1024]{1,0:T(8,128)(2,1)}, bf16[1024,1024]{1,0:T(8,128)(2,1)}, bf16[256,1024]{1,0:T(8,128)(2,1)}, bf16[256,3072]{1,0:T(8,128)(2,1)}, f32[28,128]{1,0:T(8,128)}) custom-call(bf16[3072,128]{1,0:T(8,128)(2,1)} %get-tuple-element.59.dq_ref, bf16[7680,128]{1,0:T(8,128)(2,1)} %get-tuple-element.60.dk_ref, ...), custom_call_target="tpu_custom_call" | custom-call | flops 4831838208 | bytes 209715200 | tf_op jit(solution)/shard_map/finish/pallas_call | solution.py:1570
  456.7 0.0 copy-start.2
  456.7 2.2 convert_element_type.37
  458.9 0.0 copy-done.2
  458.9 0.0 copy-start.1
  458.9 2.0 convert_element_type.36
  461.0 0.2 copy-done.1
  461.1 0.0 copy-start.7
  461.1 0.0 copy-start.3
  461.1 0.0 copy-start.8
  461.1 2.5 convert_element_type.39
  463.6 0.0 copy-done.7
  463.6 0.6 slice_bitcast_fusion
  464.2 0.6 slice_bitcast_fusion.1
  464.8 0.0 copy-start.4
  464.8 0.0 collective-permute-done.2
  464.8 0.0 copy-done.3
  464.8 0.0 copy-done.8
  464.8 3.6 fusion
  468.5 0.0 copy-start.5
  468.5 0.0 copy-done.4
  468.5 0.9 copy.41
  469.4 0.5 copy-done.5
  469.9 0.9 copy.42
  (17 shorter events, 0.2 us)
Async XLA Ops:
  81.1 3.8 copy-start
  81.1 3.9 slice-start
  81.1 42.2 %collective-permute-start = (bf16[128,4096]{1,0:T(8,128)(2,1)}, bf16[128,4096]{1,0:T(8,128)(2,1)}, u32[]{:S(2)}, u32[]{:S(2)}) collective-permute-start(bf16[128,4096]{1,0:T(8,128)(2,1)} %get-tuple-element.53.wu_half), channel_id=1, source_target_pairs={{0,1},{1,0},{2,3},{3,2},{4,5},{5,4},{6,7},{7,6},{8,9},{9,8},{10,11... | collective-permute-start | bytes 3145736 | tf_op jit(solution)/shard_map/ppermute | solution.py:1689
  84.9 6.3 %copy-start.6 = (f32[16,8,128]{2,1,0:T(8,128)S(1)}, f32[16,8,128]{2,1,0:T(8,128)}, u32[]{:S(2)}) copy-start(f32[16,8,128]{2,1,0:T(8,128)} %get-tuple-element.45) | copy-start | bytes 196612
  85.1 39.8 %collective-permute-start.1 = (bf16[768,1024]{1,0:T(8,128)(2,1)S(1)}, bf16[768,1024]{1,0:T(8,128)(2,1)S(1)}, u32[]{:S(2)}, u32[]{:S(2)}) collective-permute-start(bf16[768,1024]{1,0:T(8,128)(2,1)S(1)} %pad_maximum_fusion), channel_id=1, source_target_pairs={{0,16},{8,24},{16,0},{24,8},{1,17},{9,25},{17,1},{25,9},{2,18},{10... | collective-permute-start | bytes 4718600 | tf_op jit(solution)/shard_map/ppermute | solution.py:1687
  124.9 1.1 copy-start.9
  242.3 222.5 %collective-permute-start.2 = (bf16[2,64,4096]{2,1,0:T(8,128)(2,1)}, bf16[2,64,4096]{2,1,0:T(8,128)(2,1)}, u32[]{:S(2)}, u32[]{:S(2)}) collective-permute-start(bf16[2,64,4096]{2,1,0:T(8,128)(2,1)} %get-tuple-element.71), channel_id=1, source_target_pairs={{0,1},{1,0},{2,3},{3,2},{4,5},{5,4},{6,7},{7,6},{8,9},{9,8},{10,11... | collective-permute-start | bytes 3145736 | tf_op jit(solution)/shard_map/ppermute | solution.py:1699
  456.7 2.3 copy-start.2
  458.9 2.2 copy-start.1
  461.1 2.5 copy-start.7
  461.1 3.7 copy-start.3
  461.1 3.7 copy-start.8
  464.8 3.7 copy-start.4
  468.5 1.4 copy-start.5

commit v8 on v7

--- a/solution.py
+++ b/solution.py
@@ -253,8 +253,8 @@
 
 CHUNK = 64
 LAG = 2
-GIVE_AT = 4
-TAKE_AT = 20
+GIVE_AT = 5
+TAKE_AT = 19
 TAKE_BY = 1
 LAST_TAKE = TAKE_AT + (GROUP - 1) * TAKE_BY
 PAIR_BY = 1
@@ -997,7 +997,7 @@
     def scale_grad(at):
         slim[at, :] = low(line(5) * high(grad_ref[at, :]))
 
-    by_rows(64, scale_grad)
+    by_rows(128, scale_grad)
 
     for e in order:
         attn_copy(e).wait_recv()
@@ -1014,7 +1014,7 @@
         unit, scale = normalize(value)
         act[at, :] = low(unit * line(2) + line(3))
 
-    by_rows(64, enter_mlp)
+    by_rows(128, enter_mlp)
     act_t[...] = act[...].T
     y_copy.wait_recv()
     y_relay.start()
@@ -1058,7 +1058,7 @@
             hidden[at, :] = low(value * cdf)
             slope[at, :] = cdf + value * (jnp.exp(-0.5 * value * value) * 0.3989422804014327)
 
-        by_rows(64, activate)
+        by_rows(128, activate)
         pre[...] = lax.dot_general(slim[...], w_back, NT, preferred_element_type=jnp.float32)
         branch[...] += matmul(hidden[...], w_back)
 
@@ -1067,7 +1067,7 @@
             pre[at, :] = value
             pre_grad[at, :] = low(value)
 
-        by_rows(64, descend)
+        by_rows(128, descend)
         total = jnp.sum(pre[...], axis=0, keepdims=True)
         for owner in range(4):
             small_out[owner, pl.ds(20 + i, 1), :] = total[:, owner * tall : (owner + 1) * tall]
@@ -1109,7 +1109,7 @@
         for which, member in enumerate(rows):
             sums[which : which + 1, :] += jnp.sum(member, axis=0, keepdims=True)
 
-    by_rows(64, leave_mlp)
+    by_rows(128, leave_mlp)
     attn_grad[...] = low(
         lax.dot_general(proj_grad[...], wo[...], NT, preferred_element_type=jnp.float32)
     )

time: 472 us -> 468 us (level)
    pallas_call x1, Pallas kernels: 171 us -> 166 us  [wrap_up(): pl.pallas_call(functools.partial(finish_kernel, replicas), out_shape=(sha...]
  transfers between devices with their start and end apart: 3 -> 3, of which waited for: 1 -> 1; matrix products, arithmetic and copies ran while one was open for 3% -> 3% of each run, Pallas kernels for 51% -> 50%
where the time goes in v8:
time: 468 us; the launch traced here: 466 us
  Pallas kernels  428 us (91%)
  other arithmetic  17.9 us (4%)
  starting transfers between devices  11.8 us (3%)
  local copies, waits for them, and re-layouts  7.85 us (2%)
    pallas_call x1, Pallas kernels, wrap_up(): pl.pallas_call(functools.partial(finish_kernel, replicas), out_shape=(sha...  166 us
    pallas_call x1, Pallas kernels, middle(): pl.pallas_call(middle_kernel, out_shape=(shape((tok_rows, D), slight), sh...  116 us
    pallas_call x1, Pallas kernels, project(): pl.pallas_call(functools.partial(qkv_kernel, replicas), out_shape=(shape(...  76.7 us
    pallas_call x1, Pallas kernels, attend_back(): pl.pallas_call(attend_back_kernel, out_shape=(jax.ShapeDtypeStruct((rows,...  43.3 us
    pallas_call x1, Pallas kernels, attend(): pl.pallas_call(attend_kernel, out_shape=(jax.ShapeDtypeStruct((rows, PAIR...  26.6 us
    convert_element_type x4, other arithmetic, shards(): grads = [grad.astype(jnp.float32) for grad in grads]  10.4 us
  transfers between devices with their start and end apart: 3, of which 1 were waited for; matrix products, arithmetic and copies ran while one was open for 3% of the time, Pallas kernels for 50%

profile of v8, /device:TPU:0, one launch (start us, length us, event | category | flops | bytes accessed | tf_op | source)
XLA Modules:
  0.0 466.4 jit_solution(11508346153019306856)
XLA Ops:
  0.7 0.8 fusion.7
  1.6 0.7 convert_bitcast_fusion
  2.3 0.6 pad.5.codes_ref
  2.9 1.5 select_convert_fusion.small_ref
  4.4 76.7 %project.1 = (bf16[384,1024]{1,0:T(8,128)(2,1)}, bf16[3072,128]{1,0:T(8,128)(2,1)}, bf16[7680,128]{1,0:T(8,128)(2,1)}, bf16[7680,128]{1,0:T(8,128)(2,1)}, f32[16...) custom-call(bf16[384,1024]{1,0:T(8,128)(2,1)} %tokens_ref.5, ...), custom_call_target="tpu_custom_call" | custom-call | flops 2415919104 | bytes 62914560 | tf_op jit(solution)/shard_map/project/pallas_call | solution.py:635
  81.1 0.0 copy-start
  81.1 0.0 slice-start
  81.1 3.8 collective-permute-start
  84.9 0.0 copy-done
  84.9 0.0 copy-start.6
  85.0 0.0 slice-done
  85.0 0.1 pad_maximum_fusion
  85.1 6.1 %collective-permute-start.1 = (bf16[768,1024]{1,0:T(8,128)(2,1)S(1)}, bf16[768,1024]{1,0:T(8,128)(2,1)S(1)}, u32[]{:S(2)}, u32[]{:S(2)}) collective-permute-start(bf16[768,1024]{1,0:T(8,128)(2,1)S(1)} %pad_maximum_fusion), channel_id=1, source_target_pairs={{0,16},{8,24},{16,0},{24,8},{1,17},{9,25},{17,1},{25,9},{2,18},{10... | collective-permute-start | bytes 4718600 | tf_op jit(solution)/shard_map/ppermute | solution.py:1687
  91.2 0.0 copy-done.6
  91.3 4.3 compare_convert_fusion.m_ref
  95.5 0.1 broadcast_in_dim.179
  95.6 0.7 broadcast_in_dim.180
  96.3 0.2 fusion.6
  96.5 0.1 reduce_max.28
  96.6 0.1 reduce_max.29
  96.7 0.1 fusion.3
  96.8 0.4 select_reduce_fusion.1
  97.2 0.1 copy.38
  97.3 0.6 reshape.212.meta
  97.9 26.6 %attend.1 = (bf16[3072,128]{1,0:T(8,128)(2,1)}, f32[128,3072]{1,0:T(8,128)}, f32[8,3072]{1,0:T(8,128)}) custom-call(s32[24]{0:T(128)} %reshape.212.meta, bf16[3072,128]{1,0:T(8,128)(2,1)} %get-tuple-element.47.q_ref, bf16[7680,128]{1,0:T(8,128)(2,1)} %get-tuple-element.48.k_ref, bf16[7680,128]{1,0:T(8,128)(2,1)} %get-tuple-element.49.v_ref, ...), custom_call_target="tpu_custom_call" | custom-call | flops 4309647360 | bytes 9437184 | tf_op jit(solution)/shard_map/attend/pallas_call | solution.py:138
  124.6 0.0 collective-permute-done.wu_other
  124.6 0.3 collective-permute-done.1.wd_across
  124.9 0.0 copy-start.9
  124.9 1.1 copy-done.9
  126.0 115.5 %middle.1 = (bf16[384,1024]{1,0:T(8,128)(2,1)}, f32[384,1024]{1,0:T(8,128)}, bf16[3072,128]{1,0:T(8,128)(2,1)}, f32[4,28,128]{2,1,0:T(8,128)}, bf16[2,64,4096]{2...) custom-call(bf16[3072,128]{1,0:T(8,128)(2,1)} %get-tuple-element.50.o_ref, bf16[384,1024]{1,0:T(8,128)(2,1)} %tokens_ref.5, ...), custom_call_target="tpu_custom_call" | custom-call | flops 16106127360 | bytes 104857600 | tf_op jit(solution)/shard_map/middle/pallas_call | solution.py:1176
  241.5 1.9 collective-permute-start.2
  243.4 43.3 %attend_back.1 = (bf16[3072,128]{1,0:T(8,128)(2,1)}, bf16[7680,128]{1,0:T(8,128)(2,1)}, bf16[7680,128]{1,0:T(8,128)(2,1)}) custom-call(s32[24]{0:T(128)} %reshape.212.meta, bf16[3072,128]{1,0:T(8,128)(2,1)} %get-tuple-element.47.q_ref, bf16[7680,128]{1,0:T(8,128)(2,1)} %get-tuple-element.48.k_ref, bf16[7680,128]{1,0:T(8,128)(2,1)} %get-tuple-element.49.v_ref, ...), custom_call_target="tpu_custom_call" | custom-call | flops 10774118400 | bytes 16777216 | tf_op jit(solution)/shard_map/attend_back/pallas_call | solution.py:232
  286.7 165.5 %finish.1 = (bf16[384,1024]{1,0:T(8,128)(2,1)}, bf16[1024,1024]{1,0:T(8,128)(2,1)}, bf16[256,1024]{1,0:T(8,128)(2,1)}, bf16[256,3072]{1,0:T(8,128)(2,1)}, f32[28,128]{1,0:T(8,128)}) custom-call(bf16[3072,128]{1,0:T(8,128)(2,1)} %get-tuple-element.59.dq_ref, bf16[7680,128]{1,0:T(8,128)(2,1)} %get-tuple-element.60.dk_ref, ...), custom_call_target="tpu_custom_call" | custom-call | flops 4831838208 | bytes 209715200 | tf_op jit(solution)/shard_map/finish/pallas_call | solution.py:1570
  452.3 0.0 copy-start.2
  452.3 2.2 convert_element_type.37
  454.5 0.0 copy-done.2
  454.5 0.0 copy-start.1
  454.5 2.0 convert_element_type.36
  456.6 0.2 copy-done.1
  456.7 0.0 copy-start.7
  456.7 0.0 copy-start.3
  456.7 0.0 copy-start.8
  456.7 2.5 convert_element_type.39
  459.2 0.0 copy-done.7
  459.2 0.6 slice_bitcast_fusion
  459.8 0.6 slice_bitcast_fusion.1
  460.4 0.0 copy-start.4
  460.4 0.0 collective-permute-done.2
  460.4 0.0 copy-done.3
  460.4 0.0 copy-done.8
  460.4 3.6 fusion
  464.1 0.0 copy-start.5
  464.1 0.0 copy-done.4
  464.1 0.9 copy.41
  465.0 0.5 copy-done.5
  465.5 0.9 copy.42
  (17 shorter events, 0.2 us)
Async XLA Ops:
  81.1 3.8 copy-start
  81.1 3.9 slice-start
  81.1 43.4 %collective-permute-start = (bf16[128,4096]{1,0:T(8,128)(2,1)}, bf16[128,4096]{1,0:T(8,128)(2,1)}, u32[]{:S(2)}, u32[]{:S(2)}) collective-permute-start(bf16[128,4096]{1,0:T(8,128)(2,1)} %get-tuple-element.53.wu_half), channel_id=1, source_target_pairs={{0,1},{1,0},{2,3},{3,2},{4,5},{5,4},{6,7},{7,6},{8,9},{9,8},{10,11... | collective-permute-start | bytes 3145736 | tf_op jit(solution)/shard_map/ppermute | solution.py:1689
  84.9 6.3 %copy-start.6 = (f32[16,8,128]{2,1,0:T(8,128)S(1)}, f32[16,8,128]{2,1,0:T(8,128)}, u32[]{:S(2)}) copy-start(f32[16,8,128]{2,1,0:T(8,128)} %get-tuple-element.45) | copy-start | bytes 196612
  85.1 39.8 %collective-permute-start.1 = (bf16[768,1024]{1,0:T(8,128)(2,1)S(1)}, bf16[768,1024]{1,0:T(8,128)(2,1)S(1)}, u32[]{:S(2)}, u32[]{:S(2)}) collective-permute-start(bf16[768,1024]{1,0:T(8,128)(2,1)S(1)} %pad_maximum_fusion), channel_id=1, source_target_pairs={{0,16},{8,24},{16,0},{24,8},{1,17},{9,25},{17,1},{25,9},{2,18},{10... | collective-permute-start | bytes 4718600 | tf_op jit(solution)/shard_map/ppermute | solution.py:1687
  124.9 1.1 copy-start.9
  241.5 218.9 %collective-permute-start.2 = (bf16[2,64,4096]{2,1,0:T(8,128)(2,1)}, bf16[2,64,4096]{2,1,0:T(8,128)(2,1)}, u32[]{:S(2)}, u32[]{:S(2)}) collective-permute-start(bf16[2,64,4096]{2,1,0:T(8,128)(2,1)} %get-tuple-element.71), channel_id=1, source_target_pairs={{0,1},{1,0},{2,3},{3,2},{4,5},{5,4},{6,7},{7,6},{8,9},{9,8},{10,11... | collective-permute-start | bytes 3145736 | tf_op jit(solution)/shard_map/ppermute | solution.py:1699
  452.3 2.3 copy-start.2
  454.5 2.2 copy-start.1
  456.7 2.5 copy-start.7
  456.7 3.7 copy-start.3
  456.7 3.7 copy-start.8
  460.4 3.7 copy-start.4
  464.1 1.4 copy-start.5
